TPU v7x, 64 devices: a 2x2x8 block of a 4x4x8 slice. The times are simulated.
64 devices in a mesh: rep: 8 (over x, y, core), dp: 8 (over z).
Axes of the slice: x: 2, y: 2, z: 8, core: 2. Of those that a mesh axis runs over, the one named last changes fastest.
The devices are a block of a 4x4x8 slice.
Arguments:
- x: bfloat16 [64, 2048, 512], P(('rep', 'dp')), parts along dimension 0
- dy: bfloat16 [64, 2048, 512], P(('rep', 'dp')), parts along dimension 0
- w_gate: bfloat16 [2, 512, 3072], replicated
- w_up: bfloat16 [2, 512, 3072], replicated
- w_down: bfloat16 [2, 3072, 512], replicated
- m_w_gate: float32 [2, 512, 3072], P(None, 'dp')
- m_w_up: float32 [2, 512, 3072], P(None, 'dp')
- m_w_down: float32 [2, 3072, 512], P(None, 'dp')
- v_w_gate: float32 [2, 512, 3072], P(None, 'dp')
- v_w_up: float32 [2, 512, 3072], P(None, 'dp')
- v_w_down: float32 [2, 3072, 512], P(None, 'dp')
Outputs:
- output 1: bfloat16 [16, 512, 3072], P('rep'), parts along dimension 0
- output 2: bfloat16 [16, 512, 3072], P('rep'), parts along dimension 0
- output 3: bfloat16 [16, 3072, 512], P('rep'), parts along dimension 0
- output 4: float32 [16, 512, 3072], P('rep', 'dp'), parts along dimension 0
- output 5: float32 [16, 512, 3072], P('rep', 'dp'), parts along dimension 0
- output 6: float32 [16, 3072, 512], P('rep', 'dp'), parts along dimension 0
- output 7: float32 [16, 512, 3072], P('rep', 'dp'), parts along dimension 0
- output 8: float32 [16, 512, 3072], P('rep', 'dp'), parts along dimension 0
- output 9: float32 [16, 3072, 512], P('rep', 'dp'), parts along dimension 0
There are 8 independent parts. A program takes and returns all parts, laid end to end along the dimension named above; an argument that names none is the same for every part.
All inputs are finite; a program needn't handle non-finite values.
Results may differ from a plain program's by a relative error of at most 0.022.
Values are sent between devices in bfloat16 or wider.
A program may use at most 768 MiB of HBM per device.

v0:
```python
import jax
import jax.numpy as jnp
from jax import lax

NAMES = ("w_gate", "w_up", "w_down")


def matmul(a, w):
    return jnp.dot(a, w, preferred_element_type=jnp.float32).astype(jnp.bfloat16)


def normed(h):
    wide = h.astype(jnp.float32)
    scale = lax.rsqrt(jnp.mean(wide**2, -1, keepdims=True) + 1e-6)
    return (wide * scale).astype(jnp.bfloat16)


def layer(h, w):
    a = normed(h)
    gate = jnp.dot(a, w["w_gate"], preferred_element_type=jnp.float32)
    up = jnp.dot(a, w["w_up"], preferred_element_type=jnp.float32)
    return h + matmul((jax.nn.silu(gate) * up).astype(jnp.bfloat16), w["w_down"])


def adamw(w, m, v, g):
    m = 0.9 * m + 0.1 * g
    v = 0.95 * v + 0.05 * g * g
    step = m * lax.rsqrt(v + 1e-8) + 0.1 * w
    return (w - 0.02 * step).astype(jnp.bfloat16), m, v


def clipped(gradients, sum_of_squares, count):
    factor = jnp.minimum(1.0, 0.5 * lax.rsqrt(sum_of_squares / count + 1e-30))
    return [g * factor for g in gradients]


def stack(weights, h):
    for number in range(weights["w_gate"].shape[0]):
        h = layer(h, {name: w[number] for name, w in weights.items()})
    return h


def solution(mesh):
    groups = mesh.shape["rep"]

    def step(x, dy, *arrays):
        weights, m, v = (arrays[i : i + 3] for i in (0, 3, 6))
        x, dy = (t.reshape(groups, -1, *t.shape[1:]) for t in (x, dy))

        def of_a_group(x, dy):
            _, back = jax.vjp(lambda w: stack(w, x), dict(zip(NAMES, weights, strict=True)))
            by_weights = back(dy)[0]
            gradients = [by_weights[name].astype(jnp.float32) for name in NAMES]
            gradients = clipped(gradients, sum(jnp.sum(g * g) for g in gradients), sum(g.size for g in gradients))
            new = [adamw(w.astype(jnp.float32), m, v, g) for w, m, v, g in zip(weights, m, v, gradients, strict=True)]
            return tuple(one[which] for which in range(3) for one in new)

        return tuple(t.reshape(-1, *t.shape[2:]) for t in jax.vmap(of_a_group)(x, dy))

    return step
```

profile of v0, /device:TPU:30, one launch (start us, length us, event | category | flops | bytes accessed | tf_op | source)
XLA Modules:
  0.0 890.0 jit_solution(5075554659480581510)
XLA Ops:
  9.5 3.9 copy
  13.4 13.6 %fusion.67 = f32[2048,3072]{1,0:T(8,128)} fusion(bf16[2,512,3072]{2,1,0:T(8,128)(2,1)} %param, bf16[1,2048,512]{2,1,0:T(8,128)(2,1)S(1)} %copy-done.1, f32[2048]{0:T(1024)S(1)} %add_rsqrt_fusion), kind=kOutput, calls=%fused_computation.79 | convolution fusion | flops 6445596672 | bytes 30416896 | tf_op jit(solution)/vmap(jvp())/dot_general | solution.py:20
  27.0 13.6 %fusion.65 = f32[2048,3072]{1,0:T(8,128)} fusion(bf16[2,512,3072]{2,1,0:T(8,128)(2,1)} %param.3, bf16[1,2048,512]{2,1,0:T(8,128)(2,1)S(1)} %copy-done.1, f32[2048]{0:T(1024)S(1)} %add_rsqrt_fusion), kind=kOutput, calls=%fused_computation.77 | convolution fusion | flops 6445596672 | bytes 30416896 | tf_op jit(solution)/vmap(jvp())/dot_general | solution.py:21
  40.6 21.8 %fusion.26 = bf16[2048,3072]{1,0:T(8,128)(2,1)} fusion(f32[2048,3072]{1,0:T(8,128)} %fusion.65, f32[2048,3072]{1,0:T(8,128)} %fusion.67), kind=kLoop, calls=%fused_computation.35 | loop fusion | flops 37748736 | bytes 62914560
  62.4 10.8 %fusion.51 = (f32[2048]{0:T(1024)S(1)}, bf16[1,1,2048,512]{2,3,1,0:T(8,128)(2,1)S(1)}) fusion(bf16[2048,3072]{1,0:T(8,128)(2,1)} %fusion.26, bf16[2,3072,512]{2,1,0:T(8,128)(2,1)} %param.4, bf16[1,2048,512]{1,2,0:T(8,128)(2,1)S(1)} %copy-done.5), kind=kOutput, calls=%fused_computation.62 | convolution fusion | flops 6447691776 | bytes 19931136 | tf_op jit(solution)/vmap(jvp())/dot_general | solution.py:9
  73.3 15.1 %fusion.56 = f32[2048,3072]{1,0:T(8,128)} fusion(bf16[2,512,3072]{2,1,0:T(8,128)(2,1)} %param, bf16[1,1,2048,512]{2,3,1,0:T(8,128)(2,1)S(1)} %get-tuple-element.10, f32[2048]{0:T(1024)S(1)} %bitcast.376), kind=kOutput, calls=%fused_computation.68 | convolution fusion | flops 6445596672 | bytes 30416896 | tf_op jit(solution)/vmap(jvp())/dot_general | solution.py:20
  88.3 13.8 %fusion.59 = f32[2048,3072]{1,0:T(8,128)} fusion(bf16[2,512,3072]{2,1,0:T(8,128)(2,1)} %param.3, bf16[1,1,2048,512]{2,3,1,0:T(8,128)(2,1)S(1)} %get-tuple-element.10, f32[2048]{0:T(1024)S(1)} %bitcast.377), kind=kOutput, calls=%fused_computation.71 | convolution fusion | flops 6445596672 | bytes 30416896 | tf_op jit(solution)/vmap(jvp())/dot_general | solution.py:21
  102.2 9.8 %convolution_convert_fusion.1 = bf16[2048,3072]{1,0:T(8,128)(2,1)} fusion(bf16[2,3072,512]{2,1,0:T(8,128)(2,1)S(1)} %bitcast.372, bf16[1,2048,512]{2,1,0:T(8,128)(2,1)S(1)} %copy-done.3), kind=kOutput, calls=%fused_computation.44 | convolution fusion | flops 6448742400 | bytes 17825792 | tf_op jit(solution)/vmap(transpose(jvp()))/dot_general | solution.py:9
  114.9 21.3 %fusion.6 = bf16[2048,3072]{1,0:T(8,128)(2,1)S(1)} fusion(f32[2048,3072]{1,0:T(8,128)} %fusion.56, f32[2048,3072]{1,0:T(8,128)} %fusion.59, bf16[2048,3072]{1,0:T(8,128)(2,1)} %convolution_convert_fusion.1), kind=kLoop, calls=%fused_computation.11 | loop fusion | flops 75497472 | bytes 75497472
  136.2 4.5 copy-done
  140.7 9.3 %fusion.80 = bf16[2048,512]{0,1:T(8,128)(2,1)} fusion(bf16[2048,3072]{1,0:T(8,128)(2,1)S(1)} %fusion.6, bf16[2,512,3072]{2,1,0:T(8,128)(2,1)} %param), kind=kOutput, calls=%fused_computation.86 | convolution fusion | flops 6442450944 | bytes 17825792 | tf_op jit(solution)/vmap(transpose(jvp()))/dot_general | solution.py:20
  149.9 20.9 %fusion.53 = (f32[2048]{0:T(1024)S(1)}, bf16[1,1,2048,512]{2,3,1,0:T(8,128)(2,1)}) fusion(bf16[1,1,2048,512]{2,3,1,0:T(8,128)(2,1)} %copy-done.7, bf16[2048,512]{0,1:T(8,128)(2,1)} %fusion.80, bf16[2,512,3072]{2,1,0:T(8,128)(2,1)} %param.3, bf16[2048,3072]{1,0:T(8,128)(2,1)} %convolution_convert_fusion.1, f32[2048,3072]{1,0:T(8,128)} %fusion.56), kind=kOutput, calls=%fused_computation.64 | convolution fusion | flops 6486489088 | bytes 47194112 | tf_op jit(solution)/vmap(transpose(jvp()))/dot_general | solution.py:21
  175.7 11.6 %convolution_bitcast_fusion = f32[1,3072,512]{2,1,0:T(8,128)} fusion(bf16[2048,3072]{1,0:T(8,128)(2,1)} %fusion.26, bf16[2048,512]{0,1:T(8,128)(2,1)S(1)} %fusion.108), kind=kOutput, calls=%fused_computation.54 | convolution fusion | flops 6442450944 | bytes 20971520 | tf_op jit(solution)/vmap(transpose(jvp()))/dot_general | solution.py:9
  188.9 20.8 %fusion.35 = f32[1,3072,512]{2,1,0:T(8,128)} fusion(f32[2048,3072]{1,0:T(8,128)} %fusion.59, f32[2048,3072]{1,0:T(8,128)} %fusion.56, bf16[1,2048,512]{2,1,0:T(8,128)(2,1)S(1)} %copy-done.4), kind=kOutput, calls=%fused_computation.52 | convolution fusion | flops 6480199680 | bytes 58720256 | tf_op jit(solution)/vmap(transpose(jvp()))/dot_general | solution.py:9
  209.8 12.3 %convolution_convert_fusion = bf16[2048,3072]{1,0:T(8,128)(2,1)} fusion(bf16[2048,512]{0,1:T(8,128)(2,1)} %copy-done.9, bf16[2,3072,512]{2,1,0:T(8,128)(2,1)} %param.4), kind=kOutput, calls=%fused_computation.43 | convolution fusion | flops 6448742400 | bytes 17825792 | tf_op jit(solution)/vmap(transpose(jvp()))/dot_general | solution.py:9
  222.1 18.0 %fusion.44 = f32[1,512,3072]{2,1,0:T(8,128)} fusion(bf16[2048,3072]{1,0:T(8,128)(2,1)} %convolution_convert_fusion, f32[2048,3072]{1,0:T(8,128)} %fusion.67, bf16[1,2048,512]{1,2,0:T(8,128)(2,1)S(1)} %copy-done.6, f32[2048]{0:T(1024)S(1)} %copy-done.12), kind=kOutput, calls=%fused_computation.57 | convolution fusion | flops 6483345408 | bytes 46145536 | tf_op jit(solution)/vmap(transpose(jvp()))/dot_general | solution.py:21
  240.3 18.8 %fusion.41 = f32[1,512,3072]{2,1,0:T(8,128)} fusion(bf16[2048,3072]{1,0:T(8,128)(2,1)} %convolution_convert_fusion.1, f32[2048,3072]{1,0:T(8,128)} %fusion.56, bf16[1,1,2048,512]{2,3,1,0:T(8,128)(2,1)} %copy-done.7, f32[2048]{0:T(1024)S(1)} %bitcast.379), kind=kOutput, calls=%fused_computation.56 | convolution fusion | flops 6483345408 | bytes 46145536 | tf_op jit(solution)/vmap(transpose(jvp()))/dot_general | solution.py:21
  259.2 25.5 %fusion.38 = f32[1,512,3072]{2,1,0:T(8,128)} fusion(f32[2048,3072]{1,0:T(8,128)} %fusion.67, f32[2048,3072]{1,0:T(8,128)} %fusion.65, bf16[2048,3072]{1,0:T(8,128)(2,1)} %convolution_convert_fusion, bf16[1,2048,512]{1,2,0:T(8,128)(2,1)S(1)} %copy-done.6, f32[2048]{0:T(1024)S(1)} %copy-done.12), kind=kOutput, calls=%fused_computation.53 | convolution fusion | flops 6514802688 | bytes 71311360 | tf_op jit(solution)/vmap(transpose(jvp()))/dot_general | solution.py:20
  286.3 11.3 %convolution_bitcast_fusion.1 = f32[1,512,3072]{2,1,0:T(8,128)} fusion(bf16[2048,3072]{1,0:T(8,128)(2,1)} %copy-done, bf16[1,1,2048,512]{2,3,1,0:T(8,128)(2,1)S(1)} %copy-done.8, f32[2048]{0:T(1024)S(1)} %bitcast.380), kind=kOutput, calls=%fused_computation.55 | convolution fusion | flops 6445596672 | bytes 20979712 | tf_op jit(solution)/vmap(transpose(jvp()))/dot_general | solution.py:20
  300.7 35.0 %reduce-scatter.27.cloned.1.call-done = f32[1,384,512]{2,1,0:T(8,128)} async-done(((f32[1,3072,512]{2,1,0:T(8,128)}), f32[1,384,512]{2,1,0:T(8,128)}) %reduce-scatter.27.cloned.1.call-update) | async-done | bytes 786448
  337.8 71.2 %reduce-scatter.25.cloned.1.call-done = f32[1,64,3072]{2,1,0:T(8,128)} async-done(((f32[1,512,3072]{2,1,0:T(8,128)}), f32[1,64,3072]{2,1,0:T(8,128)}) %reduce-scatter.25.cloned.1.call-update) | async-done | bytes 786448
  410.2 71.5 %reduce-scatter.23.cloned.1.call-done = f32[1,64,3072]{2,1,0:T(8,128)} async-done(((f32[1,512,3072]{2,1,0:T(8,128)}), f32[1,64,3072]{2,1,0:T(8,128)}) %reduce-scatter.23.cloned.1.call-update) | async-done | bytes 786448
  483.9 71.1 %reduce-scatter.21.cloned.1.call-done = f32[1,64,3072]{2,1,0:T(8,128)} async-done(((f32[1,512,3072]{2,1,0:T(8,128)}), f32[1,64,3072]{2,1,0:T(8,128)}) %reduce-scatter.21.cloned.1.call-update) | async-done | bytes 786448
  556.2 72.1 %reduce-scatter.19.cloned.1.call-done = f32[1,64,3072]{2,1,0:T(8,128)} async-done(((f32[1,512,3072]{2,1,0:T(8,128)}), f32[1,64,3072]{2,1,0:T(8,128)}) %reduce-scatter.19.cloned.1.call-update) | async-done | bytes 786448
  632.4 16.7 %all-reduce.16 = f32[1]{0:T(128)} all-reduce(f32[1]{0:T(128)} %bitcast.50), channel_id=5, replica_groups=mesh['rep'=8,'dp'=8] {'dp'}, use_global_device_ids=true, to_apply=%region_3.4.clone | all-reduce | flops 1 | bytes 8 | tf_op jit(solution)/vmap()/reduce_sum | solution.py:54
  649.8 4.9 fusion.150
  654.8 5.0 fusion.151
  660.0 4.4 fusion.152
  664.5 61.3 %all-gather.14.cloned.1.call-done = bf16[1,2,3072,512]{3,2,1,0:T(8,128)(2,1)} async-done(((bf16[1,2,384,512]{3,2,1,0:T(8,128)(2,1)}), bf16[1,2,3072,512]{3,2,1,0:T(8,128)(2,1)}) %all-gather.14.cloned.1.call-update) | async-done | bytes 6291472 | tf_op jit(solution)/reshape | solution.py:58
  725.8 71.8 %all-gather.12.cloned.1.call-done = bf16[1,2,512,3072]{3,2,1,0:T(8,128)(2,1)} async-done(((bf16[1,2,64,3072]{3,2,1,0:T(8,128)(2,1)}), bf16[1,2,512,3072]{3,2,1,0:T(8,128)(2,1)}) %all-gather.12.cloned.1.call-update) | async-done | bytes 6291472 | tf_op jit(solution)/reshape | solution.py:58
  797.6 71.8 %all-gather.10.cloned.1.call-done = bf16[1,2,512,3072]{3,2,1,0:T(8,128)(2,1)} async-done(((bf16[1,2,64,3072]{3,2,1,0:T(8,128)(2,1)}), bf16[1,2,512,3072]{3,2,1,0:T(8,128)(2,1)}) %all-gather.10.cloned.1.call-update) | async-done | bytes 6291472 | tf_op jit(solution)/reshape | solution.py:58
  869.4 6.6 copy.5
  (75 shorter events, 32.5 us)
Async XLA Ops:
  7.2 6.2 copy-start.1
  7.2 292.3 %reduce-scatter.29.cloned.1.call-start = ((), (), s32[]{:S(2)}) async-start(), calls=%async_computation.14 | async-start | bytes 7077888
  13.4 13.6 %copy-start.11 = (f32[2048]{0:T(1024)}, f32[2048]{0:T(1024)S(1)}, u32[]{:S(2)}) copy-start(f32[2048]{0:T(1024)S(1)} %add_rsqrt_fusion) | copy-start | bytes 24580
  40.6 21.8 %copy-start.5 = (bf16[1,2048,512]{1,2,0:T(8,128)(2,1)S(1)}, bf16[1,2048,512]{1,2,0:T(8,128)(2,1)}, u32[]{:S(2)}) copy-start(bf16[1,2048,512]{1,2,0:T(8,128)(2,1)} %copy) | copy-start | bytes 6291460
  73.2 15.1 %copy-start.7 = (bf16[1,1,2048,512]{2,3,1,0:T(8,128)(2,1)}, bf16[1,1,2048,512]{2,3,1,0:T(8,128)(2,1)S(1)}, u32[]{:S(2)}) copy-start(bf16[1,1,2048,512]{2,3,1,0:T(8,128)(2,1)S(1)} %get-tuple-element.10) | copy-start | bytes 6291460
  73.3 28.9 %slice-start.2 = ((s8[6291456]{0:T(1024)(128)(4,1)}), s8[4194304]{0:T(1024)(128)(4,1)S(1)}, s32[]{:S(2)}) async-start(s8[6291456]{0:T(1024)(128)(4,1)} %bitcast.371), calls=%async_computation.17 | async-start | bytes 8388608
  88.3 13.9 %copy-start.3 = (bf16[1,2048,512]{2,1,0:T(8,128)(2,1)S(1)}, bf16[1,2048,512]{2,1,0:T(8,128)(2,1)}, u32[]{:S(2)}) copy-start(bf16[1,2048,512]{2,1,0:T(8,128)(2,1)} %param.5) | copy-start | bytes 6291460
  88.3 13.9 %slice-start.3 = ((s8[6291456]{0:T(1024)(128)(4,1)}), s8[2097152]{0:T(1024)(128)(4,1)S(1)}, s32[]{:S(2)}) async-start(s8[6291456]{0:T(1024)(128)(4,1)} %bitcast.371), calls=%async_computation.18 | async-start | bytes 4194304
  136.2 4.5 copy-start
  174.4 1.3 copy-start.9
  187.3 1.6 copy-start.4
  187.4 148.3 %reduce-scatter.27.cloned.1.call-start = ((), (), s32[]{:S(2)}) async-start(), calls=%async_computation.13 | async-start | bytes 7077888
  209.7 12.4 %copy-start.6 = (bf16[1,2048,512]{1,2,0:T(8,128)(2,1)S(1)}, bf16[1,2048,512]{1,2,0:T(8,128)(2,1)}, u32[]{:S(2)}) copy-start(bf16[1,2048,512]{1,2,0:T(8,128)(2,1)} %copy) | copy-start | bytes 6291460
  209.7 12.4 %copy-start.12 = (f32[2048]{0:T(1024)S(1)}, f32[2048]{0:T(1024)}, u32[]{:S(2)}) copy-start(f32[2048]{0:T(1024)} %copy-done.11) | copy-start | bytes 24580
  209.7 199.3 %reduce-scatter.25.cloned.1.call-start = ((), (), s32[]{:S(2)}) async-start(), calls=%async_computation.12 | async-start | bytes 7077888
  240.2 241.5 %reduce-scatter.23.cloned.1.call-start = ((), (), s32[]{:S(2)}) async-start(), calls=%async_computation.11 | async-start | bytes 7077888
  259.1 295.9 %reduce-scatter.21.cloned.1.call-start = ((), (), s32[]{:S(2)}) async-start(), calls=%async_computation.10 | async-start | bytes 7077888
  284.7 1.6 copy-start.8
  284.8 343.5 %reduce-scatter.19.cloned.1.call-start = ((), (), s32[]{:S(2)}) async-start(), calls=%async_computation.9 | async-start | bytes 7077888
  297.6 0.7 copy-start.13
  297.6 428.2 %all-gather.14.cloned.1.call-start = ((), (), s32[]{:S(2)}) async-start(), calls=%async_computation.8 | async-start | bytes 7077888 | tf_op jit(solution)/reshape | solution.py:58
  654.8 142.8 %all-gather.12.cloned.1.call-start = ((), (), s32[]{:S(2)}) async-start(), calls=%async_computation.7 | async-start | bytes 7077888 | tf_op jit(solution)/reshape | solution.py:58
  654.8 5.2 copy-start.10
  659.9 209.5 %all-gather.10.cloned.1.call-start = ((), (), s32[]{:S(2)}) async-start(), calls=%async_computation.6 | async-start | bytes 7077888 | tf_op jit(solution)/reshape | solution.py:58
  869.4 6.6 copy-start.2
  869.4 9.8 %slice-start = ((s8[6291456]{0:T(1024)(128)(4,1)}), s8[4194304]{0:T(1024)(128)(4,1)S(1)}, s32[]{:S(2)}) async-start(s8[6291456]{0:T(1024)(128)(4,1)} %bitcast.366), calls=%async_computation.15 | async-start | bytes 8388608
  876.0 4.5 slice-start.1
Sparse Core Ops, SparseCore 0:
  187.5 75.2 reduce-scatter.28
  265.1 70.4 reduce-scatter.26
  338.6 70.4 reduce-scatter.24
  411.2 70.4 reduce-scatter.22
  484.5 70.4 reduce-scatter.20
  557.8 70.4 reduce-scatter.18
  654.9 70.8 all-gather.13
  727.9 69.5 all-gather.11
  799.8 69.5 all-gather.9
where the time goes:
time: 899 us; the launch traced here: 890 us
  waiting for transfers between devices  526 us (59%)
  matrix products  225 us (25%)
  other arithmetic  73.3 us (8%)
  local copies, waits for them, and re-layouts  30.6 us (3%)
  between operations  17.6 us (2%)
  blocking collectives  16.7 us (2%)
    unnamed x15, waiting for transfers between devices  321 us
    reshape x3, waiting for transfers between devices, step(): t.reshape(-1, *t.shape[2:])  205 us
    dot_general x5, matrix products, layer(): up = jnp.dot(a, w['w_up'], preferred_element_type=jnp.float32)  85.1 us
    dot_general x5, matrix products, layer(): gate = jnp.dot(a, w['w_gate'], preferred_element_type=jnp.float32)  74.7 us
    dot_general x5, matrix products, matmul(): jnp.dot(a, w, preferred_element_type=jnp.float32).astype(jnp.bfloat16)  65.1 us
    unnamed x5, other arithmetic  46.6 us
    unnamed x41, local copies, waits for them, and re-layouts  30 us
  transfers between devices with their start and end apart: 9, of which 8 were waited for; matrix products, arithmetic and copies ran while one was open for 14% of the time, Pallas kernels for 0%

commit v1 on v0

v1 whole, which is shorter than its diff:
```python
import functools

import jax
import jax.numpy as jnp
from jax import lax
from jax.experimental import pallas as pl
from jax.experimental.pallas import tpu as pltpu
from jax.sharding import PartitionSpec as P

F32 = jnp.float32
BF16 = jnp.bfloat16
MESH = pl.DeviceIdType.MESH
LANES = 128
VMEM_LIMIT = 67043328


def dot(a, b):
    return jnp.dot(a, b, preferred_element_type=F32)


def dot_t(a, b):
    return lax.dot_general(a, b, (((1,), (1,)), ((), ())), preferred_element_type=F32)


def scale_of(wide):
    return lax.rsqrt(jnp.mean(wide * wide, -1, keepdims=True) + 1e-6)


def loop(count, body):
    lax.fori_loop(0, count, lambda i, c: (body(i), c)[1], 0)


def at(i, size):
    return pl.ds(pl.multiple_of(i * size, size), size)


def grad_kernel(n, layers, shapes, *refs):
    (x_hbm, dy_hbm, wg_hbm, wu_hbm, wd_hbm) = refs[:5]
    (og_hbm, ou_hbm, od_hbm, sq_hbm) = refs[5:9]
    (A, AT, D, DT, H, ACT, DG, DU, DA, WG, WU, WD, G, RU, RD, OG, OU, OD, SQ, x_sem, dy_sem, w_sem, out_sem, send_sem, recv_sem) = refs[9:]
    tokens, dim, ff, blocks = shapes
    share = ff // n
    tiles = share // LANES
    tile = n * LANES
    tb = tokens // blocks
    half = n // 2
    hr = LANES // 2
    cols = tile // 2
    strip = tile // 4
    me = lax.axis_index("dp")
    up, down = lax.rem(me + 1, n), lax.rem(me + n - 1, n)
    ring = lambda d: lax.rem(me + d + n, n)

    def tok(i):
        return at(i, tb)

    def fetch(k):
        slot = lax.rem(k, 2)
        layer = lax.rem(k // tiles, 2)
        t = lax.rem(k, tiles)

        def one(b):
            place = pl.ds(pl.multiple_of(b * share + t * LANES, LANES), LANES)
            here = at(b, LANES)
            pltpu.make_async_copy(wg_hbm.at[layer, :, place], WG.at[slot, :, here], w_sem.at[slot, 0]).start()
            pltpu.make_async_copy(wu_hbm.at[layer, :, place], WU.at[slot, :, here], w_sem.at[slot, 1]).start()
            pltpu.make_async_copy(wd_hbm.at[layer, place, :], WD.at[slot, here, :], w_sem.at[slot, 2]).start()

        loop(n, one)

    def fetched(k):
        slot = lax.rem(k, 2)
        pltpu.make_async_copy(WG.at[slot], WG.at[slot], w_sem.at[slot, 0]).wait()
        pltpu.make_async_copy(WU.at[slot], WU.at[slot], w_sem.at[slot, 1]).wait()
        pltpu.make_async_copy(WD.at[slot], WD.at[slot], w_sem.at[slot, 2]).wait()

    def x_copy(i):
        return pltpu.make_async_copy(x_hbm.at[0, tok(i), :], H.at[tok(i), :], x_sem.at[i])

    def x_again(i):
        return pltpu.make_async_copy(x_hbm.at[0, tok(i), :], ACT.at[tok(i), pl.ds(0, dim)], x_sem.at[i])

    def dy_copy(i):
        return pltpu.make_async_copy(dy_hbm.at[0, tok(i), :], D.at[tok(i), :], dy_sem.at[i])

    barrier = pltpu.get_barrier_semaphore()
    for peer in (up, down):
        pl.semaphore_signal(barrier, inc=1, device_id={"dp": peer}, device_id_type=MESH)

    loop(blocks, lambda i: x_copy(i).start())
    fetch(0)
    loop(blocks, lambda i: dy_copy(i).start())

    def first_norm(i):
        x_copy(i).wait()
        wide = H[tok(i), :].astype(F32)
        A[tok(i), :] = (wide * scale_of(wide)).astype(BF16)
        DA[tok(i), :] = jnp.zeros((tb, dim), F32)

    loop(blocks, first_norm)

    def forward_tile(k):
        slot = lax.rem(k, 2)
        fetched(k)
        fetch(k + 1)

        def some(i):
            for j in range(2):
                here = pl.ds(j * cols, cols)
                g = dot(A[tok(i), :], WG[slot, :, here])
                u = dot(A[tok(i), :], WU[slot, :, here])
                s = 0.5 * jnp.tanh(0.5 * g) + 0.5
                ACT[tok(i), here] = (g * s * u).astype(BF16)
            DA[tok(i), :] += dot(ACT[tok(i), :], WD[slot])

        loop(blocks, some)

    loop(tiles, forward_tile)

    def second_norm(i):
        h = (H[tok(i), :].astype(F32) + DA[tok(i), :].astype(BF16).astype(F32)).astype(BF16)
        H[tok(i), :] = h
        wide = h.astype(F32)
        a = (wide * scale_of(wide)).astype(BF16)
        A[tok(i), :] = a
        AT[:, tok(i)] = a.T
        DA[tok(i), :] = jnp.zeros((tb, dim), F32)
        dy_copy(i).wait()
        DT[:, tok(i)] = D[tok(i), :].T

    loop(blocks, second_norm)

    pl.semaphore_wait(barrier, 2)

    def remote(src, dst, slot, u, way, step):
        return pltpu.make_async_remote_copy(
            src_ref=src,
            dst_ref=dst,
            send_sem=send_sem.at[slot, way, step],
            recv_sem=recv_sem.at[u, way, step],
            device_id={"dp": (up, down)[way]},
            device_id_type=MESH,
        )

    low, high, whole = pl.ds(0, hr), pl.ds(hr, hr), pl.ds(0, 2 * hr)
    lands = (RU, RD)

    def rows(step):
        return pl.ds(pl.multiple_of(hr + (step - 1) * 2 * hr, hr), 2 * hr)

    def begin(u, slot):
        far = ring(half)
        remote(G.at[slot, far, low], RU.at[u, low], slot, u, 0, 0).start()
        remote(G.at[slot, far, high], RD.at[u, low], slot, u, 1, 0).start()
        remote(G.at[slot, ring(half - 1), high], RU.at[u, pl.ds(2 * hr, hr)], slot, u, 0, 1).start()
        remote(G.at[slot, ring(1 - half), low], RD.at[u, pl.ds(hr, hr)], slot, u, 1, 1).start()

    def received(u, way, step):
        dst = lands[way].at[u, low] if isinstance(step, int) and step == 0 else lands[way].at[u, rows(step)]
        pltpu.make_async_copy(dst, dst, recv_sem.at[u, way, step]).wait()

    def add(land, place, mine):
        land[place] = (land[place].astype(F32) + mine.astype(F32)).astype(BF16)

    def second(u, slot):
        received(u, 0, 0)
        received(u, 1, 0)
        add(RU, (u, low), G[slot, ring(half - 1), low])
        add(RD, (u, low), G[slot, ring(1 - half), high])
        remote(RU.at[u, low], RU.at[u, pl.ds(hr, hr)], slot, u, 0, 1).start()
        remote(RD.at[u, low], RD.at[u, pl.ds(2 * hr, hr)], slot, u, 1, 1).start()

    def later(u, slot, step):
        received(u, 0, step - 1)
        received(u, 1, step - 1)
        add(RU, (u, rows(step - 1)), G[slot, ring(half - step)])
        add(RD, (u, rows(step - 1)), G[slot, ring(step - half)])
        remote(RU.at[u, rows(step - 1)], RU.at[u, rows(step)], slot, u, 0, step).start()
        remote(RD.at[u, rows(step - 1)], RD.at[u, rows(step)], slot, u, 1, step).start()

    def finish(u, slot, which, layer, t):
        received(u, 0, half - 1)
        received(u, 1, half - 1)
        total = G[slot, me].astype(F32) + RU[u, rows(half - 1)].astype(F32) + RD[u, rows(half - 1)].astype(F32)
        total = total.astype(BF16)
        wide = total.astype(F32)
        SQ[...] += jnp.sum((wide * wide).reshape(-1, 8, dim), axis=0)
        if which == 0:
            OD[layer, at(t, LANES), :] = total
        else:
            out = (OG, OU)[which - 1]
            for b in range(n):
                piece = total[hr * (b // (n // 2)) : hr * (b // (n // 2)) + hr, LANES * (b % (n // 2)) : LANES * (b % (n // 2)) + LANES]
                out[layer, :, pl.ds(pl.multiple_of(b * share + t * LANES, LANES), LANES)] = piece
        for way in range(2):
            for step in range(half):
                src = G.at[slot, 0, whole] if step > 0 else G.at[slot, 0, low]
                pltpu.make_async_copy(src, src, send_sem.at[slot, way, step]).wait()

    SQ[...] = jnp.zeros_like(SQ)

    def tile_step(k):
        wk = k + tiles
        slot = lax.rem(wk, 2)
        base = lax.rem(k, 2) * 3
        prev = 3 - base
        u0 = 3 * k
        p0 = u0 - 3
        last_layer = k < tiles
        going = k >= 1
        pt = lax.rem(k - 1 + tiles, tiles)
        pl_layer = jnp.where(k - 1 < tiles, 1, 0)
        fetched(wk)

        @pl.when(k < 2 * tiles - 1)
        def _():
            fetch(wk + 1)

        def hidden(i):
            b, j = i // 2, lax.rem(i, 2)
            here = at(j, cols)
            g = dot(A[tok(b), :], WG[slot, :, here])
            u = dot(A[tok(b), :], WU[slot, :, here])
            back = dot_t(D[tok(b), :], WD[slot, here, :]).astype(BF16).astype(F32)
            s = 0.5 * jnp.tanh(0.5 * g) + 0.5
            silu = g * s
            ACT[tok(b), here] = (silu * u).astype(BF16)
            DU[tok(b), here] = (back * silu).astype(BF16)
            DG[tok(b), here] = (back * u * (s + silu * (1.0 - s))).astype(BF16)

            @pl.when(going & (i == 0))
            def _():
                second(p0 + 2, prev + 2)

            @pl.when(going & (lax.rem(i, 2) == 1))
            def _():
                e = i // 2
                j3 = lax.rem(e, 3)
                later(p0 + j3, prev + j3, 2 + e // 3)

        loop(2 * blocks, hidden)

        def down_part(i):
            part = dot(DT[...], ACT[:, at(i, strip)])
            flipped = part.T.astype(BF16)
            for b in range(strip // LANES):
                G[base, i * (strip // LANES) + b] = flipped[b * LANES : (b + 1) * LANES]

            @pl.when(going & (lax.rem(i, 2) == 1))
            def _():
                j3 = 1 + i // 2
                later(p0 + j3, prev + j3, 3)

        loop(4, down_part)
        begin(u0, base)

        def wide_part(src, unit, i):
            part = dot(AT[...], src[:, at(i, strip)]).astype(BF16)
            G[base + unit, :, at(i // 2, hr), at(lax.rem(i, 2), strip)] = part.reshape(n, dim // n, strip)

        def gate_part(i):
            wide_part(DG, 1, i)

            @pl.when(going & (i == 0))
            def _():
                finish(p0, prev, 0, pl_layer, pt)

            @pl.when(going & (i == 2))
            def _():
                finish(p0 + 1, prev + 1, 1, pl_layer, pt)

        loop(4, gate_part)
        begin(u0 + 1, base + 1)
        second(u0, base)

        def up_part(i):
            wide_part(DU, 2, i)

            @pl.when(going & (i == 1))
            def _():
                finish(p0 + 2, prev + 2, 2, pl_layer, pt)

        loop(4, up_part)
        begin(u0 + 2, base + 2)

        @pl.when(k == tiles - 1)
        def _():
            loop(blocks, lambda i: x_again(i).start())

        @pl.when(last_layer)
        def _():
            def input_part(i):
                DA[tok(i), :] += dot_t(DG[tok(i), :], WG[slot]) + dot_t(DU[tok(i), :], WU[slot])

            loop(blocks, input_part)

        second(u0 + 1, base + 1)

        @pl.when(k == tiles - 1)
        def _():
            def between(i):
                h = H[tok(i), :].astype(F32)
                da = DA[tok(i), :].astype(BF16).astype(F32)
                r = scale_of(h)
                dh = (r * da - h * (r * r * r * jnp.mean(h * da, -1, keepdims=True))).astype(BF16)
                d = (D[tok(i), :].astype(F32) + dh.astype(F32)).astype(BF16)
                D[tok(i), :] = d
                DT[:, tok(i)] = d.T
                x_again(i).wait()
                wide = ACT[tok(i), pl.ds(0, dim)].astype(F32)
                a = (wide * scale_of(wide)).astype(BF16)
                A[tok(i), :] = a
                AT[:, tok(i)] = a.T

            loop(blocks, between)

    loop(2 * tiles, tile_step)

    end = 2 * tiles - 1
    u0, base = 3 * end, (end % 2) * 3
    second(u0 + 2, base + 2)
    for step in range(2, half):
        loop(3, lambda j, step=step: later(u0 + j, base + j, step))
    for j in range(3):
        finish(u0 + j, base + j, j, 0, tiles - 1)

    outs = (
        pltpu.make_async_copy(OG, og_hbm, out_sem.at[0]),
        pltpu.make_async_copy(OU, ou_hbm, out_sem.at[1]),
        pltpu.make_async_copy(OD, od_hbm, out_sem.at[2]),
        pltpu.make_async_copy(SQ, sq_hbm, out_sem.at[3]),
    )
    for copy in outs:
        copy.start()
    for copy in outs:
        copy.wait()


def gradients(n, x, dy, w_gate, w_up, w_down):
    layers, dim, ff = w_gate.shape
    tokens = x.shape[1]
    blocks = 4
    share = ff // n
    tiles = share // LANES
    tile = n * LANES
    units = 3 * layers * tiles
    half = n // 2
    land = LANES // 2 + LANES * (half - 1)
    any_space = pl.BlockSpec(memory_space=pl.ANY)
    return pl.pallas_call(
        functools.partial(grad_kernel, n, layers, (tokens, dim, ff, blocks)),
        out_shape=(
            jax.ShapeDtypeStruct((layers, dim // n, ff), BF16),
            jax.ShapeDtypeStruct((layers, dim // n, ff), BF16),
            jax.ShapeDtypeStruct((layers, share, dim), BF16),
            jax.ShapeDtypeStruct((8, dim), F32),
        ),
        in_specs=[any_space] * 5,
        out_specs=(any_space,) * 4,
        scratch_shapes=[
            pltpu.VMEM((tokens, dim), BF16),
            pltpu.VMEM((dim, tokens), BF16),
            pltpu.VMEM((tokens, dim), BF16),
            pltpu.VMEM((dim, tokens), BF16),
            pltpu.VMEM((tokens, dim), BF16),
            pltpu.VMEM((tokens, tile), BF16),
            pltpu.VMEM((tokens, tile), BF16),
            pltpu.VMEM((tokens, tile), BF16),
            pltpu.VMEM((tokens, dim), F32),
            pltpu.VMEM((2, dim, tile), BF16),
            pltpu.VMEM((2, dim, tile), BF16),
            pltpu.VMEM((2, tile, dim), BF16),
            pltpu.VMEM((6, n, LANES, dim), BF16),
            pltpu.VMEM((units, land, dim), BF16),
            pltpu.VMEM((units, land, dim), BF16),
            pltpu.VMEM((layers, dim // n, ff), BF16),
            pltpu.VMEM((layers, dim // n, ff), BF16),
            pltpu.VMEM((layers, share, dim), BF16),
            pltpu.VMEM((8, dim), F32),
            pltpu.SemaphoreType.DMA((blocks,)),
            pltpu.SemaphoreType.DMA((blocks,)),
            pltpu.SemaphoreType.DMA((2, 3)),
            pltpu.SemaphoreType.DMA((4,)),
            pltpu.SemaphoreType.DMA((6, 2, half)),
            pltpu.SemaphoreType.DMA((units, 2, half)),
        ],
        compiler_params=pltpu.CompilerParams(collective_id=0, has_side_effects=True, vmem_limit_bytes=VMEM_LIMIT),
        name="grads",
    )(x, dy, w_gate, w_up, w_down)


def update_kernel(n, count, parts, *refs):
    g_hbm, w_hbm, m_hbm, v_hbm = (refs[i : i + 3] for i in (0, 3, 6, 9))
    sq_hbm = refs[12]
    nw_hbm, nm_hbm, nv_hbm = (refs[i : i + 3] for i in (13, 16, 19))
    G, W, M, V, N = (refs[i : i + 3] for i in (22, 25, 28, 31, 34))
    SQ, in_sem, sq_sem, sq_send, sq_recv, mv_sem, nw_sem, send_sem, recv_sem = refs[37:]
    me = lax.axis_index("dp")
    half = n // 2
    up, down = lax.rem(me + 1, n), lax.rem(me + n - 1, n)
    ring = lambda d: lax.rem(me + d + n, n)
    layers = G[0].shape[0]

    barrier = pltpu.get_barrier_semaphore()
    for d in range(1, n):
        pl.semaphore_signal(barrier, inc=1, device_id={"dp": ring(d)}, device_id_type=MESH)

    mine = pltpu.make_async_copy(sq_hbm, SQ.at[me], sq_sem)
    mine.start()
    loads = []
    for a in range(3):
        rows = G[a].shape[1]
        own = pl.ds(pl.multiple_of(me * rows, rows), rows)
        for l in range(layers):
            loads.append(
                (
                    pltpu.make_async_copy(g_hbm[a].at[l], G[a].at[l], in_sem.at[0, a, l]),
                    pltpu.make_async_copy(w_hbm[a].at[l, own, :], W[a].at[l], in_sem.at[1, a, l]),
                    pltpu.make_async_copy(m_hbm[a].at[l], M[a].at[l], in_sem.at[2, a, l]),
                    pltpu.make_async_copy(v_hbm[a].at[l], V[a].at[l], in_sem.at[3, a, l]),
                )
            )
            for copy in loads[-1]:
                copy.start()
    mine.wait()
    pl.semaphore_wait(barrier, n - 1)

    def tell(d):
        return pltpu.make_async_remote_copy(
            src_ref=SQ.at[me],
            dst_ref=SQ.at[me],
            send_sem=sq_send.at[d],
            recv_sem=sq_recv.at[d],
            device_id={"dp": ring(d)},
            device_id_type=MESH,
        )

    for d in range(1, n):
        tell(d).start()
    for d in range(1, n):
        tell(d).wait_recv()
    total = jnp.sum(jnp.sum(SQ[...], axis=0), axis=(0, 1), keepdims=True)
    factor = jnp.minimum(1.0, 0.5 * lax.rsqrt(total / count + 1e-30))

    def shape(a):
        rows, cols = G[a].shape[1:]
        return (rows, cols // parts, 0) if a < 2 else (rows // parts, cols, 1)

    def place(a, l, p, owner, part):
        rows = G[a].shape[1]
        r, c, split = shape(a)
        hr = r // 2
        start = owner * rows + (p * r if split else 0)
        start, size = (start, r) if part == 2 else (start + part * hr, hr)
        return (l, pl.ds(pl.multiple_of(start, hr), size), pl.ds(0 if split else p * c, c))

    def send(i, a, l, p, way, step):
        owner = ring(-step) if way == 0 else ring(step)
        ref = N[a].at[place(a, l, p, owner, 2 if step < half - 1 else way)]
        return pltpu.make_async_remote_copy(
            src_ref=ref,
            dst_ref=ref,
            send_sem=send_sem.at[i, way, step],
            recv_sem=recv_sem.at[i, way, step],
            device_id={"dp": (up, down)[way]},
            device_id_type=MESH,
        )

    def came(i, a, l, p, way, step):
        owner = ring(-step - 1) if way == 0 else ring(step + 1)
        where = place(a, l, p, owner, 2 if step < half - 1 else way)
        ref = N[a].at[where]
        pltpu.make_async_copy(ref, ref, recv_sem.at[i, way, step]).wait()
        pltpu.make_async_copy(ref, nw_hbm[a].at[where], nw_sem.at[a]).start()

    def adam(a, l, p):
        r, c, split = shape(a)
        rows = G[a].shape[1]
        step = 16
        lane = pl.ds(0 if split else p * c, c)

        def some(i):
            row = pl.ds(pl.multiple_of((p * r if split else 0) + i * step, step), step)
            g = G[a][l, row, lane].astype(F32) * factor
            m = 0.9 * M[a][l, row, lane] + 0.1 * g
            v = 0.95 * V[a][l, row, lane] + 0.05 * g * g
            M[a][l, row, lane] = m
            V[a][l, row, lane] = v
            w = W[a][l, row, lane].astype(F32)
            new = (w - 0.02 * (m * lax.rsqrt(v + 1e-8) + 0.1 * w)).astype(BF16)
            there = pl.ds(pl.multiple_of(me * rows + (p * r if split else 0) + i * step, step), step)
            N[a][l, there, lane] = new

        loop(r // step, some)

    chunks = []
    for l in reversed(range(layers)):
        for a in (2, 0, 1):
            for p in range(parts):
                chunks.append((len(chunks), a, l, p))
    for i, a, l, p in chunks:
        if p == 0:
            for copy in loads[a * layers + l]:
                copy.wait()
        adam(a, l, p)
        send(i, a, l, p, 0, 0).start()
        send(i, a, l, p, 1, 0).start()
        where = place(a, l, p, me, 2)
        pltpu.make_async_copy(N[a].at[where], nw_hbm[a].at[where], nw_sem.at[a]).start()
        if p == parts - 1:
            pltpu.make_async_copy(M[a].at[l], nm_hbm[a].at[l], mv_sem.at[0, a, l]).start()
            pltpu.make_async_copy(V[a].at[l], nv_hbm[a].at[l], mv_sem.at[1, a, l]).start()
    for step in range(half):
        for i, a, l, p in chunks:
            for way in range(2):
                came(i, a, l, p, way, step)
                if step < half - 1:
                    send(i, a, l, p, way, step + 1).start()
    for i, a, l, p in chunks:
        for way in range(2):
            for step in range(half):
                send(i, a, l, p, way, step).wait_send()
    for d in range(1, n):
        tell(d).wait_send()
    for a in range(3):
        for l in range(layers):
            pltpu.make_async_copy(M[a].at[l], nm_hbm[a].at[l], mv_sem.at[0, a, l]).wait()
            pltpu.make_async_copy(V[a].at[l], nv_hbm[a].at[l], mv_sem.at[1, a, l]).wait()
        pltpu.make_async_copy(N[a], nw_hbm[a], nw_sem.at[a]).wait()


def update(n, g, w, m, v, squares):
    layers = w[0].shape[0]
    parts = 2
    chunks = layers * 3 * parts
    count = sum(t.size for t in w)
    shard = [t.shape for t in m]
    any_space = pl.BlockSpec(memory_space=pl.ANY)
    half = n // 2
    return pl.pallas_call(
        functools.partial(update_kernel, n, float(count), parts),
        out_shape=tuple(jax.ShapeDtypeStruct(t.shape, BF16) for t in w) + tuple(jax.ShapeDtypeStruct(t.shape, F32) for t in m + v),
        in_specs=[any_space] * 13,
        out_specs=(any_space,) * 9,
        scratch_shapes=[pltpu.VMEM(s, d) for d in (BF16, BF16, F32, F32) for s in shard]
        + [pltpu.VMEM(t.shape, BF16) for t in w]
        + [
            pltpu.VMEM((n,) + squares.shape, F32),
            pltpu.SemaphoreType.DMA((4, 3, layers)),
            pltpu.SemaphoreType.DMA,
            pltpu.SemaphoreType.DMA((n,)),
            pltpu.SemaphoreType.DMA((n,)),
            pltpu.SemaphoreType.DMA((2, 3, layers)),
            pltpu.SemaphoreType.DMA((3,)),
            pltpu.SemaphoreType.DMA((chunks, 2, half)),
            pltpu.SemaphoreType.DMA((chunks, 2, half)),
        ],
        compiler_params=pltpu.CompilerParams(collective_id=1, has_side_effects=True, vmem_limit_bytes=VMEM_LIMIT),
        name="update",
    )(*g, *w, *m, *v, squares)


def solution(mesh):
    n = mesh.shape["dp"]

    def step(x, dy, *arrays):
        w, m, v = (arrays[i : i + 3] for i in (0, 3, 6))
        *g, squares = gradients(n, x, dy, *w)
        return update(n, g, w, m, v, squares)

    shard = P(None, "dp", None)
    return jax.shard_map(
        step,
        mesh=mesh,
        in_specs=(P(("rep", "dp"), None, None),) * 2 + (P(),) * 3 + (shard,) * 6,
        out_specs=(P("rep", None, None),) * 3 + (P("rep", "dp", None),) * 6,
        check_vma=False,
    )
```

time: 899 us -> 455 us (0.51)
  waiting for transfers between devices: 526 us -> 0 us
  Pallas kernels: 0 us -> 429 us
  matrix products: 225 us -> 0 us
  other arithmetic: 73.3 us -> 0.01 us
  between operations: 17.6 us -> 0.69 us
  blocking collectives: 16.7 us -> 0 us
    pallas_call x0 -> x2, Pallas kernels: none -> 429 us  [the longest x1 241 us: gradients(): pl.pallas_call(functools.partial(grad_kernel, n, layers, (tokens, dim, ff...]
    unnamed x15 -> x0, waiting for transfers between devices: 321 us -> none
    dot_general x15 -> x0, matrix products: 225 us -> none  [the longest x5 85.1 us: layer(): up = jnp.dot(a, w['w_up'], preferred_element_type=jnp.float32)]
    reshape x3 -> x0, waiting for transfers between devices: 205 us -> none  [step(): t.reshape(-1, *t.shape[2:])]
    unnamed x5 -> x1, other arithmetic: 46.6 us -> 0.01 us
    reduce_sum x1 -> x0, blocking collectives: 16.7 us -> none  [of_a_group(): jnp.sum(g * g)]
    reshape x3 -> x0, other arithmetic: 14.3 us -> none  [step(): t.reshape(-1, *t.shape[2:])]
    unnamed x41 -> x27, local copies, waits for them, and re-layouts: 30 us -> 24.8 us
  transfers between devices with their start and end apart: 9 -> 0, of which waited for: 8 -> 0; matrix products, arithmetic and copies ran while one was open for 14% -> 0% of each run, Pallas kernels for 0% -> 0%
where the time goes in v1:
time: 455 us
  Pallas kernels  429 us (94%)
  local copies, waits for them, and re-layouts  24.8 us (5%)
    pallas_call x1, Pallas kernels, gradients(): pl.pallas_call(functools.partial(grad_kernel, n, layers, (tokens, dim, ff...  241 us
    pallas_call x1, Pallas kernels, update(): pl.pallas_call(functools.partial(update_kernel, n, float(count), parts),...  188 us
    unnamed x27, local copies, waits for them, and re-layouts  24.8 us

profile of v1, /device:TPU:30, one launch (start us, length us, event | category | flops | bytes accessed | tf_op | source)
XLA Modules:
  0.0 454.6 jit_solution(5296756004158162278)
XLA Ops:
  0.6 241.0 %grads.1 = (bf16[2,64,3072]{2,1,0:T(8,128)(2,1)}, bf16[2,64,3072]{2,1,0:T(8,128)(2,1)}, bf16[2,384,512]{2,1,0:T(8,128)(2,1)}, f32[8,512]{1,0:T(8,128)}) custom-call(bf16[1,2048,512]{2,1,0:T(8,128)(2,1)} %refs_0_.1, bf16[1,2048,512]{2,1,0:T(8,128)(2,1)} %refs_1_.1, bf16[2,512,3072]{2,1,0:T(8,128)(2,1)} %refs_3_.3, bf16[2,512,3072]{2,1,0:T(8,128)(2,1)} %refs_4_.3, ...), custom_call_target="tpu_custom_call" | custom-call | tf_op jit(solution)/shard_map/grads/pallas_call | solution.py:350
  241.6 188.2 %update.1 = (bf16[2,512,3072]{2,1,0:T(8,128)(2,1)}, bf16[2,512,3072]{2,1,0:T(8,128)(2,1)}, bf16[2,3072,512]{2,1,0:T(8,128)(2,1)}, f32[2,64,3072]{2,1,0:T(8,128)}...) custom-call(bf16[2,64,3072]{2,1,0:T(8,128)(2,1)} %get-tuple-element., ...), custom_call_target="tpu_custom_call" | custom-call | tf_op jit(solution)/shard_map/update/pallas_call | solution.py:540
  429.8 0.0 copy-start
  429.8 0.0 slice-start
  429.8 6.6 %copy.29 = bf16[2,512,3072]{2,1,0:T(8,128)(2,1)} copy(bf16[2,512,3072]{2,1,0:T(8,128)(2,1)} %get-tuple-element.26) | data formatting | bytes 12582912
  436.4 0.0 copy-done
  436.4 0.0 slice-start.1
  436.4 3.2 copy.30
  439.6 0.0 slice-done
  439.6 1.3 slice-done.1
  440.9 0.0 copy-start.6
  440.9 2.7 copy.31
  443.6 0.0 copy-done.6
  443.6 0.0 copy-start.5
  443.6 1.1 copy.32
  444.8 0.8 copy-done.5
  445.6 0.0 copy-start.4
  445.6 1.1 copy.33
  446.7 0.8 copy-done.4
  447.6 0.0 copy-start.3
  447.6 1.1 copy.34
  448.7 0.8 copy-done.3
  449.6 0.0 copy-start.2
  449.6 1.1 copy.35
  450.7 0.8 copy-done.2
  451.5 0.0 copy-start.1
  451.5 1.1 copy.36
  452.7 0.8 copy-done.1
  453.5 1.1 copy.37
  (1 shorter events, 0.0 us)
Async XLA Ops:
  429.8 6.6 %copy-start = (bf16[2,512,3072]{2,1,0:T(8,128)(2,1)S(1)}, bf16[2,512,3072]{2,1,0:T(8,128)(2,1)}, u32[]{:S(2)}) copy-start(bf16[2,512,3072]{2,1,0:T(8,128)(2,1)} %get-tuple-element.27) | copy-start | bytes 18874372
  429.8 9.8 %slice-start = ((s8[6291456]{0:T(1024)(128)(4,1)}), s8[4194304]{0:T(1024)(128)(4,1)S(1)}, s32[]{:S(2)}) async-start(s8[6291456]{0:T(1024)(128)(4,1)} %bitcast), calls=%async_computation | async-start | bytes 8388608
  436.4 4.5 slice-start.1
  440.9 2.7 copy-start.6
  443.6 2.0 copy-start.5
  445.6 2.0 copy-start.4
  447.6 2.0 copy-start.3
  449.6 2.0 copy-start.2
  451.5 2.0 copy-start.1

commit v2 on v1

--- a/solution.py
+++ b/solution.py
@@ -26,6 +26,14 @@
     return lax.rsqrt(jnp.mean(wide * wide, -1, keepdims=True) + 1e-6)
 
 
+def pinned(t, space):
+    return pltpu.with_memory_space_constraint(t, space)
+
+
+def kept(t, dtype):
+    return pltpu.VMEM(t.shape, dtype)
+
+
 def loop(count, body):
     lax.fori_loop(0, count, lambda i, c: (body(i), c)[1], 0)
 
@@ -37,7 +45,8 @@
 def grad_kernel(n, layers, shapes, *refs):
     (x_hbm, dy_hbm, wg_hbm, wu_hbm, wd_hbm) = refs[:5]
     (og_hbm, ou_hbm, od_hbm, sq_hbm) = refs[5:9]
-    (A, AT, D, DT, H, ACT, DG, DU, DA, WG, WU, WD, G, RU, RD, OG, OU, OD, SQ, x_sem, dy_sem, w_sem, out_sem, send_sem, recv_sem) = refs[9:]
+    (A, AT, D, DT, H, ACT, DG, DU, DA, WG, WU, WD, G, RU, RD, OG, OU, OD, SQ, ALL, *sems) = refs[9:]
+    x_sem, dy_sem, w_sem, out_sem, send_sem, recv_sem, sq_send, sq_recv = sems
     tokens, dim, ff, blocks = shapes
     share = ff // n
     tiles = share // LANES
@@ -46,7 +55,6 @@
     half = n // 2
     hr = LANES // 2
     cols = tile // 2
-    strip = tile // 4
     me = lax.axis_index("dp")
     up, down = lax.rem(me + 1, n), lax.rem(me + n - 1, n)
     ring = lambda d: lax.rem(me + d + n, n)
@@ -84,8 +92,8 @@
         return pltpu.make_async_copy(dy_hbm.at[0, tok(i), :], D.at[tok(i), :], dy_sem.at[i])
 
     barrier = pltpu.get_barrier_semaphore()
-    for peer in (up, down):
-        pl.semaphore_signal(barrier, inc=1, device_id={"dp": peer}, device_id_type=MESH)
+    for d in range(1, n):
+        pl.semaphore_signal(barrier, inc=1, device_id={"dp": ring(d)}, device_id_type=MESH)
 
     loop(blocks, lambda i: x_copy(i).start())
     fetch(0)
@@ -130,7 +138,7 @@
 
     loop(blocks, second_norm)
 
-    pl.semaphore_wait(barrier, 2)
+    pl.semaphore_wait(barrier, n - 1)
 
     def remote(src, dst, slot, u, way, step):
         return pltpu.make_async_remote_copy(
@@ -148,12 +156,13 @@
     def rows(step):
         return pl.ds(pl.multiple_of(hr + (step - 1) * 2 * hr, hr), 2 * hr)
 
-    def begin(u, slot):
-        far = ring(half)
-        remote(G.at[slot, far, low], RU.at[u, low], slot, u, 0, 0).start()
-        remote(G.at[slot, far, high], RD.at[u, low], slot, u, 1, 0).start()
+    def begin_low(u, slot):
+        remote(G.at[slot, ring(half), low], RU.at[u, low], slot, u, 0, 0).start()
+        remote(G.at[slot, ring(1 - half), low], RD.at[u, pl.ds(hr, hr)], slot, u, 1, 1).start()
+
+    def begin_high(u, slot):
+        remote(G.at[slot, ring(half), high], RD.at[u, low], slot, u, 1, 0).start()
         remote(G.at[slot, ring(half - 1), high], RU.at[u, pl.ds(2 * hr, hr)], slot, u, 0, 1).start()
-        remote(G.at[slot, ring(1 - half), low], RD.at[u, pl.ds(hr, hr)], slot, u, 1, 1).start()
 
     def received(u, way, step):
         dst = lands[way].at[u, low] if isinstance(step, int) and step == 0 else lands[way].at[u, rows(step)]
@@ -162,12 +171,14 @@
     def add(land, place, mine):
         land[place] = (land[place].astype(F32) + mine.astype(F32)).astype(BF16)
 
-    def second(u, slot):
+    def second_low(u, slot):
         received(u, 0, 0)
+        add(RU, (u, low), G[slot, ring(half - 1), low])
+        remote(RU.at[u, low], RU.at[u, pl.ds(hr, hr)], slot, u, 0, 1).start()
+
+    def second_high(u, slot):
         received(u, 1, 0)
-        add(RU, (u, low), G[slot, ring(half - 1), low])
         add(RD, (u, low), G[slot, ring(1 - half), high])
-        remote(RU.at[u, low], RU.at[u, pl.ds(hr, hr)], slot, u, 0, 1).start()
         remote(RD.at[u, low], RD.at[u, pl.ds(2 * hr, hr)], slot, u, 1, 1).start()
 
     def later(u, slot, step):
@@ -206,95 +217,134 @@
         prev = 3 - base
         u0 = 3 * k
         p0 = u0 - 3
-        last_layer = k < tiles
         going = k >= 1
-        pt = lax.rem(k - 1 + tiles, tiles)
-        pl_layer = jnp.where(k - 1 < tiles, 1, 0)
+        old_t = lax.rem(k - 1 + tiles, tiles)
+        old_layer = jnp.where(k - 1 < tiles, 1, 0)
         fetched(wk)
 
         @pl.when(k < 2 * tiles - 1)
         def _():
             fetch(wk + 1)
 
-        def hidden(i):
-            b, j = i // 2, lax.rem(i, 2)
+        def when(cond):
+            return pl.when(going & cond)
+
+        def hidden(j, i):
             here = at(j, cols)
-            g = dot(A[tok(b), :], WG[slot, :, here])
-            u = dot(A[tok(b), :], WU[slot, :, here])
-            back = dot_t(D[tok(b), :], WD[slot, here, :]).astype(BF16).astype(F32)
-            s = 0.5 * jnp.tanh(0.5 * g) + 0.5
-            silu = g * s
-            ACT[tok(b), here] = (silu * u).astype(BF16)
-            DU[tok(b), here] = (back * silu).astype(BF16)
-            DG[tok(b), here] = (back * u * (s + silu * (1.0 - s))).astype(BF16)
-
-            @pl.when(going & (i == 0))
-            def _():
-                second(p0 + 2, prev + 2)
-
-            @pl.when(going & (lax.rem(i, 2) == 1))
-            def _():
-                e = i // 2
-                j3 = lax.rem(e, 3)
-                later(p0 + j3, prev + j3, 2 + e // 3)
-
-        loop(2 * blocks, hidden)
-
-        def down_part(i):
-            part = dot(DT[...], ACT[:, at(i, strip)])
+            for b in range(2):
+                place = tok(2 * i + b)
+                g = dot(A[place, :], WG[slot, :, here])
+                u = dot(A[place, :], WU[slot, :, here])
+                back = dot_t(D[place, :], WD[slot, here, :]).astype(BF16).astype(F32)
+                s = 0.5 * jnp.tanh(0.5 * g) + 0.5
+                silu = g * s
+                ACT[place, here] = (silu * u).astype(BF16)
+                DU[place, here] = (back * silu).astype(BF16)
+                DG[place, here] = (back * u * (s + silu * (1.0 - s))).astype(BF16)
+
+        def wide_part(src, unit, j):
+            part = dot(AT[...], src[:, at(j, cols)]).astype(BF16)
+            G[base + unit, :, at(j, hr), :] = part.reshape(n, dim // n, cols)
+
+        def halves(j):
+            def some(i):
+                hidden(j, i)
+
+                @when((j == 0) & (i == 0))
+                def _():
+                    later(p0 + 1, prev + 1, 3)
+
+            loop(blocks // 2, some)
+
+            @when(j == 1)
+            def _():
+                finish(p0 + 1, prev + 1, 1, old_layer, old_t)
+
+            wide_part(DG, 1, j)
+
+            @pl.when(j == 0)
+            def _():
+                begin_low(u0 + 1, base + 1)
+
+            @when(j == 0)
+            def _():
+                later(p0, prev, 2)
+
+            @pl.when(j == 1)
+            def _():
+                begin_high(u0 + 1, base + 1)
+
+            @when(j == 1)
+            def _():
+                later(p0, prev, 3)
+
+            @pl.when(j == 1)
+            def _():
+                second_low(u0 + 1, base + 1)
+
+            wide_part(DU, 2, j)
+
+            @pl.when(j == 0)
+            def _():
+                begin_low(u0 + 2, base + 2)
+
+            @when(j == 0)
+            def _():
+                later(p0 + 2, prev + 2, 3)
+
+            @pl.when(j == 1)
+            def _():
+                begin_high(u0 + 2, base + 2)
+                second_low(u0 + 2, base + 2)
+
+        loop(2, halves)
+
+        def down_part(j):
+            part = dot(DT[...], ACT[:, at(j, cols)])
             flipped = part.T.astype(BF16)
-            for b in range(strip // LANES):
-                G[base, i * (strip // LANES) + b] = flipped[b * LANES : (b + 1) * LANES]
-
-            @pl.when(going & (lax.rem(i, 2) == 1))
-            def _():
-                j3 = 1 + i // 2
-                later(p0 + j3, prev + j3, 3)
-
-        loop(4, down_part)
-        begin(u0, base)
-
-        def wide_part(src, unit, i):
-            part = dot(AT[...], src[:, at(i, strip)]).astype(BF16)
-            G[base + unit, :, at(i // 2, hr), at(lax.rem(i, 2), strip)] = part.reshape(n, dim // n, strip)
-
-        def gate_part(i):
-            wide_part(DG, 1, i)
-
-            @pl.when(going & (i == 0))
-            def _():
-                finish(p0, prev, 0, pl_layer, pt)
-
-            @pl.when(going & (i == 2))
-            def _():
-                finish(p0 + 1, prev + 1, 1, pl_layer, pt)
-
-        loop(4, gate_part)
-        begin(u0 + 1, base + 1)
-        second(u0, base)
-
-        def up_part(i):
-            wide_part(DU, 2, i)
-
-            @pl.when(going & (i == 1))
-            def _():
-                finish(p0 + 2, prev + 2, 2, pl_layer, pt)
-
-        loop(4, up_part)
-        begin(u0 + 2, base + 2)
+            for b in range(cols // LANES):
+                G[base, j * (cols // LANES) + b] = flipped[b * LANES : (b + 1) * LANES]
+
+            @pl.when(j == 0)
+            def _():
+                second_high(u0 + 1, base + 1)
+
+            @when(j == 0)
+            def _():
+                finish(p0 + 2, prev + 2, 2, old_layer, old_t)
+
+        loop(2, down_part)
+        begin_low(u0, base)
+        begin_high(u0, base)
 
         @pl.when(k == tiles - 1)
         def _():
             loop(blocks, lambda i: x_again(i).start())
 
-        @pl.when(last_layer)
+        def ring_part(i):
+            @pl.when(i == 1)
+            def _():
+                second_high(u0 + 2, base + 2)
+
+            @when(i == 1)
+            def _():
+                finish(p0, prev, 0, old_layer, old_t)
+
+            @pl.when(i == 2)
+            def _():
+                later(u0 + 1, base + 1, 2)
+
+        @pl.when(k < tiles)
         def _():
             def input_part(i):
                 DA[tok(i), :] += dot_t(DG[tok(i), :], WG[slot]) + dot_t(DU[tok(i), :], WU[slot])
+                ring_part(i)
 
             loop(blocks, input_part)
 
-        second(u0 + 1, base + 1)
+        @pl.when(k >= tiles)
+        def _():
+            loop(blocks, ring_part)
 
         @pl.when(k == tiles - 1)
         def _():
@@ -314,25 +364,51 @@
 
             loop(blocks, between)
 
+        second_low(u0, base)
+        second_high(u0, base)
+        later(u0 + 2, base + 2, 2)
+
     loop(2 * tiles, tile_step)
 
     end = 2 * tiles - 1
     u0, base = 3 * end, (end % 2) * 3
-    second(u0 + 2, base + 2)
-    for step in range(2, half):
-        loop(3, lambda j, step=step: later(u0 + j, base + j, step))
-    for j in range(3):
+    later(u0 + 1, base + 1, 3)
+    later(u0, base, 2)
+    later(u0 + 2, base + 2, 3)
+    later(u0, base, 3)
+    for j in (1, 2, 0):
         finish(u0 + j, base + j, j, 0, tiles - 1)
+
+    squares = SQ[:, :LANES]
+    for j in range(1, dim // LANES):
+        squares += SQ[:, j * LANES : (j + 1) * LANES]
+    ALL[me] = squares
 
     outs = (
         pltpu.make_async_copy(OG, og_hbm, out_sem.at[0]),
         pltpu.make_async_copy(OU, ou_hbm, out_sem.at[1]),
         pltpu.make_async_copy(OD, od_hbm, out_sem.at[2]),
-        pltpu.make_async_copy(SQ, sq_hbm, out_sem.at[3]),
     )
     for copy in outs:
         copy.start()
-    for copy in outs:
+
+    def tell(d):
+        return pltpu.make_async_remote_copy(
+            src_ref=ALL.at[me],
+            dst_ref=ALL.at[me],
+            send_sem=sq_send.at[d],
+            recv_sem=sq_recv.at[d],
+            device_id={"dp": ring(d)},
+            device_id_type=MESH,
+        )
+
+    for d in range(1, n):
+        tell(d).start()
+    for d in range(1, n):
+        tell(d).wait()
+    last = pltpu.make_async_copy(ALL, sq_hbm, out_sem.at[3])
+    last.start()
+    for copy in outs + (last,):
         copy.wait()
 
 
@@ -353,7 +429,7 @@
             jax.ShapeDtypeStruct((layers, dim // n, ff), BF16),
             jax.ShapeDtypeStruct((layers, dim // n, ff), BF16),
             jax.ShapeDtypeStruct((layers, share, dim), BF16),
-            jax.ShapeDtypeStruct((8, dim), F32),
+            jax.ShapeDtypeStruct((n, 8, LANES), F32),
         ),
         in_specs=[any_space] * 5,
         out_specs=(any_space,) * 4,
@@ -377,12 +453,15 @@
             pltpu.VMEM((layers, dim // n, ff), BF16),
             pltpu.VMEM((layers, share, dim), BF16),
             pltpu.VMEM((8, dim), F32),
+            pltpu.VMEM((n, 8, LANES), F32),
             pltpu.SemaphoreType.DMA((blocks,)),
             pltpu.SemaphoreType.DMA((blocks,)),
             pltpu.SemaphoreType.DMA((2, 3)),
             pltpu.SemaphoreType.DMA((4,)),
             pltpu.SemaphoreType.DMA((6, 2, half)),
             pltpu.SemaphoreType.DMA((units, 2, half)),
+            pltpu.SemaphoreType.DMA((n,)),
+            pltpu.SemaphoreType.DMA((n,)),
         ],
         compiler_params=pltpu.CompilerParams(collective_id=0, has_side_effects=True, vmem_limit_bytes=VMEM_LIMIT),
         name="grads",
@@ -392,9 +471,9 @@
 def update_kernel(n, count, parts, *refs):
     g_hbm, w_hbm, m_hbm, v_hbm = (refs[i : i + 3] for i in (0, 3, 6, 9))
     sq_hbm = refs[12]
-    nw_hbm, nm_hbm, nv_hbm = (refs[i : i + 3] for i in (13, 16, 19))
-    G, W, M, V, N = (refs[i : i + 3] for i in (22, 25, 28, 31, 34))
-    SQ, in_sem, sq_sem, sq_send, sq_recv, mv_sem, nw_sem, send_sem, recv_sem = refs[37:]
+    N, M, V = (refs[i : i + 3] for i in (13, 16, 19))
+    G, W = (refs[i : i + 3] for i in (22, 25))
+    SQ, in_sem, sq_sem, send_sem, recv_sem = refs[28:]
     me = lax.axis_index("dp")
     half = n // 2
     up, down = lax.rem(me + 1, n), lax.rem(me + n - 1, n)
@@ -402,43 +481,25 @@
     layers = G[0].shape[0]
 
     barrier = pltpu.get_barrier_semaphore()
-    for d in range(1, n):
-        pl.semaphore_signal(barrier, inc=1, device_id={"dp": ring(d)}, device_id_type=MESH)
-
-    mine = pltpu.make_async_copy(sq_hbm, SQ.at[me], sq_sem)
-    mine.start()
-    loads = []
-    for a in range(3):
-        rows = G[a].shape[1]
-        own = pl.ds(pl.multiple_of(me * rows, rows), rows)
-        for l in range(layers):
-            loads.append(
-                (
-                    pltpu.make_async_copy(g_hbm[a].at[l], G[a].at[l], in_sem.at[0, a, l]),
-                    pltpu.make_async_copy(w_hbm[a].at[l, own, :], W[a].at[l], in_sem.at[1, a, l]),
-                    pltpu.make_async_copy(m_hbm[a].at[l], M[a].at[l], in_sem.at[2, a, l]),
-                    pltpu.make_async_copy(v_hbm[a].at[l], V[a].at[l], in_sem.at[3, a, l]),
-                )
+    for peer in (up, down):
+        pl.semaphore_signal(barrier, inc=1, device_id={"dp": peer}, device_id_type=MESH)
+
+    squares = pltpu.make_async_copy(sq_hbm, SQ, sq_sem)
+    squares.start()
+    loads = {}
+    for l in reversed(range(layers)):
+        for a in (2, 0, 1):
+            rows = G[a].shape[1]
+            own = pl.ds(pl.multiple_of(me * rows, rows), rows)
+            loads[a, l] = (
+                pltpu.make_async_copy(g_hbm[a].at[l], G[a].at[l], in_sem.at[0, a, l]),
+                pltpu.make_async_copy(w_hbm[a].at[l, own, :], W[a].at[l], in_sem.at[1, a, l]),
+                pltpu.make_async_copy(m_hbm[a].at[l], M[a].at[l], in_sem.at[2, a, l]),
+                pltpu.make_async_copy(v_hbm[a].at[l], V[a].at[l], in_sem.at[3, a, l]),
             )
-            for copy in loads[-1]:
+            for copy in loads[a, l]:
                 copy.start()
-    mine.wait()
-    pl.semaphore_wait(barrier, n - 1)
-
-    def tell(d):
-        return pltpu.make_async_remote_copy(
-            src_ref=SQ.at[me],
-            dst_ref=SQ.at[me],
-            send_sem=sq_send.at[d],
-            recv_sem=sq_recv.at[d],
-            device_id={"dp": ring(d)},
-            device_id_type=MESH,
-        )
-
-    for d in range(1, n):
-        tell(d).start()
-    for d in range(1, n):
-        tell(d).wait_recv()
+    squares.wait()
     total = jnp.sum(jnp.sum(SQ[...], axis=0), axis=(0, 1), keepdims=True)
     factor = jnp.minimum(1.0, 0.5 * lax.rsqrt(total / count + 1e-30))
 
@@ -471,7 +532,6 @@
         where = place(a, l, p, owner, 2 if step < half - 1 else way)
         ref = N[a].at[where]
         pltpu.make_async_copy(ref, ref, recv_sem.at[i, way, step]).wait()
-        pltpu.make_async_copy(ref, nw_hbm[a].at[where], nw_sem.at[a]).start()
 
     def adam(a, l, p):
         r, c, split = shape(a)
@@ -500,16 +560,13 @@
                 chunks.append((len(chunks), a, l, p))
     for i, a, l, p in chunks:
         if p == 0:
-            for copy in loads[a * layers + l]:
+            for copy in loads[a, l]:
                 copy.wait()
         adam(a, l, p)
+        if i == 0:
+            pl.semaphore_wait(barrier, 2)
         send(i, a, l, p, 0, 0).start()
         send(i, a, l, p, 1, 0).start()
-        where = place(a, l, p, me, 2)
-        pltpu.make_async_copy(N[a].at[where], nw_hbm[a].at[where], nw_sem.at[a]).start()
-        if p == parts - 1:
-            pltpu.make_async_copy(M[a].at[l], nm_hbm[a].at[l], mv_sem.at[0, a, l]).start()
-            pltpu.make_async_copy(V[a].at[l], nv_hbm[a].at[l], mv_sem.at[1, a, l]).start()
     for step in range(half):
         for i, a, l, p in chunks:
             for way in range(2):
@@ -520,13 +577,28 @@
         for way in range(2):
             for step in range(half):
                 send(i, a, l, p, way, step).wait_send()
-    for d in range(1, n):
-        tell(d).wait_send()
-    for a in range(3):
-        for l in range(layers):
-            pltpu.make_async_copy(M[a].at[l], nm_hbm[a].at[l], mv_sem.at[0, a, l]).wait()
-            pltpu.make_async_copy(V[a].at[l], nv_hbm[a].at[l], mv_sem.at[1, a, l]).wait()
-        pltpu.make_async_copy(N[a], nw_hbm[a], nw_sem.at[a]).wait()
+
+
+def store_kernel(count, *refs):
+    src, dst, sem = refs[:count], refs[count : 2 * count], refs[-1]
+    copies = [pltpu.make_async_copy(a, b, sem.at[i]) for i, (a, b) in enumerate(zip(src, dst, strict=True))]
+    for copy in copies:
+        copy.start()
+    for copy in copies:
+        copy.wait()
+
+
+def store(arrays):
+    count = len(arrays)
+    return pl.pallas_call(
+        functools.partial(store_kernel, count),
+        out_shape=tuple(jax.ShapeDtypeStruct(t.shape, t.dtype) for t in arrays),
+        in_specs=[pl.BlockSpec(memory_space=pltpu.VMEM)] * count,
+        out_specs=(pl.BlockSpec(memory_space=pl.ANY),) * count,
+        scratch_shapes=[pltpu.SemaphoreType.DMA((count,))],
+        compiler_params=pltpu.CompilerParams(vmem_limit_bytes=2**20),
+        name="store",
+    )(*(pinned(t, pltpu.VMEM) for t in arrays))
 
 
 def update(n, g, w, m, v, squares):
@@ -539,25 +611,20 @@
     half = n // 2
     return pl.pallas_call(
         functools.partial(update_kernel, n, float(count), parts),
-        out_shape=tuple(jax.ShapeDtypeStruct(t.shape, BF16) for t in w) + tuple(jax.ShapeDtypeStruct(t.shape, F32) for t in m + v),
+        out_shape=tuple(kept(t, BF16) for t in w) + tuple(kept(t, F32) for t in m + v),
         in_specs=[any_space] * 13,
-        out_specs=(any_space,) * 9,
-        scratch_shapes=[pltpu.VMEM(s, d) for d in (BF16, BF16, F32, F32) for s in shard]
-        + [pltpu.VMEM(t.shape, BF16) for t in w]
+        out_specs=(pl.BlockSpec(memory_space=pltpu.VMEM),) * 9,
+        scratch_shapes=[pltpu.VMEM(s, BF16) for _ in range(2) for s in shard]
         + [
-            pltpu.VMEM((n,) + squares.shape, F32),
+            pltpu.VMEM(squares.shape, F32),
             pltpu.SemaphoreType.DMA((4, 3, layers)),
             pltpu.SemaphoreType.DMA,
-            pltpu.SemaphoreType.DMA((n,)),
-            pltpu.SemaphoreType.DMA((n,)),
-            pltpu.SemaphoreType.DMA((2, 3, layers)),
-            pltpu.SemaphoreType.DMA((3,)),
             pltpu.SemaphoreType.DMA((chunks, 2, half)),
             pltpu.SemaphoreType.DMA((chunks, 2, half)),
         ],
-        compiler_params=pltpu.CompilerParams(collective_id=1, has_side_effects=True, vmem_limit_bytes=VMEM_LIMIT),
+        compiler_params=pltpu.CompilerParams(collective_id=1, has_side_effects=True, vmem_limit_bytes=12 * 2**20),
         name="update",
-    )(*g, *w, *m, *v, squares)
+    )(*(pinned(t, pltpu.HBM) for t in (*g, *w, *m, *v, squares)))
 
 
 def solution(mesh):
@@ -566,7 +633,7 @@
     def step(x, dy, *arrays):
         w, m, v = (arrays[i : i + 3] for i in (0, 3, 6))
         *g, squares = gradients(n, x, dy, *w)
-        return update(n, g, w, m, v, squares)
+        return store(update(n, g, w, m, v, squares))
 
     shard = P(None, "dp", None)
     return jax.shard_map(

time: 455 us -> 426 us (0.936)
  local copies, waits for them, and re-layouts: 24.8 us -> 0 us
    unnamed x27 -> x0, local copies, waits for them, and re-layouts: 24.8 us -> none
    pallas_call x1, Pallas kernels: 241 us -> 231 us  [gradients(): pl.pallas_call(functools.partial(grad_kernel, n, layers, (tokens, dim, ff...]
    pallas_call x0 -> x1, Pallas kernels: none -> 9.45 us  [store(): pl.pallas_call(functools.partial(store_kernel, count), out_shape=tuple((j...]
where the time goes in v2:
time: 426 us
  Pallas kernels  425 us (100%)
    pallas_call x1, Pallas kernels, gradients(): pl.pallas_call(functools.partial(grad_kernel, n, layers, (tokens, dim, ff...  231 us
    pallas_call x1, Pallas kernels, update(): pl.pallas_call(functools.partial(update_kernel, n, float(count), parts),...  184 us
    pallas_call x1, Pallas kernels, store(): pl.pallas_call(functools.partial(store_kernel, count), out_shape=tuple((j...  9.45 us

profile of v2, /device:TPU:30, one launch (start us, length us, event | category | flops | bytes accessed | tf_op | source)
XLA Modules:
  0.0 425.8 jit_solution(14415762600123174548)
XLA Ops:
  0.6 231.3 %grads.1 = (bf16[2,64,3072]{2,1,0:T(8,128)(2,1)}, bf16[2,64,3072]{2,1,0:T(8,128)(2,1)}, bf16[2,384,512]{2,1,0:T(8,128)(2,1)}, f32[8,8,128]{2,1,0:T(8,128)}) custom-call(bf16[1,2048,512]{2,1,0:T(8,128)(2,1)} %refs_0_.1, bf16[1,2048,512]{2,1,0:T(8,128)(2,1)} %refs_1_.1, bf16[2,512,3072]{2,1,0:T(8,128)(2,1)} %refs_3_.3, bf16[2,512,3072]{2,1,0:T(8,128)(2,1)} %refs_4_.3, ...), custom_call_target="tpu_custom_call" | custom-call | tf_op jit(solution)/shard_map/grads/pallas_call | solution.py:426
  231.9 184.4 %update.1 = (bf16[2,512,3072]{2,1,0:T(8,128)(2,1)S(1)}, bf16[2,512,3072]{2,1,0:T(8,128)(2,1)S(1)}, bf16[2,3072,512]{2,1,0:T(8,128)(2,1)S(1)}, f32[2,64,3072]{2,1...) custom-call(bf16[2,64,3072]{2,1,0:T(8,128)(2,1)} %get-tuple-element., ...), custom_call_target="tpu_custom_call" | custom-call | tf_op jit(solution)/shard_map/update/pallas_call | solution.py:612
  416.3 9.4 %store.1 = (bf16[2,512,3072]{2,1,0:T(8,128)(2,1)}, bf16[2,512,3072]{2,1,0:T(8,128)(2,1)}, bf16[2,3072,512]{2,1,0:T(8,128)(2,1)}, f32[2,64,3072]{2,1,0:T(8,128)},...) custom-call(bf16[2,512,3072]{2,1,0:T(8,128)(2,1)S(1)} %get-tuple-ele, ...), custom_call_target="tpu_custom_call" | custom-call | tf_op jit(solution)/shard_map/store/pallas_call | solution.py:593

commit v3 on v2

--- a/solution.py
+++ b/solution.py
@@ -30,8 +30,8 @@
     return pltpu.with_memory_space_constraint(t, space)
 
 
-def kept(t, dtype):
-    return pltpu.VMEM(t.shape, dtype)
+def kept(shape, dtype):
+    return pltpu.VMEM(shape, dtype)
 
 
 def loop(count, body):
@@ -43,10 +43,10 @@
 
 
 def grad_kernel(n, layers, shapes, *refs):
-    (x_hbm, dy_hbm, wg_hbm, wu_hbm, wd_hbm) = refs[:5]
-    (og_hbm, ou_hbm, od_hbm, sq_hbm) = refs[5:9]
-    (A, AT, D, DT, H, ACT, DG, DU, DA, WG, WU, WD, G, RU, RD, OG, OU, OD, SQ, ALL, *sems) = refs[9:]
-    x_sem, dy_sem, w_sem, out_sem, send_sem, recv_sem, sq_send, sq_recv = sems
+    (x_hbm, dy_hbm, wg_hbm, wu_hbm, wd_hbm, md_hbm, vd_hbm) = refs[:7]
+    (OG, OU, OD, ALL, PW, PM, PV) = refs[7:14]
+    (A, AT, D, DT, H, ACT, DG, DU, DA, WG, WU, WD, G, RU, RD, SQ, *sems) = refs[14:]
+    x_sem, dy_sem, w_sem, ahead_sem, send_sem, recv_sem, sq_send, sq_recv = sems
     tokens, dim, ff, blocks = shapes
     share = ff // n
     tiles = share // LANES
@@ -100,30 +100,19 @@
     loop(blocks, lambda i: dy_copy(i).start())
 
     def first_norm(i):
-        x_copy(i).wait()
         wide = H[tok(i), :].astype(F32)
         A[tok(i), :] = (wide * scale_of(wide)).astype(BF16)
         DA[tok(i), :] = jnp.zeros((tb, dim), F32)
 
-    loop(blocks, first_norm)
-
-    def forward_tile(k):
+    def forward(k, i):
         slot = lax.rem(k, 2)
-        fetched(k)
-        fetch(k + 1)
-
-        def some(i):
-            for j in range(2):
-                here = pl.ds(j * cols, cols)
-                g = dot(A[tok(i), :], WG[slot, :, here])
-                u = dot(A[tok(i), :], WU[slot, :, here])
-                s = 0.5 * jnp.tanh(0.5 * g) + 0.5
-                ACT[tok(i), here] = (g * s * u).astype(BF16)
-            DA[tok(i), :] += dot(ACT[tok(i), :], WD[slot])
-
-        loop(blocks, some)
-
-    loop(tiles, forward_tile)
+        for j in range(2):
+            here = pl.ds(j * cols, cols)
+            g = dot(A[tok(i), :], WG[slot, :, here])
+            u = dot(A[tok(i), :], WU[slot, :, here])
+            s = 0.5 * jnp.tanh(0.5 * g) + 0.5
+            ACT[tok(i), here] = (g * s * u).astype(BF16)
+        DA[tok(i), :] += dot(ACT[tok(i), :], WD[slot])
 
     def second_norm(i):
         h = (H[tok(i), :].astype(F32) + DA[tok(i), :].astype(BF16).astype(F32)).astype(BF16)
@@ -133,10 +122,44 @@
         A[tok(i), :] = a
         AT[:, tok(i)] = a.T
         DA[tok(i), :] = jnp.zeros((tb, dim), F32)
-        dy_copy(i).wait()
-        DT[:, tok(i)] = D[tok(i), :].T
-
-    loop(blocks, second_norm)
+
+    x_copy(0).wait()
+    first_norm(0)
+    fetched(0)
+    fetch(1)
+
+    def opening(i):
+        x_copy(i + 1).wait()
+        forward(0, i)
+        first_norm(i + 1)
+
+    loop(blocks - 1, opening)
+
+    def middle(j):
+        q = blocks - 1 + j
+        k, i = q // blocks, lax.rem(q, blocks)
+
+        @pl.when(i == 0)
+        def _():
+            fetched(k)
+            fetch(k + 1)
+
+        @pl.when(j < blocks)
+        def _():
+            dy_copy(j).wait()
+
+        forward(k, i)
+        seen = jnp.minimum(j, blocks - 1)
+        DT[:, tok(seen)] = D[tok(seen), :].T
+
+    loop((tiles - 2) * blocks + 2, middle)
+
+    def closing(i):
+        forward(tiles - 1, i + 1)
+        second_norm(i)
+
+    loop(blocks - 1, closing)
+    second_norm(blocks - 1)
 
     pl.semaphore_wait(barrier, n - 1)
 
@@ -370,6 +393,14 @@
 
     loop(2 * tiles, tile_step)
 
+    ahead = (
+        pltpu.make_async_copy(wd_hbm.at[layers - 1, at(me, share), :], PW, ahead_sem.at[0]),
+        pltpu.make_async_copy(md_hbm.at[layers - 1], PM, ahead_sem.at[1]),
+        pltpu.make_async_copy(vd_hbm.at[layers - 1], PV, ahead_sem.at[2]),
+    )
+    for copy in ahead:
+        copy.start()
+
     end = 2 * tiles - 1
     u0, base = 3 * end, (end % 2) * 3
     later(u0 + 1, base + 1, 3)
@@ -383,14 +414,6 @@
     for j in range(1, dim // LANES):
         squares += SQ[:, j * LANES : (j + 1) * LANES]
     ALL[me] = squares
-
-    outs = (
-        pltpu.make_async_copy(OG, og_hbm, out_sem.at[0]),
-        pltpu.make_async_copy(OU, ou_hbm, out_sem.at[1]),
-        pltpu.make_async_copy(OD, od_hbm, out_sem.at[2]),
-    )
-    for copy in outs:
-        copy.start()
 
     def tell(d):
         return pltpu.make_async_remote_copy(
@@ -406,13 +429,11 @@
         tell(d).start()
     for d in range(1, n):
         tell(d).wait()
-    last = pltpu.make_async_copy(ALL, sq_hbm, out_sem.at[3])
-    last.start()
-    for copy in outs + (last,):
+    for copy in ahead:
         copy.wait()
 
 
-def gradients(n, x, dy, w_gate, w_up, w_down):
+def gradients(n, x, dy, w_gate, w_up, w_down, m_down, v_down):
     layers, dim, ff = w_gate.shape
     tokens = x.shape[1]
     blocks = 4
@@ -425,14 +446,20 @@
     any_space = pl.BlockSpec(memory_space=pl.ANY)
     return pl.pallas_call(
         functools.partial(grad_kernel, n, layers, (tokens, dim, ff, blocks)),
-        out_shape=(
-            jax.ShapeDtypeStruct((layers, dim // n, ff), BF16),
-            jax.ShapeDtypeStruct((layers, dim // n, ff), BF16),
-            jax.ShapeDtypeStruct((layers, share, dim), BF16),
-            jax.ShapeDtypeStruct((n, 8, LANES), F32),
+        out_shape=tuple(
+            kept(shape, dtype)
+            for shape, dtype in (
+                ((layers, dim // n, ff), BF16),
+                ((layers, dim // n, ff), BF16),
+                ((layers, share, dim), BF16),
+                ((n, 8, LANES), F32),
+                ((share, dim), BF16),
+                ((share, dim), F32),
+                ((share, dim), F32),
+            )
         ),
-        in_specs=[any_space] * 5,
-        out_specs=(any_space,) * 4,
+        in_specs=[any_space] * 7,
+        out_specs=(pl.BlockSpec(memory_space=pltpu.VMEM),) * 7,
         scratch_shapes=[
             pltpu.VMEM((tokens, dim), BF16),
             pltpu.VMEM((dim, tokens), BF16),
@@ -449,31 +476,27 @@
             pltpu.VMEM((6, n, LANES, dim), BF16),
             pltpu.VMEM((units, land, dim), BF16),
             pltpu.VMEM((units, land, dim), BF16),
-            pltpu.VMEM((layers, dim // n, ff), BF16),
-            pltpu.VMEM((layers, dim // n, ff), BF16),
-            pltpu.VMEM((layers, share, dim), BF16),
             pltpu.VMEM((8, dim), F32),
-            pltpu.VMEM((n, 8, LANES), F32),
             pltpu.SemaphoreType.DMA((blocks,)),
             pltpu.SemaphoreType.DMA((blocks,)),
             pltpu.SemaphoreType.DMA((2, 3)),
-            pltpu.SemaphoreType.DMA((4,)),
+            pltpu.SemaphoreType.DMA((3,)),
             pltpu.SemaphoreType.DMA((6, 2, half)),
             pltpu.SemaphoreType.DMA((units, 2, half)),
             pltpu.SemaphoreType.DMA((n,)),
             pltpu.SemaphoreType.DMA((n,)),
         ],
-        compiler_params=pltpu.CompilerParams(collective_id=0, has_side_effects=True, vmem_limit_bytes=VMEM_LIMIT),
+        compiler_params=pltpu.CompilerParams(collective_id=0, has_side_effects=True, vmem_limit_bytes=59 * 2**20),
         name="grads",
-    )(x, dy, w_gate, w_up, w_down)
+    )(*(pinned(t, pltpu.HBM) for t in (x, dy, w_gate, w_up, w_down, m_down, v_down)))
 
 
 def update_kernel(n, count, parts, *refs):
-    g_hbm, w_hbm, m_hbm, v_hbm = (refs[i : i + 3] for i in (0, 3, 6, 9))
-    sq_hbm = refs[12]
-    N, M, V = (refs[i : i + 3] for i in (13, 16, 19))
-    G, W = (refs[i : i + 3] for i in (22, 25))
-    SQ, in_sem, sq_sem, send_sem, recv_sem = refs[28:]
+    G, w_hbm, m_hbm, v_hbm = (refs[i : i + 3] for i in (0, 4, 10, 13))
+    SQ, PW, PM, PV = refs[3], *refs[7:10]
+    N, M, V = (refs[i : i + 3] for i in (16, 19, 22))
+    W = refs[25:28]
+    in_sem, send_sem, recv_sem = refs[28:]
     me = lax.axis_index("dp")
     half = n // 2
     up, down = lax.rem(me + 1, n), lax.rem(me + n - 1, n)
@@ -484,22 +507,18 @@
     for peer in (up, down):
         pl.semaphore_signal(barrier, inc=1, device_id={"dp": peer}, device_id_type=MESH)
 
-    squares = pltpu.make_async_copy(sq_hbm, SQ, sq_sem)
-    squares.start()
+    order = [(a, l) for l in reversed(range(layers)) for a in (2, 0, 1)]
     loads = {}
-    for l in reversed(range(layers)):
-        for a in (2, 0, 1):
-            rows = G[a].shape[1]
-            own = pl.ds(pl.multiple_of(me * rows, rows), rows)
-            loads[a, l] = (
-                pltpu.make_async_copy(g_hbm[a].at[l], G[a].at[l], in_sem.at[0, a, l]),
-                pltpu.make_async_copy(w_hbm[a].at[l, own, :], W[a].at[l], in_sem.at[1, a, l]),
-                pltpu.make_async_copy(m_hbm[a].at[l], M[a].at[l], in_sem.at[2, a, l]),
-                pltpu.make_async_copy(v_hbm[a].at[l], V[a].at[l], in_sem.at[3, a, l]),
-            )
-            for copy in loads[a, l]:
-                copy.start()
-    squares.wait()
+    for a, l in order[1:]:
+        rows = G[a].shape[1]
+        own = pl.ds(pl.multiple_of(me * rows, rows), rows)
+        loads[a, l] = (
+            pltpu.make_async_copy(w_hbm[a].at[l, own, :], W[a].at[l], in_sem.at[0, a, l]),
+            pltpu.make_async_copy(m_hbm[a].at[l], M[a].at[l], in_sem.at[1, a, l]),
+            pltpu.make_async_copy(v_hbm[a].at[l], V[a].at[l], in_sem.at[2, a, l]),
+        )
+        for copy in loads[a, l]:
+            copy.start()
     total = jnp.sum(jnp.sum(SQ[...], axis=0), axis=(0, 1), keepdims=True)
     factor = jnp.minimum(1.0, 0.5 * lax.rsqrt(total / count + 1e-30))
 
@@ -541,12 +560,13 @@
 
         def some(i):
             row = pl.ds(pl.multiple_of((p * r if split else 0) + i * step, step), step)
+            old = (PW[row, lane], PM[row, lane], PV[row, lane]) if (a, l) == order[0] else (W[a][l, row, lane], M[a][l, row, lane], V[a][l, row, lane])
             g = G[a][l, row, lane].astype(F32) * factor
-            m = 0.9 * M[a][l, row, lane] + 0.1 * g
-            v = 0.95 * V[a][l, row, lane] + 0.05 * g * g
+            m = 0.9 * old[1] + 0.1 * g
+            v = 0.95 * old[2] + 0.05 * g * g
             M[a][l, row, lane] = m
             V[a][l, row, lane] = v
-            w = W[a][l, row, lane].astype(F32)
+            w = old[0].astype(F32)
             new = (w - 0.02 * (m * lax.rsqrt(v + 1e-8) + 0.1 * w)).astype(BF16)
             there = pl.ds(pl.multiple_of(me * rows + (p * r if split else 0) + i * step, step), step)
             N[a][l, there, lane] = new
@@ -554,13 +574,12 @@
         loop(r // step, some)
 
     chunks = []
-    for l in reversed(range(layers)):
-        for a in (2, 0, 1):
-            for p in range(parts):
-                chunks.append((len(chunks), a, l, p))
+    for a, l in order:
+        for p in range(parts):
+            chunks.append((len(chunks), a, l, p))
     for i, a, l, p in chunks:
         if p == 0:
-            for copy in loads[a, l]:
+            for copy in loads.get((a, l), ()):
                 copy.wait()
         adam(a, l, p)
         if i == 0:
@@ -601,30 +620,34 @@
     )(*(pinned(t, pltpu.VMEM) for t in arrays))
 
 
-def update(n, g, w, m, v, squares):
+def update(n, made, w, m, v):
     layers = w[0].shape[0]
     parts = 2
     chunks = layers * 3 * parts
     count = sum(t.size for t in w)
-    shard = [t.shape for t in m]
     any_space = pl.BlockSpec(memory_space=pl.ANY)
+    in_vmem = pl.BlockSpec(memory_space=pltpu.VMEM)
     half = n // 2
+    g, squares, ahead = made[:3], made[3], made[4:]
     return pl.pallas_call(
         functools.partial(update_kernel, n, float(count), parts),
-        out_shape=tuple(kept(t, BF16) for t in w) + tuple(kept(t, F32) for t in m + v),
-        in_specs=[any_space] * 13,
-        out_specs=(pl.BlockSpec(memory_space=pltpu.VMEM),) * 9,
-        scratch_shapes=[pltpu.VMEM(s, BF16) for _ in range(2) for s in shard]
+        out_shape=tuple(kept(t.shape, BF16) for t in w) + tuple(kept(t.shape, F32) for t in m + v),
+        in_specs=[in_vmem] * 4 + [any_space] * 3 + [in_vmem] * 3 + [any_space] * 6,
+        out_specs=(in_vmem,) * 9,
+        scratch_shapes=[pltpu.VMEM(t.shape, BF16) for t in m]
         + [
-            pltpu.VMEM(squares.shape, F32),
-            pltpu.SemaphoreType.DMA((4, 3, layers)),
-            pltpu.SemaphoreType.DMA,
+            pltpu.SemaphoreType.DMA((3, 3, layers)),
             pltpu.SemaphoreType.DMA((chunks, 2, half)),
             pltpu.SemaphoreType.DMA((chunks, 2, half)),
         ],
         compiler_params=pltpu.CompilerParams(collective_id=1, has_side_effects=True, vmem_limit_bytes=12 * 2**20),
         name="update",
-    )(*(pinned(t, pltpu.HBM) for t in (*g, *w, *m, *v, squares)))
+    )(
+        *(pinned(t, pltpu.VMEM) for t in (*g, squares)),
+        *(pinned(t, pltpu.HBM) for t in w),
+        *(pinned(t, pltpu.VMEM) for t in ahead),
+        *(pinned(t, pltpu.HBM) for t in (*m, *v)),
+    )
 
 
 def solution(mesh):
@@ -632,8 +655,7 @@
 
     def step(x, dy, *arrays):
         w, m, v = (arrays[i : i + 3] for i in (0, 3, 6))
-        *g, squares = gradients(n, x, dy, *w)
-        return store(update(n, g, w, m, v, squares))
+        return store(update(n, gradients(n, x, dy, *w, m[2], v[2]), w, m, v))
 
     shard = P(None, "dp", None)
     return jax.shard_map(

time: 426 us -> 421 us (0.988)
  no operation moved by 1% of the time
where the time goes in v3:
time: 421 us
  Pallas kernels  421 us (100%)
    pallas_call x1, Pallas kernels, gradients(): pl.pallas_call(functools.partial(grad_kernel, n, layers, (tokens, dim, ff...  231 us
    pallas_call x1, Pallas kernels, update(): pl.pallas_call(functools.partial(update_kernel, n, float(count), parts),...  181 us
    pallas_call x1, Pallas kernels, store(): pl.pallas_call(functools.partial(store_kernel, count), out_shape=tuple((j...  9.45 us

profile of v3, /device:TPU:30, one launch (start us, length us, event | category | flops | bytes accessed | tf_op | source)
XLA Modules:
  0.0 421.4 jit_solution(15212561449266120408)
XLA Ops:
  0.6 230.6 %grads.1 = (bf16[2,64,3072]{2,1,0:T(8,128)(2,1)S(1)}, bf16[2,64,3072]{2,1,0:T(8,128)(2,1)S(1)}, bf16[2,384,512]{2,1,0:T(8,128)(2,1)S(1)}, f32[8,8,128]{2,1,0:T(8...) custom-call(bf16[1,2048,512]{2,1,0:T(8,128)(2,1)} %refs_0_.1, ...), custom_call_target="tpu_custom_call" | custom-call | tf_op jit(solution)/shard_map/grads/pallas_call | solution.py:447
  231.3 180.5 %update.1 = (bf16[2,512,3072]{2,1,0:T(8,128)(2,1)S(1)}, bf16[2,512,3072]{2,1,0:T(8,128)(2,1)S(1)}, bf16[2,3072,512]{2,1,0:T(8,128)(2,1)S(1)}, f32[2,64,3072]{2,1...) custom-call(bf16[2,64,3072]{2,1,0:T(8,128)(2,1)S(1)} %get-tuple-elem, ...), custom_call_target="tpu_custom_call" | custom-call | tf_op jit(solution)/shard_map/update/pallas_call | solution.py:632
  411.8 9.4 %store.1 = (bf16[2,512,3072]{2,1,0:T(8,128)(2,1)}, bf16[2,512,3072]{2,1,0:T(8,128)(2,1)}, bf16[2,3072,512]{2,1,0:T(8,128)(2,1)}, f32[2,64,3072]{2,1,0:T(8,128)},...) custom-call(bf16[2,512,3072]{2,1,0:T(8,128)(2,1)S(1)} %get-tuple-ele, ...), custom_call_target="tpu_custom_call" | custom-call | tf_op jit(solution)/shard_map/store/pallas_call | solution.py:612

commit v4 on v3

--- a/solution.py
+++ b/solution.py
@@ -116,12 +116,13 @@
 
     def second_norm(i):
         h = (H[tok(i), :].astype(F32) + DA[tok(i), :].astype(BF16).astype(F32)).astype(BF16)
+        wide = h.astype(F32)
+        return h, (wide * scale_of(wide)).astype(BF16)
+
+    def second_norm_kept(i, h, a):
         H[tok(i), :] = h
-        wide = h.astype(F32)
-        a = (wide * scale_of(wide)).astype(BF16)
         A[tok(i), :] = a
         AT[:, tok(i)] = a.T
-        DA[tok(i), :] = jnp.zeros((tb, dim), F32)
 
     x_copy(0).wait()
     first_norm(0)
@@ -155,11 +156,12 @@
     loop((tiles - 2) * blocks + 2, middle)
 
     def closing(i):
+        normed = second_norm(i)
         forward(tiles - 1, i + 1)
-        second_norm(i)
+        second_norm_kept(i, *normed)
 
     loop(blocks - 1, closing)
-    second_norm(blocks - 1)
+    second_norm_kept(blocks - 1, *second_norm(blocks - 1))
 
     pl.semaphore_wait(barrier, n - 1)
 
@@ -253,8 +255,8 @@
             return pl.when(going & cond)
 
         def hidden(j, i):
-            here = at(j, cols)
-            for b in range(2):
+            for b, c in ((0, 0), (0, 1), (1, 0), (1, 1)):
+                here = pl.ds(pl.multiple_of(j * cols + c * (cols // 2), cols // 2), cols // 2)
                 place = tok(2 * i + b)
                 g = dot(A[place, :], WG[slot, :, here])
                 u = dot(A[place, :], WU[slot, :, here])
@@ -360,7 +362,8 @@
         @pl.when(k < tiles)
         def _():
             def input_part(i):
-                DA[tok(i), :] += dot_t(DG[tok(i), :], WG[slot]) + dot_t(DU[tok(i), :], WU[slot])
+                so_far = jnp.where(k == 0, 0.0, DA[tok(i), :])
+                DA[tok(i), :] = so_far + (dot_t(DG[tok(i), :], WG[slot]) + dot_t(DU[tok(i), :], WU[slot]))
                 ring_part(i)
 
             loop(blocks, input_part)
@@ -385,10 +388,18 @@
                 A[tok(i), :] = a
                 AT[:, tok(i)] = a.T
 
+                @pl.when(i == 1)
+                def _():
+                    second_low(u0, base)
+                    second_high(u0, base)
+
             loop(blocks, between)
 
-        second_low(u0, base)
-        second_high(u0, base)
+        @pl.when(k != tiles - 1)
+        def _():
+            second_low(u0, base)
+            second_high(u0, base)
+
         later(u0 + 2, base + 2, 2)
 
     loop(2 * tiles, tile_step)
@@ -517,8 +528,6 @@
             pltpu.make_async_copy(m_hbm[a].at[l], M[a].at[l], in_sem.at[1, a, l]),
             pltpu.make_async_copy(v_hbm[a].at[l], V[a].at[l], in_sem.at[2, a, l]),
         )
-        for copy in loads[a, l]:
-            copy.start()
     total = jnp.sum(jnp.sum(SQ[...], axis=0), axis=(0, 1), keepdims=True)
     factor = jnp.minimum(1.0, 0.5 * lax.rsqrt(total / count + 1e-30))
 
@@ -555,7 +564,7 @@
     def adam(a, l, p):
         r, c, split = shape(a)
         rows = G[a].shape[1]
-        step = 16
+        step = 32
         lane = pl.ds(0 if split else p * c, c)
 
         def some(i):
@@ -586,6 +595,10 @@
             pl.semaphore_wait(barrier, 2)
         send(i, a, l, p, 0, 0).start()
         send(i, a, l, p, 1, 0).start()
+        if i == 0:
+            for copies in loads.values():
+                for copy in copies:
+                    copy.start()
     for step in range(half):
         for i, a, l, p in chunks:
             for way in range(2):
@@ -600,7 +613,11 @@
 
 def store_kernel(count, *refs):
     src, dst, sem = refs[:count], refs[count : 2 * count], refs[-1]
-    copies = [pltpu.make_async_copy(a, b, sem.at[i]) for i, (a, b) in enumerate(zip(src, dst, strict=True))]
+    copies = [
+        pltpu.make_async_copy(a.at[l], b.at[l], sem.at[i, l])
+        for i, (a, b) in enumerate(zip(src, dst, strict=True))
+        for l in range(a.shape[0])
+    ]
     for copy in copies:
         copy.start()
     for copy in copies:
@@ -614,7 +631,7 @@
         out_shape=tuple(jax.ShapeDtypeStruct(t.shape, t.dtype) for t in arrays),
         in_specs=[pl.BlockSpec(memory_space=pltpu.VMEM)] * count,
         out_specs=(pl.BlockSpec(memory_space=pl.ANY),) * count,
-        scratch_shapes=[pltpu.SemaphoreType.DMA((count,))],
+        scratch_shapes=[pltpu.SemaphoreType.DMA((count, arrays[0].shape[0]))],
         compiler_params=pltpu.CompilerParams(vmem_limit_bytes=2**20),
         name="store",
     )(*(pinned(t, pltpu.VMEM) for t in arrays))

time: 421 us -> 419 us (level)
  no operation moved by 1% of the time
where the time goes in v4:
time: 419 us
  Pallas kernels  418 us (100%)
    pallas_call x1, Pallas kernels, gradients(): pl.pallas_call(functools.partial(grad_kernel, n, layers, (tokens, dim, ff...  228 us
    pallas_call x1, Pallas kernels, update(): pl.pallas_call(functools.partial(update_kernel, n, float(count), parts),...  181 us
    pallas_call x1, Pallas kernels, store(): pl.pallas_call(functools.partial(store_kernel, count), out_shape=tuple((j...  9.5 us

profile of v4, /device:TPU:30, one launch (start us, length us, event | category | flops | bytes accessed | tf_op | source)
XLA Modules:
  0.0 419.0 jit_solution(5463482821882828408)
XLA Ops:
  0.6 227.6 %grads.1 = (bf16[2,64,3072]{2,1,0:T(8,128)(2,1)S(1)}, bf16[2,64,3072]{2,1,0:T(8,128)(2,1)S(1)}, bf16[2,384,512]{2,1,0:T(8,128)(2,1)S(1)}, f32[8,8,128]{2,1,0:T(8...) custom-call(bf16[1,2048,512]{2,1,0:T(8,128)(2,1)} %refs_0_.1, ...), custom_call_target="tpu_custom_call" | custom-call | tf_op jit(solution)/shard_map/grads/pallas_call | solution.py:458
  228.3 181.1 %update.1 = (bf16[2,512,3072]{2,1,0:T(8,128)(2,1)S(1)}, bf16[2,512,3072]{2,1,0:T(8,128)(2,1)S(1)}, bf16[2,3072,512]{2,1,0:T(8,128)(2,1)S(1)}, f32[2,64,3072]{2,1...) custom-call(bf16[2,64,3072]{2,1,0:T(8,128)(2,1)S(1)} %get-tuple-elem, ...), custom_call_target="tpu_custom_call" | custom-call | tf_op jit(solution)/shard_map/update/pallas_call | solution.py:649
  409.4 9.5 %store.1 = (bf16[2,512,3072]{2,1,0:T(8,128)(2,1)}, bf16[2,512,3072]{2,1,0:T(8,128)(2,1)}, bf16[2,3072,512]{2,1,0:T(8,128)(2,1)}, f32[2,64,3072]{2,1,0:T(8,128)},...) custom-call(bf16[2,512,3072]{2,1,0:T(8,128)(2,1)S(1)} %get-tuple-ele, ...), custom_call_target="tpu_custom_call" | custom-call | tf_op jit(solution)/shard_map/store/pallas_call | solution.py:629

commit v5 on v4

--- a/solution.py
+++ b/solution.py
@@ -11,7 +11,7 @@
 BF16 = jnp.bfloat16
 MESH = pl.DeviceIdType.MESH
 LANES = 128
-VMEM_LIMIT = 67043328
+LATE = 2
 
 
 def dot(a, b):
@@ -506,8 +506,9 @@
     G, w_hbm, m_hbm, v_hbm = (refs[i : i + 3] for i in (0, 4, 10, 13))
     SQ, PW, PM, PV = refs[3], *refs[7:10]
     N, M, V = (refs[i : i + 3] for i in (16, 19, 22))
-    W = refs[25:28]
-    in_sem, send_sem, recv_sem = refs[28:]
+    last = refs[25:27]
+    W = refs[27:30]
+    in_sem, last_sem, send_sem, recv_sem = refs[30:]
     me = lax.axis_index("dp")
     half = n // 2
     up, down = lax.rem(me + 1, n), lax.rem(me + n - 1, n)
@@ -599,16 +600,33 @@
             for copies in loads.values():
                 for copy in copies:
                     copy.start()
+    late = order[len(order) - LATE :]
+
+    def hops(a, l):
+        return half - 1 if (a, l) in late else half
+
+    def to_permute(a, l, way):
+        rows = G[a].shape[1]
+        owner = ring(1 - half) if way == 0 else ring(half - 1)
+        src = N[a].at[l, pl.ds(pl.multiple_of(owner * rows + way * (rows // 2), rows // 2), rows // 2), :]
+        return pltpu.make_async_copy(src, last[way].at[late.index((a, l))], last_sem.at[way, late.index((a, l))])
+
     for step in range(half):
         for i, a, l, p in chunks:
             for way in range(2):
-                came(i, a, l, p, way, step)
-                if step < half - 1:
+                if step < hops(a, l):
+                    came(i, a, l, p, way, step)
+                if step < hops(a, l) - 1:
                     send(i, a, l, p, way, step + 1).start()
+                elif step == half - 2 and p == parts - 1:
+                    to_permute(a, l, way).start()
     for i, a, l, p in chunks:
         for way in range(2):
-            for step in range(half):
+            for step in range(hops(a, l)):
                 send(i, a, l, p, way, step).wait_send()
+    for a, l in late:
+        for way in range(2):
+            to_permute(a, l, way).wait()
 
 
 def store_kernel(count, *refs):
@@ -633,8 +651,41 @@
         out_specs=(pl.BlockSpec(memory_space=pl.ANY),) * count,
         scratch_shapes=[pltpu.SemaphoreType.DMA((count, arrays[0].shape[0]))],
         compiler_params=pltpu.CompilerParams(vmem_limit_bytes=2**20),
+        cost_estimate=pl.CostEstimate(flops=10_000_000_000, bytes_accessed=0, transcendentals=0),
         name="store",
     )(*(pinned(t, pltpu.VMEM) for t in arrays))
+
+
+def place_kernel(n, count, *refs):
+    up_ref, down_ref = refs[count : count + 2]
+    outs, sem = refs[count + 2 : -1], refs[-1]
+    opposite = lax.rem(lax.axis_index("dp") + n // 2, n)
+    hr = up_ref.shape[1]
+    copies = []
+    for i, out in enumerate(outs):
+        for way, src in enumerate((up_ref, down_ref)):
+            there = pl.ds(pl.multiple_of(opposite * 2 * hr + way * hr, hr), hr)
+            copies.append(pltpu.make_async_copy(src.at[i], out.at[0, there, :], sem.at[i, way]))
+    for copy in copies:
+        copy.start()
+    for copy in copies:
+        copy.wait()
+
+
+def place_last(n, arrays, came):
+    count = len(arrays)
+    any_space = pl.BlockSpec(memory_space=pl.ANY)
+    in_vmem = pl.BlockSpec(memory_space=pltpu.VMEM)
+    return pl.pallas_call(
+        functools.partial(place_kernel, n, count),
+        out_shape=tuple(jax.ShapeDtypeStruct(t.shape, t.dtype) for t in arrays),
+        in_specs=[any_space] * count + [in_vmem] * 2,
+        out_specs=(any_space,) * count,
+        scratch_shapes=[pltpu.SemaphoreType.DMA((count, 2))],
+        input_output_aliases={i: i for i in range(count)},
+        compiler_params=pltpu.CompilerParams(vmem_limit_bytes=2**20),
+        name="place",
+    )(*(pinned(t, pltpu.HBM) for t in arrays), *came)
 
 
 def update(n, made, w, m, v):
@@ -648,12 +699,15 @@
     g, squares, ahead = made[:3], made[3], made[4:]
     return pl.pallas_call(
         functools.partial(update_kernel, n, float(count), parts),
-        out_shape=tuple(kept(t.shape, BF16) for t in w) + tuple(kept(t.shape, F32) for t in m + v),
+        out_shape=tuple(kept(t.shape, BF16) for t in w)
+        + tuple(kept(t.shape, F32) for t in m + v)
+        + (jax.ShapeDtypeStruct((LATE, m[0].shape[1] // 2, m[0].shape[2]), BF16),) * 2,
         in_specs=[in_vmem] * 4 + [any_space] * 3 + [in_vmem] * 3 + [any_space] * 6,
-        out_specs=(in_vmem,) * 9,
+        out_specs=(in_vmem,) * 9 + (any_space,) * 2,
         scratch_shapes=[pltpu.VMEM(t.shape, BF16) for t in m]
         + [
             pltpu.SemaphoreType.DMA((3, 3, layers)),
+            pltpu.SemaphoreType.DMA((2, LATE)),
             pltpu.SemaphoreType.DMA((chunks, 2, half)),
             pltpu.SemaphoreType.DMA((chunks, 2, half)),
         ],
@@ -672,7 +726,10 @@
 
     def step(x, dy, *arrays):
         w, m, v = (arrays[i : i + 3] for i in (0, 3, 6))
-        return store(update(n, gradients(n, x, dy, *w, m[2], v[2]), w, m, v))
+        *new, up, down = update(n, gradients(n, x, dy, *w, m[2], v[2]), w, m, v)
+        came = tuple(lax.ppermute(t, "dp", [(i, (i + d) % n) for i in range(n)]) for t, d in ((up, 1), (down, -1)))
+        out = store(new)
+        return (*place_last(n, out[:LATE], came), *out[LATE:])
 
     shard = P(None, "dp", None)
     return jax.shard_map(

time: 419 us -> 415 us (level)
  Pallas kernels: 418 us -> 411 us
    pallas_call x1, Pallas kernels: 181 us -> 173 us  [update(): pl.pallas_call(functools.partial(update_kernel, n, float(count), parts),...]
  transfers between devices with their start and end apart: 0 -> 2, of which waited for: 0 -> 0; matrix products, arithmetic and copies ran while one was open for 0% -> 0% of each run, Pallas kernels for 0% -> 2%
where the time goes in v5:
time: 415 us
  Pallas kernels  411 us (99%)
    pallas_call x1, Pallas kernels, gradients(): pl.pallas_call(functools.partial(grad_kernel, n, layers, (tokens, dim, ff...  228 us
    pallas_call x1, Pallas kernels, update(): pl.pallas_call(functools.partial(update_kernel, n, float(count), parts),...  173 us
    pallas_call x1, Pallas kernels, store(): pl.pallas_call(functools.partial(store_kernel, count), out_shape=tuple((j...  9.49 us
  transfers between devices with their start and end apart: 2, of which 0 were waited for; matrix products, arithmetic and copies ran while one was open for 0% of the time, Pallas kernels for 2%

profile of v5, /device:TPU:30, one launch (start us, length us, event | category | flops | bytes accessed | tf_op | source)
XLA Modules:
  0.0 414.9 jit_solution(3087796793667246192)
XLA Ops:
  0.6 227.6 %grads.1 = (bf16[2,64,3072]{2,1,0:T(8,128)(2,1)S(1)}, bf16[2,64,3072]{2,1,0:T(8,128)(2,1)S(1)}, bf16[2,384,512]{2,1,0:T(8,128)(2,1)S(1)}, f32[8,8,128]{2,1,0:T(8...) custom-call(bf16[1,2048,512]{2,1,0:T(8,128)(2,1)} %refs_0_.1, ...), custom_call_target="tpu_custom_call" | custom-call | tf_op jit(solution)/shard_map/grads/pallas_call | solution.py:458
  228.3 172.7 %update.1 = (bf16[2,512,3072]{2,1,0:T(8,128)(2,1)S(1)}, bf16[2,512,3072]{2,1,0:T(8,128)(2,1)S(1)}, bf16[2,3072,512]{2,1,0:T(8,128)(2,1)S(1)}, f32[2,64,3072]{2,1...) custom-call(bf16[2,64,3072]{2,1,0:T(8,128)(2,1)S(1)} %get-tuple-elem, ...), custom_call_target="tpu_custom_call" | custom-call | tf_op jit(solution)/shard_map/update/pallas_call | solution.py:700
  401.0 0.5 collective-permute-start
  401.4 2.9 collective-permute-start.1
  404.3 9.5 %store.1 = (bf16[2,512,3072]{2,1,0:T(8,128)(2,1)}, bf16[2,512,3072]{2,1,0:T(8,128)(2,1)}, bf16[2,3072,512]{2,1,0:T(8,128)(2,1)}, f32[2,64,3072]{2,1,0:T(8,128)},...) custom-call(bf16[2,512,3072]{2,1,0:T(8,128)(2,1)S(1)} %get-tuple-ele, ...), custom_call_target="tpu_custom_call" | custom-call | flops 10000000000 | tf_op jit(solution)/shard_map/store/pallas_call | solution.py:647
  413.8 0.0 collective-permute-done.refs_2_
  413.8 0.0 collective-permute-done.1.refs_3_
  413.8 0.9 place.1
Async XLA Ops:
  401.0 12.8 %collective-permute-start = (bf16[2,32,3072]{2,1,0:T(8,128)(2,1)S(1)}, bf16[2,32,3072]{2,1,0:T(8,128)(2,1)S(1)}, u32[]{:S(2)}, u32[]{:S(2)}) collective-permute-start(bf16[2,32,3072]{2,1,0:T(8,128)(2,1)S(1)} %get-tuple-element.56), channel_id=1, source_target_pairs={{0,1},{1,2},{2,3},{3,4},{4,5},{5,6},{6,7},{7,0},{8,9},{9,10},{10,1... | collective-permute-start | bytes 1179656 | tf_op jit(solution)/shard_map/ppermute | solution.py:730
  401.4 12.4 %collective-permute-start.1 = (bf16[2,32,3072]{2,1,0:T(8,128)(2,1)S(1)}, bf16[2,32,3072]{2,1,0:T(8,128)(2,1)S(1)}, u32[]{:S(2)}, u32[]{:S(2)}) collective-permute-start(bf16[2,32,3072]{2,1,0:T(8,128)(2,1)S(1)} %get-tuple-element.57), channel_id=1, source_target_pairs={{0,7},{1,0},{2,1},{3,2},{4,3},{5,4},{6,5},{7,6},{8,15},{9,8},{10,9... | collective-permute-start | bytes 1179656 | tf_op jit(solution)/shard_map/ppermute | solution.py:730

commit v6 on v5

--- a/solution.py
+++ b/solution.py
@@ -46,7 +46,7 @@
     (x_hbm, dy_hbm, wg_hbm, wu_hbm, wd_hbm, md_hbm, vd_hbm) = refs[:7]
     (OG, OU, OD, ALL, PW, PM, PV) = refs[7:14]
     (A, AT, D, DT, H, ACT, DG, DU, DA, WG, WU, WD, G, RU, RD, SQ, *sems) = refs[14:]
-    x_sem, dy_sem, w_sem, ahead_sem, send_sem, recv_sem, sq_send, sq_recv = sems
+    x_sem, dy_sem, w_sem, ahead_sem, send_sem, recv_sem, low_sem, sq_send, sq_recv = sems
     tokens, dim, ff, blocks = shapes
     share = ff // n
     tiles = share // LANES
@@ -95,8 +95,9 @@
     for d in range(1, n):
         pl.semaphore_signal(barrier, inc=1, device_id={"dp": ring(d)}, device_id_type=MESH)
 
-    loop(blocks, lambda i: x_copy(i).start())
+    x_copy(0).start()
     fetch(0)
+    loop(blocks - 1, lambda i: x_copy(i + 1).start())
     loop(blocks, lambda i: dy_copy(i).start())
 
     def first_norm(i):
@@ -165,12 +166,12 @@
 
     pl.semaphore_wait(barrier, n - 1)
 
-    def remote(src, dst, slot, u, way, step):
+    def remote(src, dst, slot, u, way, step, arrival=None):
         return pltpu.make_async_remote_copy(
             src_ref=src,
             dst_ref=dst,
             send_sem=send_sem.at[slot, way, step],
-            recv_sem=recv_sem.at[u, way, step],
+            recv_sem=recv_sem.at[u, way, step] if arrival is None else arrival,
             device_id={"dp": (up, down)[way]},
             device_id_type=MESH,
         )
@@ -179,19 +180,25 @@
     lands = (RU, RD)
 
     def rows(step):
-        return pl.ds(pl.multiple_of(hr + (step - 1) * 2 * hr, hr), 2 * hr)
+        return pl.ds(hr + (step - 1) * 2 * hr, 2 * hr)
 
     def begin_low(u, slot):
         remote(G.at[slot, ring(half), low], RU.at[u, low], slot, u, 0, 0).start()
-        remote(G.at[slot, ring(1 - half), low], RD.at[u, pl.ds(hr, hr)], slot, u, 1, 1).start()
+        remote(G.at[slot, ring(1 - half), low], RD.at[u, pl.ds(hr, hr)], slot, u, 1, 1, low_sem.at[u]).start()
 
     def begin_high(u, slot):
         remote(G.at[slot, ring(half), high], RD.at[u, low], slot, u, 1, 0).start()
         remote(G.at[slot, ring(half - 1), high], RU.at[u, pl.ds(2 * hr, hr)], slot, u, 0, 1).start()
 
+    def arrived(land, sem):
+        pltpu.make_async_copy(land, land, sem).wait()
+
     def received(u, way, step):
-        dst = lands[way].at[u, low] if isinstance(step, int) and step == 0 else lands[way].at[u, rows(step)]
-        pltpu.make_async_copy(dst, dst, recv_sem.at[u, way, step]).wait()
+        if (way, step) == (1, 1):
+            arrived(RD.at[u, pl.ds(hr, hr)], low_sem.at[u])
+            arrived(RD.at[u, pl.ds(2 * hr, hr)], recv_sem.at[u, 1, 1])
+        else:
+            arrived(lands[way].at[u, rows(step) if step else low], recv_sem.at[u, way, step])
 
     def add(land, place, mine):
         land[place] = (land[place].astype(F32) + mine.astype(F32)).astype(BF16)
@@ -206,13 +213,27 @@
         add(RD, (u, low), G[slot, ring(1 - half), high])
         remote(RD.at[u, low], RD.at[u, pl.ds(2 * hr, hr)], slot, u, 1, 1).start()
 
+    def pass_on(u, slot, way, step):
+        received(u, way, step - 1)
+        add(lands[way], (u, rows(step - 1)), G[slot, ring(half - step if way == 0 else step - half)])
+        remote(lands[way].at[u, rows(step - 1)], lands[way].at[u, rows(step)], slot, u, way, step).start()
+
     def later(u, slot, step):
-        received(u, 0, step - 1)
-        received(u, 1, step - 1)
-        add(RU, (u, rows(step - 1)), G[slot, ring(half - step)])
-        add(RD, (u, rows(step - 1)), G[slot, ring(step - half)])
-        remote(RU.at[u, rows(step - 1)], RU.at[u, rows(step)], slot, u, 0, step).start()
-        remote(RD.at[u, rows(step - 1)], RD.at[u, rows(step)], slot, u, 1, step).start()
+        pass_on(u, slot, 0, step)
+        pass_on(u, slot, 1, step)
+
+    def half_on(u, slot, part, sem):
+        here, there = pl.ds((1 + part) * hr, hr), pl.ds((3 + part) * hr, hr)
+        arrived(RD.at[u, here], sem)
+        add(RD, (u, here), G[slot, ring(2 - half), (low, high)[part]])
+        remote(RD.at[u, here], RD.at[u, there], slot, u, 1, 2).start()
+
+    def third_low(u, slot):
+        half_on(u, slot, 0, low_sem.at[u])
+
+    def third_rest(u, slot):
+        pass_on(u, slot, 0, 2)
+        half_on(u, slot, 1, recv_sem.at[u, 1, 1])
 
     def finish(u, slot, which, layer, t):
         received(u, 0, half - 1)
@@ -271,56 +292,61 @@
             part = dot(AT[...], src[:, at(j, cols)]).astype(BF16)
             G[base + unit, :, at(j, hr), :] = part.reshape(n, dim // n, cols)
 
+        gate, upper = (u0 + 1, base + 1), (u0 + 2, base + 2)
+        old, old_gate, old_upper = (p0, prev), (p0 + 1, prev + 1), (p0 + 2, prev + 2)
+
         def halves(j):
             def some(i):
                 hidden(j, i)
 
                 @when((j == 0) & (i == 0))
                 def _():
-                    later(p0 + 1, prev + 1, 3)
+                    later(*old, 2)
+                    later(*old_upper, 3)
+
+                @pl.when((k == 0) & (j == 1) & (i == 0))
+                def _():
+                    third_low(*gate)
+
+                @pl.when((k == 0) & (j == 1) & (i == 1))
+                def _():
+                    second_low(*upper)
 
             loop(blocks // 2, some)
+            wide_part(DG, 1, j)
+
+            @pl.when(j == 0)
+            def _():
+                begin_low(*gate)
+
+            @pl.when(j == 1)
+            def _():
+                begin_high(*gate)
+
+            @pl.when((j == 1) & (k == 0))
+            def _():
+                second_low(*gate)
+
+            wide_part(DU, 2, j)
+
+            @pl.when(j == 0)
+            def _():
+                begin_low(*upper)
+
+            @pl.when(j == 1)
+            def _():
+                begin_high(*upper)
 
             @when(j == 1)
             def _():
-                finish(p0 + 1, prev + 1, 1, old_layer, old_t)
-
-            wide_part(DG, 1, j)
-
-            @pl.when(j == 0)
-            def _():
-                begin_low(u0 + 1, base + 1)
-
-            @when(j == 0)
-            def _():
-                later(p0, prev, 2)
-
-            @pl.when(j == 1)
-            def _():
-                begin_high(u0 + 1, base + 1)
-
-            @when(j == 1)
-            def _():
-                later(p0, prev, 3)
-
-            @pl.when(j == 1)
-            def _():
-                second_low(u0 + 1, base + 1)
-
-            wide_part(DU, 2, j)
-
-            @pl.when(j == 0)
-            def _():
-                begin_low(u0 + 2, base + 2)
-
-            @when(j == 0)
-            def _():
-                later(p0 + 2, prev + 2, 3)
-
-            @pl.when(j == 1)
-            def _():
-                begin_high(u0 + 2, base + 2)
-                second_low(u0 + 2, base + 2)
+                later(*old, 3)
+                finish(*old_gate, 1, old_layer, old_t)
+                finish(*old_upper, 2, old_layer, old_t)
+                second_low(*gate)
+
+            @pl.when((j == 1) & (k == 0))
+            def _():
+                third_low(*upper)
 
         loop(2, halves)
 
@@ -332,32 +358,34 @@
 
             @pl.when(j == 0)
             def _():
-                second_high(u0 + 1, base + 1)
-
-            @when(j == 0)
-            def _():
-                finish(p0 + 2, prev + 2, 2, old_layer, old_t)
+                second_high(*gate)
 
         loop(2, down_part)
         begin_low(u0, base)
         begin_high(u0, base)
 
+        @pl.when(going)
+        def _():
+            second_low(*upper)
+
         @pl.when(k == tiles - 1)
         def _():
             loop(blocks, lambda i: x_again(i).start())
 
         def ring_part(i):
-            @pl.when(i == 1)
-            def _():
-                second_high(u0 + 2, base + 2)
-
-            @when(i == 1)
-            def _():
-                finish(p0, prev, 0, old_layer, old_t)
-
-            @pl.when(i == 2)
-            def _():
-                later(u0 + 1, base + 1, 2)
+            @pl.when(i == 0)
+            def _():
+                second_high(*upper)
+
+            @pl.when((i == 0) & (k == 0))
+            def _():
+                second_low(u0, base)
+                third_rest(*gate)
+
+            @when(i == 2)
+            def _():
+                finish(*old, 0, old_layer, old_t)
+                later(*gate, 2)
 
         @pl.when(k < tiles)
         def _():
@@ -395,12 +423,23 @@
 
             loop(blocks, between)
 
+        @pl.when(going & (k != tiles - 1))
+        def _():
+            second_low(u0, base)
+
         @pl.when(k != tiles - 1)
         def _():
-            second_low(u0, base)
             second_high(u0, base)
 
-        later(u0 + 2, base + 2, 2)
+        @pl.when(k == 0)
+        def _():
+            third_rest(*upper)
+
+        @pl.when(going)
+        def _():
+            later(*upper, 2)
+
+        later(*gate, 3)
 
     loop(2 * tiles, tile_step)
 
@@ -414,7 +453,6 @@
 
     end = 2 * tiles - 1
     u0, base = 3 * end, (end % 2) * 3
-    later(u0 + 1, base + 1, 3)
     later(u0, base, 2)
     later(u0 + 2, base + 2, 3)
     later(u0, base, 3)
@@ -494,6 +532,7 @@
             pltpu.SemaphoreType.DMA((3,)),
             pltpu.SemaphoreType.DMA((6, 2, half)),
             pltpu.SemaphoreType.DMA((units, 2, half)),
+            pltpu.SemaphoreType.DMA((units,)),
             pltpu.SemaphoreType.DMA((n,)),
             pltpu.SemaphoreType.DMA((n,)),
         ],

time: 415 us -> 413 us (level)
    pallas_call x1, Pallas kernels: 173 us -> 167 us  [update(): pl.pallas_call(functools.partial(update_kernel, n, float(count), parts),...]
where the time goes in v6:
time: 413 us
  Pallas kernels  409 us (99%)
    pallas_call x1, Pallas kernels, gradients(): pl.pallas_call(functools.partial(grad_kernel, n, layers, (tokens, dim, ff...  231 us
    pallas_call x1, Pallas kernels, update(): pl.pallas_call(functools.partial(update_kernel, n, float(count), parts),...  167 us
    pallas_call x1, Pallas kernels, store(): pl.pallas_call(functools.partial(store_kernel, count), out_shape=tuple((j...  9.49 us
  transfers between devices with their start and end apart: 2, of which 0 were waited for; matrix products, arithmetic and copies ran while one was open for 0% of the time, Pallas kernels for 2%

profile of v6, /device:TPU:30, one launch (start us, length us, event | category | flops | bytes accessed | tf_op | source)
XLA Modules:
  0.0 412.7 jit_solution(18063537255898755927)
XLA Ops:
  0.6 231.0 %grads.1 = (bf16[2,64,3072]{2,1,0:T(8,128)(2,1)S(1)}, bf16[2,64,3072]{2,1,0:T(8,128)(2,1)S(1)}, bf16[2,384,512]{2,1,0:T(8,128)(2,1)S(1)}, f32[8,8,128]{2,1,0:T(8...) custom-call(bf16[1,2048,512]{2,1,0:T(8,128)(2,1)} %refs_0_.1, ...), custom_call_target="tpu_custom_call" | custom-call | tf_op jit(solution)/shard_map/grads/pallas_call | solution.py:496
  231.6 167.2 %update.1 = (bf16[2,512,3072]{2,1,0:T(8,128)(2,1)S(1)}, bf16[2,512,3072]{2,1,0:T(8,128)(2,1)S(1)}, bf16[2,3072,512]{2,1,0:T(8,128)(2,1)S(1)}, f32[2,64,3072]{2,1...) custom-call(bf16[2,64,3072]{2,1,0:T(8,128)(2,1)S(1)} %get-tuple-elem, ...), custom_call_target="tpu_custom_call" | custom-call | tf_op jit(solution)/shard_map/update/pallas_call | solution.py:739
  398.8 1.3 collective-permute-start
  400.1 2.1 collective-permute-start.1
  402.1 9.5 %store.1 = (bf16[2,512,3072]{2,1,0:T(8,128)(2,1)}, bf16[2,512,3072]{2,1,0:T(8,128)(2,1)}, bf16[2,3072,512]{2,1,0:T(8,128)(2,1)}, f32[2,64,3072]{2,1,0:T(8,128)},...) custom-call(bf16[2,512,3072]{2,1,0:T(8,128)(2,1)S(1)} %get-tuple-ele, ...), custom_call_target="tpu_custom_call" | custom-call | flops 10000000000 | tf_op jit(solution)/shard_map/store/pallas_call | solution.py:686
  411.6 0.0 collective-permute-done.refs_2_
  411.6 0.0 collective-permute-done.1.refs_3_
  411.7 0.9 place.1
Async XLA Ops:
  398.8 12.8 %collective-permute-start = (bf16[2,32,3072]{2,1,0:T(8,128)(2,1)S(1)}, bf16[2,32,3072]{2,1,0:T(8,128)(2,1)S(1)}, u32[]{:S(2)}, u32[]{:S(2)}) collective-permute-start(bf16[2,32,3072]{2,1,0:T(8,128)(2,1)S(1)} %get-tuple-element.56), channel_id=1, source_target_pairs={{0,1},{1,2},{2,3},{3,4},{4,5},{5,6},{6,7},{7,0},{8,9},{9,10},{10,1... | collective-permute-start | bytes 1179656 | tf_op jit(solution)/shard_map/ppermute | solution.py:769
  400.1 11.6 %collective-permute-start.1 = (bf16[2,32,3072]{2,1,0:T(8,128)(2,1)S(1)}, bf16[2,32,3072]{2,1,0:T(8,128)(2,1)S(1)}, u32[]{:S(2)}, u32[]{:S(2)}) collective-permute-start(bf16[2,32,3072]{2,1,0:T(8,128)(2,1)S(1)} %get-tuple-element.57), channel_id=1, source_target_pairs={{0,7},{1,0},{2,1},{3,2},{4,3},{5,4},{6,5},{7,6},{8,15},{9,8},{10,9... | collective-permute-start | bytes 1179656 | tf_op jit(solution)/shard_map/ppermute | solution.py:769

commit v7 on v6

--- a/solution.py
+++ b/solution.py
@@ -11,7 +11,7 @@
 BF16 = jnp.bfloat16
 MESH = pl.DeviceIdType.MESH
 LANES = 128
-LATE = 2
+LATE = 4
 
 
 def dot(a, b):
@@ -541,6 +541,10 @@
     )(*(pinned(t, pltpu.HBM) for t in (x, dy, w_gate, w_up, w_down, m_down, v_down)))
 
 
+def turns(layers):
+    return [(2, l) for l in reversed(range(layers))] + [(a, l) for l in reversed(range(layers)) for a in (0, 1)]
+
+
 def update_kernel(n, count, parts, *refs):
     G, w_hbm, m_hbm, v_hbm = (refs[i : i + 3] for i in (0, 4, 10, 13))
     SQ, PW, PM, PV = refs[3], *refs[7:10]
@@ -558,7 +562,7 @@
     for peer in (up, down):
         pl.semaphore_signal(barrier, inc=1, device_id={"dp": peer}, device_id_type=MESH)
 
-    order = [(a, l) for l in reversed(range(layers)) for a in (2, 0, 1)]
+    order = turns(layers)
     loads = {}
     for a, l in order[1:]:
         rows = G[a].shape[1]
@@ -701,10 +705,10 @@
     opposite = lax.rem(lax.axis_index("dp") + n // 2, n)
     hr = up_ref.shape[1]
     copies = []
-    for i, out in enumerate(outs):
+    for i, (a, l) in enumerate(turns(outs[0].shape[0])[-LATE:]):
         for way, src in enumerate((up_ref, down_ref)):
             there = pl.ds(pl.multiple_of(opposite * 2 * hr + way * hr, hr), hr)
-            copies.append(pltpu.make_async_copy(src.at[i], out.at[0, there, :], sem.at[i, way]))
+            copies.append(pltpu.make_async_copy(src.at[i], outs[a].at[l, there, :], sem.at[i, way]))
     for copy in copies:
         copy.start()
     for copy in copies:
@@ -720,7 +724,7 @@
         out_shape=tuple(jax.ShapeDtypeStruct(t.shape, t.dtype) for t in arrays),
         in_specs=[any_space] * count + [in_vmem] * 2,
         out_specs=(any_space,) * count,
-        scratch_shapes=[pltpu.SemaphoreType.DMA((count, 2))],
+        scratch_shapes=[pltpu.SemaphoreType.DMA((LATE, 2))],
         input_output_aliases={i: i for i in range(count)},
         compiler_params=pltpu.CompilerParams(vmem_limit_bytes=2**20),
         name="place",
@@ -768,7 +772,7 @@
         *new, up, down = update(n, gradients(n, x, dy, *w, m[2], v[2]), w, m, v)
         came = tuple(lax.ppermute(t, "dp", [(i, (i + d) % n) for i in range(n)]) for t, d in ((up, 1), (down, -1)))
         out = store(new)
-        return (*place_last(n, out[:LATE], came), *out[LATE:])
+        return (*place_last(n, out[:2], came), *out[2:])
 
     shard = P(None, "dp", None)
     return jax.shard_map(

time: 413 us -> 408 us (0.988)
  Pallas kernels: 409 us -> 402 us
    pallas_call x1, Pallas kernels: 167 us -> 160 us  [update(): pl.pallas_call(functools.partial(update_kernel, n, float(count), parts),...]
  transfers between devices with their start and end apart: 2 -> 2, of which waited for: 0 -> 2; matrix products, arithmetic and copies ran while one was open for 0% -> 0% of each run, Pallas kernels for 2% -> 2%
where the time goes in v7:
time: 408 us; the launch traced here: 407 us
  Pallas kernels  402 us (99%)
    pallas_call x1, Pallas kernels, gradients(): pl.pallas_call(functools.partial(grad_kernel, n, layers, (tokens, dim, ff...  231 us
    pallas_call x1, Pallas kernels, update(): pl.pallas_call(functools.partial(update_kernel, n, float(count), parts),...  160 us
    pallas_call x1, Pallas kernels, store(): pl.pallas_call(functools.partial(store_kernel, count), out_shape=tuple((j...  9.49 us
  transfers between devices with their start and end apart: 2, of which 2 were waited for; matrix products, arithmetic and copies ran while one was open for 0% of the time, Pallas kernels for 2%

profile of v7, /device:TPU:30, one launch (start us, length us, event | category | flops | bytes accessed | tf_op | source)
XLA Modules:
  0.0 406.7 jit_solution(15321171332331023267)
XLA Ops:
  0.6 231.0 %grads.1 = (bf16[2,64,3072]{2,1,0:T(8,128)(2,1)S(1)}, bf16[2,64,3072]{2,1,0:T(8,128)(2,1)S(1)}, bf16[2,384,512]{2,1,0:T(8,128)(2,1)S(1)}, f32[8,8,128]{2,1,0:T(8...) custom-call(bf16[1,2048,512]{2,1,0:T(8,128)(2,1)} %refs_0_.1, ...), custom_call_target="tpu_custom_call" | custom-call | tf_op jit(solution)/shard_map/grads/pallas_call | solution.py:496
  231.6 160.1 %update.1 = (bf16[2,512,3072]{2,1,0:T(8,128)(2,1)S(1)}, bf16[2,512,3072]{2,1,0:T(8,128)(2,1)S(1)}, bf16[2,3072,512]{2,1,0:T(8,128)(2,1)S(1)}, f32[2,64,3072]{2,1...) custom-call(bf16[2,64,3072]{2,1,0:T(8,128)(2,1)S(1)} %get-tuple-elem, ...), custom_call_target="tpu_custom_call" | custom-call | tf_op jit(solution)/shard_map/update/pallas_call | solution.py:743
  391.7 1.7 collective-permute-start
  393.4 1.6 collective-permute-start.1
  395.0 9.5 %store.1 = (bf16[2,512,3072]{2,1,0:T(8,128)(2,1)}, bf16[2,512,3072]{2,1,0:T(8,128)(2,1)}, bf16[2,3072,512]{2,1,0:T(8,128)(2,1)}, f32[2,64,3072]{2,1,0:T(8,128)},...) custom-call(bf16[2,512,3072]{2,1,0:T(8,128)(2,1)S(1)} %get-tuple-ele, ...), custom_call_target="tpu_custom_call" | custom-call | flops 10000000000 | tf_op jit(solution)/shard_map/store/pallas_call | solution.py:690
  404.5 0.5 collective-permute-done.refs_2_
  405.0 0.4 collective-permute-done.1.refs_3_
  405.4 1.2 place.1
Async XLA Ops:
  391.7 13.3 %collective-permute-start = (bf16[4,32,3072]{2,1,0:T(8,128)(2,1)S(1)}, bf16[4,32,3072]{2,1,0:T(8,128)(2,1)S(1)}, u32[]{:S(2)}, u32[]{:S(2)}) collective-permute-start(bf16[4,32,3072]{2,1,0:T(8,128)(2,1)S(1)} %get-tuple-element.56), channel_id=1, source_target_pairs={{0,1},{1,2},{2,3},{3,4},{4,5},{5,6},{6,7},{7,0},{8,9},{9,10},{10,1... | collective-permute-start | bytes 2359304 | tf_op jit(solution)/shard_map/ppermute | solution.py:773
  393.4 12.0 %collective-permute-start.1 = (bf16[4,32,3072]{2,1,0:T(8,128)(2,1)S(1)}, bf16[4,32,3072]{2,1,0:T(8,128)(2,1)S(1)}, u32[]{:S(2)}, u32[]{:S(2)}) collective-permute-start(bf16[4,32,3072]{2,1,0:T(8,128)(2,1)S(1)} %get-tuple-element.57), channel_id=1, source_target_pairs={{0,7},{1,0},{2,1},{3,2},{4,3},{5,4},{6,5},{7,6},{8,15},{9,8},{10,9... | collective-permute-start | bytes 2359304 | tf_op jit(solution)/shard_map/ppermute | solution.py:773

commit v8 on v7

--- a/solution.py
+++ b/solution.py
@@ -105,15 +105,15 @@
         A[tok(i), :] = (wide * scale_of(wide)).astype(BF16)
         DA[tok(i), :] = jnp.zeros((tb, dim), F32)
 
-    def forward(k, i):
+    def forward(k, i, act=ACT):
         slot = lax.rem(k, 2)
-        for j in range(2):
-            here = pl.ds(j * cols, cols)
+        for j in range(4):
+            here = pl.ds(j * (tile // 4), tile // 4)
             g = dot(A[tok(i), :], WG[slot, :, here])
             u = dot(A[tok(i), :], WU[slot, :, here])
             s = 0.5 * jnp.tanh(0.5 * g) + 0.5
-            ACT[tok(i), here] = (g * s * u).astype(BF16)
-        DA[tok(i), :] += dot(ACT[tok(i), :], WD[slot])
+            act[tok(i), here] = (g * s * u).astype(BF16)
+        DA[tok(i), :] += dot(act[tok(i), :], WD[slot])
 
     def second_norm(i):
         h = (H[tok(i), :].astype(F32) + DA[tok(i), :].astype(BF16).astype(F32)).astype(BF16)
@@ -138,23 +138,30 @@
     loop(blocks - 1, opening)
 
     def middle(j):
-        q = blocks - 1 + j
-        k, i = q // blocks, lax.rem(q, blocks)
-
-        @pl.when(i == 0)
-        def _():
-            fetched(k)
-            fetch(k + 1)
-
-        @pl.when(j < blocks)
-        def _():
-            dy_copy(j).wait()
-
-        forward(k, i)
-        seen = jnp.minimum(j, blocks - 1)
-        DT[:, tok(seen)] = D[tok(seen), :].T
-
-    loop((tiles - 2) * blocks + 2, middle)
+        q = blocks - 1 + 2 * j
+
+        @pl.when(lax.rem(q + 1, blocks) == 0)
+        def _():
+            fetched((q + 1) // blocks)
+
+        @pl.when((lax.rem(q, blocks) == 1) & (q // blocks < tiles - 1))
+        def _():
+            fetch(q // blocks + 1)
+
+        seen = [jnp.minimum(2 * j + d, blocks - 1) for d in range(2)]
+
+        @pl.when(2 * j < blocks)
+        def _():
+            dy_copy(2 * j).wait()
+            dy_copy(2 * j + 1).wait()
+
+        forward(q // blocks, lax.rem(q, blocks))
+        forward((q + 1) // blocks, lax.rem(q + 1, blocks), DG)
+        for i in seen:
+            DT[:, tok(i)] = D[tok(i), :].T
+
+    loop((tiles - 2) * blocks // 2 + 1, middle)
+    fetch(tiles)
 
     def closing(i):
         normed = second_norm(i)
@@ -276,9 +283,9 @@
             return pl.when(going & cond)
 
         def hidden(j, i):
-            for b, c in ((0, 0), (0, 1), (1, 0), (1, 1)):
+            place = pl.ds(pl.multiple_of(i * 2 * tb, 2 * tb), 2 * tb)
+            for c in range(2):
                 here = pl.ds(pl.multiple_of(j * cols + c * (cols // 2), cols // 2), cols // 2)
-                place = tok(2 * i + b)
                 g = dot(A[place, :], WG[slot, :, here])
                 u = dot(A[place, :], WU[slot, :, here])
                 back = dot_t(D[place, :], WD[slot, here, :]).astype(BF16).astype(F32)

time: 408 us -> 406 us (level)
  no operation moved by 1% of the time
where the time goes in v8:
time: 406 us; the launch traced here: 405 us
  Pallas kernels  400 us (99%)
    pallas_call x1, Pallas kernels, gradients(): pl.pallas_call(functools.partial(grad_kernel, n, layers, (tokens, dim, ff...  229 us
    pallas_call x1, Pallas kernels, update(): pl.pallas_call(functools.partial(update_kernel, n, float(count), parts),...  160 us
    pallas_call x1, Pallas kernels, store(): pl.pallas_call(functools.partial(store_kernel, count), out_shape=tuple((j...  9.49 us
  transfers between devices with their start and end apart: 2, of which 2 were waited for; matrix products, arithmetic and copies ran while one was open for 0% of the time, Pallas kernels for 2%

profile of v8, /device:TPU:30, one launch (start us, length us, event | category | flops | bytes accessed | tf_op | source)
XLA Modules:
  0.0 405.2 jit_solution(5298112864733414524)
XLA Ops:
  0.6 229.0 %grads.1 = (bf16[2,64,3072]{2,1,0:T(8,128)(2,1)S(1)}, bf16[2,64,3072]{2,1,0:T(8,128)(2,1)S(1)}, bf16[2,384,512]{2,1,0:T(8,128)(2,1)S(1)}, f32[8,8,128]{2,1,0:T(8...) custom-call(bf16[1,2048,512]{2,1,0:T(8,128)(2,1)} %refs_0_.1, ...), custom_call_target="tpu_custom_call" | custom-call | tf_op jit(solution)/shard_map/grads/pallas_call | solution.py:503
  229.7 160.3 %update.1 = (bf16[2,512,3072]{2,1,0:T(8,128)(2,1)S(1)}, bf16[2,512,3072]{2,1,0:T(8,128)(2,1)S(1)}, bf16[2,3072,512]{2,1,0:T(8,128)(2,1)S(1)}, f32[2,64,3072]{2,1...) custom-call(bf16[2,64,3072]{2,1,0:T(8,128)(2,1)S(1)} %get-tuple-elem, ...), custom_call_target="tpu_custom_call" | custom-call | tf_op jit(solution)/shard_map/update/pallas_call | solution.py:750
  390.0 1.9 collective-permute-start
  391.8 1.5 collective-permute-start.1
  393.3 9.5 %store.1 = (bf16[2,512,3072]{2,1,0:T(8,128)(2,1)}, bf16[2,512,3072]{2,1,0:T(8,128)(2,1)}, bf16[2,3072,512]{2,1,0:T(8,128)(2,1)}, f32[2,64,3072]{2,1,0:T(8,128)},...) custom-call(bf16[2,512,3072]{2,1,0:T(8,128)(2,1)S(1)} %get-tuple-ele, ...), custom_call_target="tpu_custom_call" | custom-call | flops 10000000000 | tf_op jit(solution)/shard_map/store/pallas_call | solution.py:697
  402.8 0.5 collective-permute-done.refs_2_
  403.2 0.6 collective-permute-done.1.refs_3_
  403.8 1.2 place.1
Async XLA Ops:
  390.0 13.3 %collective-permute-start = (bf16[4,32,3072]{2,1,0:T(8,128)(2,1)S(1)}, bf16[4,32,3072]{2,1,0:T(8,128)(2,1)S(1)}, u32[]{:S(2)}, u32[]{:S(2)}) collective-permute-start(bf16[4,32,3072]{2,1,0:T(8,128)(2,1)S(1)} %get-tuple-element.56), channel_id=1, source_target_pairs={{0,1},{1,2},{2,3},{3,4},{4,5},{5,6},{6,7},{7,0},{8,9},{9,10},{10,1... | collective-permute-start | bytes 2359304 | tf_op jit(solution)/shard_map/ppermute | solution.py:780
  391.8 12.0 %collective-permute-start.1 = (bf16[4,32,3072]{2,1,0:T(8,128)(2,1)S(1)}, bf16[4,32,3072]{2,1,0:T(8,128)(2,1)S(1)}, u32[]{:S(2)}, u32[]{:S(2)}) collective-permute-start(bf16[4,32,3072]{2,1,0:T(8,128)(2,1)S(1)} %get-tuple-element.57), channel_id=1, source_target_pairs={{0,7},{1,0},{2,1},{3,2},{4,3},{5,4},{6,5},{7,6},{8,15},{9,8},{10,9... | collective-permute-start | bytes 2359304 | tf_op jit(solution)/shard_map/ppermute | solution.py:780

commit v9 on v8

--- a/solution.py
+++ b/solution.py
@@ -263,6 +263,8 @@
 
     SQ[...] = jnp.zeros_like(SQ)
 
+    end = 2 * tiles - 1
+
     def tile_step(k):
         wk = k + tiles
         slot = lax.rem(wk, 2)
@@ -368,10 +370,13 @@
                 second_high(*gate)
 
         loop(2, down_part)
-        begin_low(u0, base)
-        begin_high(u0, base)
-
-        @pl.when(going)
+
+        @pl.when(k < end)
+        def _():
+            begin_low(u0, base)
+            begin_high(u0, base)
+
+        @when(k < end)
         def _():
             second_low(*upper)
 
@@ -403,7 +408,7 @@
 
             loop(blocks, input_part)
 
-        @pl.when(k >= tiles)
+        @pl.when((k >= tiles) & (k < end))
         def _():
             loop(blocks, ring_part)
 
@@ -430,11 +435,11 @@
 
             loop(blocks, between)
 
-        @pl.when(going & (k != tiles - 1))
+        @when((k != tiles - 1) & (k < end))
         def _():
             second_low(u0, base)
 
-        @pl.when(k != tiles - 1)
+        @pl.when((k != tiles - 1) & (k < end))
         def _():
             second_high(u0, base)
 
@@ -442,11 +447,13 @@
         def _():
             third_rest(*upper)
 
-        @pl.when(going)
+        @when(k < end)
         def _():
             later(*upper, 2)
 
-        later(*gate, 3)
+        @pl.when(k < end)
+        def _():
+            later(*gate, 3)
 
     loop(2 * tiles, tile_step)
 
@@ -458,13 +465,21 @@
     for copy in ahead:
         copy.start()
 
-    end = 2 * tiles - 1
-    u0, base = 3 * end, (end % 2) * 3
-    later(u0, base, 2)
-    later(u0 + 2, base + 2, 3)
-    later(u0, base, 3)
-    for j in (1, 2, 0):
-        finish(u0 + j, base + j, j, 0, tiles - 1)
+    base = (end % 2) * 3
+    down_unit, gate, upper = ((3 * end + j, base + j) for j in range(3))
+    begin_high(*down_unit)
+    second_high(*upper)
+    begin_low(*down_unit)
+    second_low(*upper)
+    second_high(*down_unit)
+    second_low(*down_unit)
+    for step in range(2, half):
+        for unit in (gate, upper, down_unit):
+            later(*unit, step)
+    finish(*gate, 1, 0, tiles - 1)
+    finish(3 * (end - 1), 3 - base, 0, 0, tiles - 2)
+    finish(*upper, 2, 0, tiles - 1)
+    finish(*down_unit, 0, 0, tiles - 1)
 
     squares = SQ[:, :LANES]
     for j in range(1, dim // LANES):

time: 406 us -> 405 us (level)
  no operation moved by 1% of the time
where the time goes in v9:
time: 405 us; the launch traced here: 404 us
  Pallas kernels  399 us (99%)
    pallas_call x1, Pallas kernels, gradients(): pl.pallas_call(functools.partial(grad_kernel, n, layers, (tokens, dim, ff...  228 us
    pallas_call x1, Pallas kernels, update(): pl.pallas_call(functools.partial(update_kernel, n, float(count), parts),...  161 us
    pallas_call x1, Pallas kernels, store(): pl.pallas_call(functools.partial(store_kernel, count), out_shape=tuple((j...  9.49 us
  transfers between devices with their start and end apart: 2, of which 2 were waited for; matrix products, arithmetic and copies ran while one was open for 0% of the time, Pallas kernels for 2%

profile of v9, /device:TPU:30, one launch (start us, length us, event | category | flops | bytes accessed | tf_op | source)
XLA Modules:
  0.0 404.4 jit_solution(4979985880223402349)
XLA Ops:
  0.6 227.8 %grads.1 = (bf16[2,64,3072]{2,1,0:T(8,128)(2,1)S(1)}, bf16[2,64,3072]{2,1,0:T(8,128)(2,1)S(1)}, bf16[2,384,512]{2,1,0:T(8,128)(2,1)S(1)}, f32[8,8,128]{2,1,0:T(8...) custom-call(bf16[1,2048,512]{2,1,0:T(8,128)(2,1)} %refs_0_.1, ...), custom_call_target="tpu_custom_call" | custom-call | tf_op jit(solution)/shard_map/grads/pallas_call | solution.py:518
  228.4 161.0 %update.1 = (bf16[2,512,3072]{2,1,0:T(8,128)(2,1)S(1)}, bf16[2,512,3072]{2,1,0:T(8,128)(2,1)S(1)}, bf16[2,3072,512]{2,1,0:T(8,128)(2,1)S(1)}, f32[2,64,3072]{2,1...) custom-call(bf16[2,64,3072]{2,1,0:T(8,128)(2,1)S(1)} %get-tuple-elem, ...), custom_call_target="tpu_custom_call" | custom-call | tf_op jit(solution)/shard_map/update/pallas_call | solution.py:765
  389.4 1.7 collective-permute-start
  391.1 1.7 collective-permute-start.1
  392.8 9.5 %store.1 = (bf16[2,512,3072]{2,1,0:T(8,128)(2,1)}, bf16[2,512,3072]{2,1,0:T(8,128)(2,1)}, bf16[2,3072,512]{2,1,0:T(8,128)(2,1)}, f32[2,64,3072]{2,1,0:T(8,128)},...) custom-call(bf16[2,512,3072]{2,1,0:T(8,128)(2,1)S(1)} %get-tuple-ele, ...), custom_call_target="tpu_custom_call" | custom-call | flops 10000000000 | tf_op jit(solution)/shard_map/store/pallas_call | solution.py:712
  402.3 0.5 collective-permute-done.refs_2_
  402.7 0.4 collective-permute-done.1.refs_3_
  403.1 1.2 place.1
Async XLA Ops:
  389.4 13.3 %collective-permute-start = (bf16[4,32,3072]{2,1,0:T(8,128)(2,1)S(1)}, bf16[4,32,3072]{2,1,0:T(8,128)(2,1)S(1)}, u32[]{:S(2)}, u32[]{:S(2)}) collective-permute-start(bf16[4,32,3072]{2,1,0:T(8,128)(2,1)S(1)} %get-tuple-element.56), channel_id=1, source_target_pairs={{0,1},{1,2},{2,3},{3,4},{4,5},{5,6},{6,7},{7,0},{8,9},{9,10},{10,1... | collective-permute-start | bytes 2359304 | tf_op jit(solution)/shard_map/ppermute | solution.py:795
  391.1 12.0 %collective-permute-start.1 = (bf16[4,32,3072]{2,1,0:T(8,128)(2,1)S(1)}, bf16[4,32,3072]{2,1,0:T(8,128)(2,1)S(1)}, u32[]{:S(2)}, u32[]{:S(2)}) collective-permute-start(bf16[4,32,3072]{2,1,0:T(8,128)(2,1)S(1)} %get-tuple-element.57), channel_id=1, source_target_pairs={{0,7},{1,0},{2,1},{3,2},{4,3},{5,4},{6,5},{7,6},{8,15},{9,8},{10,9... | collective-permute-start | bytes 2359304 | tf_op jit(solution)/shard_map/ppermute | solution.py:795

commit v10 on v9

--- a/solution.py
+++ b/solution.py
@@ -91,14 +91,12 @@
     def dy_copy(i):
         return pltpu.make_async_copy(dy_hbm.at[0, tok(i), :], D.at[tok(i), :], dy_sem.at[i])
 
+    x_copy(0).start()
+    fetch(0)
+    x_copy(1).start()
     barrier = pltpu.get_barrier_semaphore()
     for d in range(1, n):
         pl.semaphore_signal(barrier, inc=1, device_id={"dp": ring(d)}, device_id_type=MESH)
-
-    x_copy(0).start()
-    fetch(0)
-    loop(blocks - 1, lambda i: x_copy(i + 1).start())
-    loop(blocks, lambda i: dy_copy(i).start())
 
     def first_norm(i):
         wide = H[tok(i), :].astype(F32)
@@ -128,7 +126,9 @@
     x_copy(0).wait()
     first_norm(0)
     fetched(0)
+    loop(blocks - 2, lambda i: x_copy(i + 2).start())
     fetch(1)
+    loop(blocks, lambda i: dy_copy(i).start())
 
     def opening(i):
         x_copy(i + 1).wait()
@@ -169,7 +169,25 @@
         second_norm_kept(i, *normed)
 
     loop(blocks - 1, closing)
-    second_norm_kept(blocks - 1, *second_norm(blocks - 1))
+
+    def hidden(slot, j, i, pieces=1):
+        size = 2 * tb // pieces
+        for p, c in [(p, c) for p in range(pieces) for c in range(2)]:
+            place = at(i * pieces + p, size)
+            here = at(2 * j + c, cols // 2)
+            g = dot(A[place, :], WG[slot, :, here])
+            u = dot(A[place, :], WU[slot, :, here])
+            back = dot_t(D[place, :], WD[slot, here, :]).astype(BF16).astype(F32)
+            s = 0.5 * jnp.tanh(0.5 * g) + 0.5
+            silu = g * s
+            ACT[place, here] = (silu * u).astype(BF16)
+            DU[place, here] = (back * silu).astype(BF16)
+            DG[place, here] = (back * u * (s + silu * (1.0 - s))).astype(BF16)
+
+    fetched(tiles)
+    normed = second_norm(blocks - 1)
+    hidden(tiles % 2, 0, 0, 2)
+    second_norm_kept(blocks - 1, *normed)
 
     pl.semaphore_wait(barrier, n - 1)
 
@@ -275,7 +293,10 @@
         going = k >= 1
         old_t = lax.rem(k - 1 + tiles, tiles)
         old_layer = jnp.where(k - 1 < tiles, 1, 0)
-        fetched(wk)
+
+        @pl.when(k > 0)
+        def _():
+            fetched(wk)
 
         @pl.when(k < 2 * tiles - 1)
         def _():
@@ -283,19 +304,6 @@
 
         def when(cond):
             return pl.when(going & cond)
-
-        def hidden(j, i):
-            place = pl.ds(pl.multiple_of(i * 2 * tb, 2 * tb), 2 * tb)
-            for c in range(2):
-                here = pl.ds(pl.multiple_of(j * cols + c * (cols // 2), cols // 2), cols // 2)
-                g = dot(A[place, :], WG[slot, :, here])
-                u = dot(A[place, :], WU[slot, :, here])
-                back = dot_t(D[place, :], WD[slot, here, :]).astype(BF16).astype(F32)
-                s = 0.5 * jnp.tanh(0.5 * g) + 0.5
-                silu = g * s
-                ACT[place, here] = (silu * u).astype(BF16)
-                DU[place, here] = (back * silu).astype(BF16)
-                DG[place, here] = (back * u * (s + silu * (1.0 - s))).astype(BF16)
 
         def wide_part(src, unit, j):
             part = dot(AT[...], src[:, at(j, cols)]).astype(BF16)
@@ -306,7 +314,9 @@
 
         def halves(j):
             def some(i):
-                hidden(j, i)
+                @pl.when((k > 0) | (j > 0) | (i > 0))
+                def _():
+                    hidden(slot, j, i)
 
                 @when((j == 0) & (i == 0))
                 def _():
@@ -558,7 +568,7 @@
             pltpu.SemaphoreType.DMA((n,)),
             pltpu.SemaphoreType.DMA((n,)),
         ],
-        compiler_params=pltpu.CompilerParams(collective_id=0, has_side_effects=True, vmem_limit_bytes=59 * 2**20),
+        compiler_params=pltpu.CompilerParams(collective_id=0, has_side_effects=True, vmem_limit_bytes=62_500_000),
         name="grads",
     )(*(pinned(t, pltpu.HBM) for t in (x, dy, w_gate, w_up, w_down, m_down, v_down)))
 

time: 405 us -> 404 us (level)
  no operation moved by 1% of the time
where the time goes in v10:
time: 404 us
  Pallas kernels  399 us (99%)
    pallas_call x1, Pallas kernels, gradients(): pl.pallas_call(functools.partial(grad_kernel, n, layers, (tokens, dim, ff...  227 us
    pallas_call x1, Pallas kernels, update(): pl.pallas_call(functools.partial(update_kernel, n, float(count), parts),...  161 us
    pallas_call x1, Pallas kernels, store(): pl.pallas_call(functools.partial(store_kernel, count), out_shape=tuple((j...  9.49 us
  transfers between devices with their start and end apart: 2, of which 2 were waited for; matrix products, arithmetic and copies ran while one was open for 0% of the time, Pallas kernels for 2%

profile of v10, /device:TPU:30, one launch (start us, length us, event | category | flops | bytes accessed | tf_op | source)
XLA Modules:
  0.0 404.1 jit_solution(787689666559154750)
XLA Ops:
  0.6 227.5 %grads.1 = (bf16[2,64,3072]{2,1,0:T(8,128)(2,1)S(1)}, bf16[2,64,3072]{2,1,0:T(8,128)(2,1)S(1)}, bf16[2,384,512]{2,1,0:T(8,128)(2,1)S(1)}, f32[8,8,128]{2,1,0:T(8...) custom-call(bf16[1,2048,512]{2,1,0:T(8,128)(2,1)} %refs_0_.1, ...), custom_call_target="tpu_custom_call" | custom-call | tf_op jit(solution)/shard_map/grads/pallas_call | solution.py:528
  228.1 161.0 %update.1 = (bf16[2,512,3072]{2,1,0:T(8,128)(2,1)S(1)}, bf16[2,512,3072]{2,1,0:T(8,128)(2,1)S(1)}, bf16[2,3072,512]{2,1,0:T(8,128)(2,1)S(1)}, f32[2,64,3072]{2,1...) custom-call(bf16[2,64,3072]{2,1,0:T(8,128)(2,1)S(1)} %get-tuple-elem, ...), custom_call_target="tpu_custom_call" | custom-call | tf_op jit(solution)/shard_map/update/pallas_call | solution.py:775
  389.1 1.7 collective-permute-start
  390.8 1.7 collective-permute-start.1
  392.5 9.5 %store.1 = (bf16[2,512,3072]{2,1,0:T(8,128)(2,1)}, bf16[2,512,3072]{2,1,0:T(8,128)(2,1)}, bf16[2,3072,512]{2,1,0:T(8,128)(2,1)}, f32[2,64,3072]{2,1,0:T(8,128)},...) custom-call(bf16[2,512,3072]{2,1,0:T(8,128)(2,1)S(1)} %get-tuple-ele, ...), custom_call_target="tpu_custom_call" | custom-call | flops 10000000000 | tf_op jit(solution)/shard_map/store/pallas_call | solution.py:722
  402.0 0.5 collective-permute-done.refs_2_
  402.4 0.4 collective-permute-done.1.refs_3_
  402.8 1.2 place.1
Async XLA Ops:
  389.1 13.3 %collective-permute-start = (bf16[4,32,3072]{2,1,0:T(8,128)(2,1)S(1)}, bf16[4,32,3072]{2,1,0:T(8,128)(2,1)S(1)}, u32[]{:S(2)}, u32[]{:S(2)}) collective-permute-start(bf16[4,32,3072]{2,1,0:T(8,128)(2,1)S(1)} %get-tuple-element.56), channel_id=1, source_target_pairs={{0,1},{1,2},{2,3},{3,4},{4,5},{5,6},{6,7},{7,0},{8,9},{9,10},{10,1... | collective-permute-start | bytes 2359304 | tf_op jit(solution)/shard_map/ppermute | solution.py:805
  390.8 12.0 %collective-permute-start.1 = (bf16[4,32,3072]{2,1,0:T(8,128)(2,1)S(1)}, bf16[4,32,3072]{2,1,0:T(8,128)(2,1)S(1)}, u32[]{:S(2)}, u32[]{:S(2)}) collective-permute-start(bf16[4,32,3072]{2,1,0:T(8,128)(2,1)S(1)} %get-tuple-element.57), channel_id=1, source_target_pairs={{0,7},{1,0},{2,1},{3,2},{4,3},{5,4},{6,5},{7,6},{8,15},{9,8},{10,9... | collective-permute-start | bytes 2359304 | tf_op jit(solution)/shard_map/ppermute | solution.py:805

commit v11 on v10

--- a/solution.py
+++ b/solution.py
@@ -12,6 +12,11 @@
 MESH = pl.DeviceIdType.MESH
 LANES = 128
 LATE = 4
+TAIL = (
+    ("H0d", "H1u", "L0d", "S2g0h", "L1u", "S2g1l", "F0d", "S2g0l", "S2g1h", "H1d", "L1d", "S2u0h", "S2d0h", "S2u1l", "S2d1l", "S2u1h", "S2u0l")
+    + ("S3g0h", "S3g1l", "S2d1h", "S2d0l", "S3g1h", "S3g0l", "S3d1l", "S3d0h", "S3u0l", "S3u1h", "S3u0h", "S3u1l", "S3d1h", "S3d0l")
+    + ("F1u", "F1g", "F1d")
+)
 
 
 def dot(a, b):
@@ -46,7 +51,7 @@
     (x_hbm, dy_hbm, wg_hbm, wu_hbm, wd_hbm, md_hbm, vd_hbm) = refs[:7]
     (OG, OU, OD, ALL, PW, PM, PV) = refs[7:14]
     (A, AT, D, DT, H, ACT, DG, DU, DA, WG, WU, WD, G, RU, RD, SQ, *sems) = refs[14:]
-    x_sem, dy_sem, w_sem, ahead_sem, send_sem, recv_sem, low_sem, sq_send, sq_recv = sems
+    x_sem, dy_sem, w_sem, ahead_sem, send_sem, recv_sem, low_sem, high_sem, tail_sem, sq_send, sq_recv = sems
     tokens, dim, ff, blocks = shapes
     share = ff // n
     tiles = share // LANES
@@ -213,15 +218,18 @@
 
     def begin_high(u, slot):
         remote(G.at[slot, ring(half), high], RD.at[u, low], slot, u, 1, 0).start()
-        remote(G.at[slot, ring(half - 1), high], RU.at[u, pl.ds(2 * hr, hr)], slot, u, 0, 1).start()
+        remote(G.at[slot, ring(half - 1), high], RU.at[u, pl.ds(2 * hr, hr)], slot, u, 0, 1, high_sem.at[u]).start()
 
     def arrived(land, sem):
         pltpu.make_async_copy(land, land, sem).wait()
 
+    def first_arrival(u, way, part):
+        return (low_sem, high_sem)[part].at[u] if part != way else recv_sem.at[u, way, 1]
+
     def received(u, way, step):
-        if (way, step) == (1, 1):
-            arrived(RD.at[u, pl.ds(hr, hr)], low_sem.at[u])
-            arrived(RD.at[u, pl.ds(2 * hr, hr)], recv_sem.at[u, 1, 1])
+        if step == 1:
+            for part in range(2):
+                arrived(lands[way].at[u, pl.ds((1 + part) * hr, hr)], first_arrival(u, way, part))
         else:
             arrived(lands[way].at[u, rows(step) if step else low], recv_sem.at[u, way, step])
 
@@ -247,22 +255,26 @@
         pass_on(u, slot, 0, step)
         pass_on(u, slot, 1, step)
 
-    def half_on(u, slot, part, sem):
-        here, there = pl.ds((1 + part) * hr, hr), pl.ds((3 + part) * hr, hr)
-        arrived(RD.at[u, here], sem)
-        add(RD, (u, here), G[slot, ring(2 - half), (low, high)[part]])
-        remote(RD.at[u, here], RD.at[u, there], slot, u, 1, 2).start()
+    def half_on(u, slot, way, step, part, sem, arrival=None):
+        here, there = (pl.ds((2 * step - d + part) * hr, hr) for d in (3, 1))
+        arrived(lands[way].at[u, here], sem)
+        add(lands[way], (u, here), G[slot, ring(half - step if way == 0 else step - half), (low, high)[part]])
+        remote(lands[way].at[u, here], lands[way].at[u, there], slot, u, way, step, arrival).start()
 
     def third_low(u, slot):
-        half_on(u, slot, 0, low_sem.at[u])
+        half_on(u, slot, 1, 2, 0, first_arrival(u, 1, 0))
 
     def third_rest(u, slot):
         pass_on(u, slot, 0, 2)
-        half_on(u, slot, 1, recv_sem.at[u, 1, 1])
-
-    def finish(u, slot, which, layer, t):
-        received(u, 0, half - 1)
-        received(u, 1, half - 1)
+        half_on(u, slot, 1, 2, 1, first_arrival(u, 1, 1))
+
+    def finish(u, slot, which, layer, t, halves=None):
+        for way in range(2):
+            if halves is None:
+                received(u, way, half - 1)
+            else:
+                for part in range(2):
+                    arrived(lands[way].at[u, pl.ds((2 * half - 3 + part) * hr, hr)], halves.at[way, half - 1, part])
         total = G[slot, me].astype(F32) + RU[u, rows(half - 1)].astype(F32) + RD[u, rows(half - 1)].astype(F32)
         total = total.astype(BF16)
         wide = total.astype(F32)
@@ -476,20 +488,27 @@
         copy.start()
 
     base = (end % 2) * 3
-    down_unit, gate, upper = ((3 * end + j, base + j) for j in range(3))
-    begin_high(*down_unit)
-    second_high(*upper)
-    begin_low(*down_unit)
-    second_low(*upper)
-    second_high(*down_unit)
-    second_low(*down_unit)
-    for step in range(2, half):
-        for unit in (gate, upper, down_unit):
-            later(*unit, step)
-    finish(*gate, 1, 0, tiles - 1)
-    finish(3 * (end - 1), 3 - base, 0, 0, tiles - 2)
-    finish(*upper, 2, 0, tiles - 1)
-    finish(*down_unit, 0, 0, tiles - 1)
+    last = {x: (3 * end + j, base + j) for j, x in enumerate("dgu")}
+    for name in TAIL:
+        kind, x = name[:2], name[2]
+        j = "dgu".index(x)
+        sems = tail_sem.at[j]
+        if kind == "L0":
+            begin_low(*last[x])
+        elif kind == "H0":
+            begin_high(*last[x])
+        elif kind == "L1":
+            second_low(*last[x])
+        elif kind == "H1":
+            second_high(*last[x])
+        elif kind == "F0":
+            finish(3 * (end - 1) + j, 3 - base + j, j, 0, tiles - 2)
+        elif kind == "F1":
+            finish(*last[x], j, 0, tiles - 1, sems)
+        else:
+            step, way, part = int(kind[1]), int(name[3]), "lh".index(name[4])
+            sem = first_arrival(last[x][0], way, part) if step == 2 else sems.at[way, step - 1, part]
+            half_on(*last[x], way, step, part, sem, sems.at[way, step, part])
 
     squares = SQ[:, :LANES]
     for j in range(1, dim // LANES):
@@ -565,6 +584,8 @@
             pltpu.SemaphoreType.DMA((6, 2, half)),
             pltpu.SemaphoreType.DMA((units, 2, half)),
             pltpu.SemaphoreType.DMA((units,)),
+            pltpu.SemaphoreType.DMA((units,)),
+            pltpu.SemaphoreType.DMA((3, 2, half, 2)),
             pltpu.SemaphoreType.DMA((n,)),
             pltpu.SemaphoreType.DMA((n,)),
         ],

time: 404 us -> 405 us (level)
  no operation moved by 1% of the time
where the time goes in v11:
time: 405 us; the launch traced here: 404 us
  Pallas kernels  400 us (99%)
    pallas_call x1, Pallas kernels, gradients(): pl.pallas_call(functools.partial(grad_kernel, n, layers, (tokens, dim, ff...  228 us
    pallas_call x1, Pallas kernels, update(): pl.pallas_call(functools.partial(update_kernel, n, float(count), parts),...  161 us
    pallas_call x1, Pallas kernels, store(): pl.pallas_call(functools.partial(store_kernel, count), out_shape=tuple((j...  9.49 us
  transfers between devices with their start and end apart: 2, of which 2 were waited for; matrix products, arithmetic and copies ran while one was open for 0% of the time, Pallas kernels for 2%

profile of v11, /device:TPU:30, one launch (start us, length us, event | category | flops | bytes accessed | tf_op | source)
XLA Modules:
  0.0 404.5 jit_solution(11259547034417650415)
XLA Ops:
  0.6 228.1 %grads.1 = (bf16[2,64,3072]{2,1,0:T(8,128)(2,1)S(1)}, bf16[2,64,3072]{2,1,0:T(8,128)(2,1)S(1)}, bf16[2,384,512]{2,1,0:T(8,128)(2,1)S(1)}, f32[8,8,128]{2,1,0:T(8...) custom-call(bf16[1,2048,512]{2,1,0:T(8,128)(2,1)} %refs_0_.1, ...), custom_call_target="tpu_custom_call" | custom-call | tf_op jit(solution)/shard_map/grads/pallas_call | solution.py:547
  228.8 160.9 %update.1 = (bf16[2,512,3072]{2,1,0:T(8,128)(2,1)S(1)}, bf16[2,512,3072]{2,1,0:T(8,128)(2,1)S(1)}, bf16[2,3072,512]{2,1,0:T(8,128)(2,1)S(1)}, f32[2,64,3072]{2,1...) custom-call(bf16[2,64,3072]{2,1,0:T(8,128)(2,1)S(1)} %get-tuple-elem, ...), custom_call_target="tpu_custom_call" | custom-call | tf_op jit(solution)/shard_map/update/pallas_call | solution.py:796
  389.7 1.4 collective-permute-start
  391.1 1.9 collective-permute-start.1
  393.0 9.5 %store.1 = (bf16[2,512,3072]{2,1,0:T(8,128)(2,1)}, bf16[2,512,3072]{2,1,0:T(8,128)(2,1)}, bf16[2,3072,512]{2,1,0:T(8,128)(2,1)}, f32[2,64,3072]{2,1,0:T(8,128)},...) custom-call(bf16[2,512,3072]{2,1,0:T(8,128)(2,1)S(1)} %get-tuple-ele, ...), custom_call_target="tpu_custom_call" | custom-call | flops 10000000000 | tf_op jit(solution)/shard_map/store/pallas_call | solution.py:743
  402.5 0.5 collective-permute-done.refs_2_
  403.0 0.1 collective-permute-done.1.refs_3_
  403.1 1.2 place.1
Async XLA Ops:
  389.7 13.3 %collective-permute-start = (bf16[4,32,3072]{2,1,0:T(8,128)(2,1)S(1)}, bf16[4,32,3072]{2,1,0:T(8,128)(2,1)S(1)}, u32[]{:S(2)}, u32[]{:S(2)}) collective-permute-start(bf16[4,32,3072]{2,1,0:T(8,128)(2,1)S(1)} %get-tuple-element.56), channel_id=1, source_target_pairs={{0,1},{1,2},{2,3},{3,4},{4,5},{5,6},{6,7},{7,0},{8,9},{9,10},{10,1... | collective-permute-start | bytes 2359304 | tf_op jit(solution)/shard_map/ppermute | solution.py:826
  391.1 12.0 %collective-permute-start.1 = (bf16[4,32,3072]{2,1,0:T(8,128)(2,1)S(1)}, bf16[4,32,3072]{2,1,0:T(8,128)(2,1)S(1)}, u32[]{:S(2)}, u32[]{:S(2)}) collective-permute-start(bf16[4,32,3072]{2,1,0:T(8,128)(2,1)S(1)} %get-tuple-element.57), channel_id=1, source_target_pairs={{0,7},{1,0},{2,1},{3,2},{4,3},{5,4},{6,5},{7,6},{8,15},{9,8},{10,9... | collective-permute-start | bytes 2359304 | tf_op jit(solution)/shard_map/ppermute | solution.py:826

commit v12 on v10

--- a/solution.py
+++ b/solution.py
@@ -312,6 +312,8 @@
         gate, upper = (u0 + 1, base + 1), (u0 + 2, base + 2)
         old, old_gate, old_upper = (p0, prev), (p0 + 1, prev + 1), (p0 + 2, prev + 2)
 
+        held = (k == 0) & (lax.rem(lax.axis_index("rep"), 2) == 0)
+
         def halves(j):
             def some(i):
                 @pl.when((k > 0) | (j > 0) | (i > 0))
@@ -334,7 +336,7 @@
             loop(blocks // 2, some)
             wide_part(DG, 1, j)
 
-            @pl.when(j == 0)
+            @pl.when((j == 0) & jnp.logical_not(held))
             def _():
                 begin_low(*gate)
 
@@ -347,6 +349,10 @@
                 second_low(*gate)
 
             wide_part(DU, 2, j)
+
+            @pl.when((j == 0) & held)
+            def _():
+                begin_low(*gate)
 
             @pl.when(j == 0)
             def _():
@@ -704,27 +710,35 @@
             to_permute(a, l, way).wait()
 
 
-def store_kernel(count, *refs):
+def store_kernel(n, count, *refs):
     src, dst, sem = refs[:count], refs[count : 2 * count], refs[-1]
-    copies = [
-        pltpu.make_async_copy(a.at[l], b.at[l], sem.at[i, l])
-        for i, (a, b) in enumerate(zip(src, dst, strict=True))
-        for l in range(a.shape[0])
-    ]
+    layers = src[0].shape[0]
+    late = turns(layers)[-LATE:]
+    opposite = lax.axis_index("dp") + n // 2
+    copies = []
+    for i, (a, b) in enumerate(zip(src, dst, strict=True)):
+        rows = a.shape[1] // n
+        for l in range(layers):
+            if (i, l) in late:
+                for d in range(1, n):
+                    here = at(lax.rem(opposite + d, n), rows)
+                    copies.append(pltpu.make_async_copy(a.at[l, here], b.at[l, here], sem.at[i, l, d]))
+            else:
+                copies.append(pltpu.make_async_copy(a.at[l], b.at[l], sem.at[i, l, 0]))
     for copy in copies:
         copy.start()
     for copy in copies:
         copy.wait()
 
 
-def store(arrays):
+def store(n, arrays):
     count = len(arrays)
     return pl.pallas_call(
-        functools.partial(store_kernel, count),
+        functools.partial(store_kernel, n, count),
         out_shape=tuple(jax.ShapeDtypeStruct(t.shape, t.dtype) for t in arrays),
         in_specs=[pl.BlockSpec(memory_space=pltpu.VMEM)] * count,
         out_specs=(pl.BlockSpec(memory_space=pl.ANY),) * count,
-        scratch_shapes=[pltpu.SemaphoreType.DMA((count, arrays[0].shape[0]))],
+        scratch_shapes=[pltpu.SemaphoreType.DMA((count, arrays[0].shape[0], n))],
         compiler_params=pltpu.CompilerParams(vmem_limit_bytes=2**20),
         cost_estimate=pl.CostEstimate(flops=10_000_000_000, bytes_accessed=0, transcendentals=0),
         name="store",
@@ -803,7 +817,7 @@
         w, m, v = (arrays[i : i + 3] for i in (0, 3, 6))
         *new, up, down = update(n, gradients(n, x, dy, *w, m[2], v[2]), w, m, v)
         came = tuple(lax.ppermute(t, "dp", [(i, (i + d) % n) for i in range(n)]) for t, d in ((up, 1), (down, -1)))
-        out = store(new)
+        out = store(n, new)
         return (*place_last(n, out[:2], came), *out[2:])
 
     shard = P(None, "dp", None)

time: 404 us -> 405 us (level)
  transfers between devices with their start and end apart: 2 -> 2, of which waited for: 2 -> 1; matrix products, arithmetic and copies ran while one was open for 0% -> 0% of each run, Pallas kernels for 2% -> 2%
where the time goes in v12:
time: 405 us
  Pallas kernels  400 us (99%)
    pallas_call x1, Pallas kernels, gradients(): pl.pallas_call(functools.partial(grad_kernel, n, layers, (tokens, dim, ff...  228 us
    pallas_call x1, Pallas kernels, update(): pl.pallas_call(functools.partial(update_kernel, n, float(count), parts),...  161 us
    pallas_call x1, Pallas kernels, store(): pl.pallas_call(functools.partial(store_kernel, n, count), out_shape=tuple...  10.1 us
  transfers between devices with their start and end apart: 2, of which 1 were waited for; matrix products, arithmetic and copies ran while one was open for 0% of the time, Pallas kernels for 2%

profile of v12, /device:TPU:30, one launch (start us, length us, event | category | flops | bytes accessed | tf_op | source)
XLA Modules:
  0.0 404.7 jit_solution(3555240056233952347)
XLA Ops:
  0.6 227.6 %grads.1 = (bf16[2,64,3072]{2,1,0:T(8,128)(2,1)S(1)}, bf16[2,64,3072]{2,1,0:T(8,128)(2,1)S(1)}, bf16[2,384,512]{2,1,0:T(8,128)(2,1)S(1)}, f32[8,8,128]{2,1,0:T(8...) custom-call(bf16[1,2048,512]{2,1,0:T(8,128)(2,1)} %refs_0_.1, ...), custom_call_target="tpu_custom_call" | custom-call | tf_op jit(solution)/shard_map/grads/pallas_call | solution.py:534
  228.3 161.1 %update.1 = (bf16[2,512,3072]{2,1,0:T(8,128)(2,1)S(1)}, bf16[2,512,3072]{2,1,0:T(8,128)(2,1)S(1)}, bf16[2,3072,512]{2,1,0:T(8,128)(2,1)S(1)}, f32[2,64,3072]{2,1...) custom-call(bf16[2,64,3072]{2,1,0:T(8,128)(2,1)S(1)} %get-tuple-elem, ...), custom_call_target="tpu_custom_call" | custom-call | tf_op jit(solution)/shard_map/update/pallas_call | solution.py:789
  389.3 2.0 collective-permute-start
  391.3 1.3 collective-permute-start.1
  392.7 10.1 %store.1 = (bf16[2,512,3072]{2,1,0:T(8,128)(2,1)}, bf16[2,512,3072]{2,1,0:T(8,128)(2,1)}, bf16[2,3072,512]{2,1,0:T(8,128)(2,1)}, f32[2,64,3072]{2,1,0:T(8,128)},...) custom-call(bf16[2,512,3072]{2,1,0:T(8,128)(2,1)S(1)} %get-tuple-ele, ...), custom_call_target="tpu_custom_call" | custom-call | flops 10000000000 | tf_op jit(solution)/shard_map/store/pallas_call | solution.py:736
  402.7 0.0 collective-permute-done.refs_2_
  402.8 0.6 collective-permute-done.1.refs_3_
  403.3 1.2 place.1
Async XLA Ops:
  389.3 13.4 %collective-permute-start = (bf16[4,32,3072]{2,1,0:T(8,128)(2,1)S(1)}, bf16[4,32,3072]{2,1,0:T(8,128)(2,1)S(1)}, u32[]{:S(2)}, u32[]{:S(2)}) collective-permute-start(bf16[4,32,3072]{2,1,0:T(8,128)(2,1)S(1)} %get-tuple-element.56), channel_id=1, source_target_pairs={{0,1},{1,2},{2,3},{3,4},{4,5},{5,6},{6,7},{7,0},{8,9},{9,10},{10,1... | collective-permute-start | bytes 2359304 | tf_op jit(solution)/shard_map/ppermute | solution.py:819
  391.3 12.0 %collective-permute-start.1 = (bf16[4,32,3072]{2,1,0:T(8,128)(2,1)S(1)}, bf16[4,32,3072]{2,1,0:T(8,128)(2,1)S(1)}, u32[]{:S(2)}, u32[]{:S(2)}) collective-permute-start(bf16[4,32,3072]{2,1,0:T(8,128)(2,1)S(1)} %get-tuple-element.57), channel_id=1, source_target_pairs={{0,7},{1,0},{2,1},{3,2},{4,3},{5,4},{6,5},{7,6},{8,15},{9,8},{10,9... | collective-permute-start | bytes 2359304 | tf_op jit(solution)/shard_map/ppermute | solution.py:819

commit v13 on v10

--- a/solution.py
+++ b/solution.py
@@ -101,17 +101,17 @@
     def first_norm(i):
         wide = H[tok(i), :].astype(F32)
         A[tok(i), :] = (wide * scale_of(wide)).astype(BF16)
-        DA[tok(i), :] = jnp.zeros((tb, dim), F32)
-
-    def forward(k, i, act=ACT):
-        slot = lax.rem(k, 2)
+
+    def forward(k, i, act=ACT, fresh=False):
+        slot = k % 2 if isinstance(k, int) else lax.rem(k, 2)
         for j in range(4):
             here = pl.ds(j * (tile // 4), tile // 4)
             g = dot(A[tok(i), :], WG[slot, :, here])
             u = dot(A[tok(i), :], WU[slot, :, here])
             s = 0.5 * jnp.tanh(0.5 * g) + 0.5
             act[tok(i), here] = (g * s * u).astype(BF16)
-        DA[tok(i), :] += dot(act[tok(i), :], WD[slot])
+        part = dot(act[tok(i), :], WD[slot])
+        DA[tok(i), :] = part if fresh else DA[tok(i), :] + part
 
     def second_norm(i):
         h = (H[tok(i), :].astype(F32) + DA[tok(i), :].astype(BF16).astype(F32)).astype(BF16)
@@ -130,45 +130,60 @@
     fetch(1)
     loop(blocks, lambda i: dy_copy(i).start())
 
-    def opening(i):
+    def opening(j):
+        i = 2 * j
         x_copy(i + 1).wait()
-        forward(0, i)
+
+        @pl.when(i + 2 < blocks)
+        def _():
+            x_copy(i + 2).wait()
+
+        forward(0, i, fresh=True)
         first_norm(i + 1)
-
-    loop(blocks - 1, opening)
+        forward(0, i + 1, DG, True)
+        first_norm(jnp.minimum(i + 2, blocks - 1))
+
+    loop(blocks // 2, opening)
 
     def middle(j):
-        q = blocks - 1 + 2 * j
-
-        @pl.when(lax.rem(q + 1, blocks) == 0)
-        def _():
-            fetched((q + 1) // blocks)
-
-        @pl.when((lax.rem(q, blocks) == 1) & (q // blocks < tiles - 1))
-        def _():
-            fetch(q // blocks + 1)
-
-        seen = [jnp.minimum(2 * j + d, blocks - 1) for d in range(2)]
+        k, i = 1 + 2 * j // blocks, lax.rem(2 * j, blocks)
+
+        @pl.when(i == 0)
+        def _():
+            fetched(k)
+            fetch(k + 1)
 
         @pl.when(2 * j < blocks)
         def _():
-            dy_copy(2 * j).wait()
-            dy_copy(2 * j + 1).wait()
-
-        forward(q // blocks, lax.rem(q, blocks))
-        forward((q + 1) // blocks, lax.rem(q + 1, blocks), DG)
-        for i in seen:
-            DT[:, tok(i)] = D[tok(i), :].T
-
-    loop((tiles - 2) * blocks // 2 + 1, middle)
+            dy_copy(i).wait()
+            dy_copy(i + 1).wait()
+
+        forward(k, i)
+        forward(k, i + 1, DG)
+        for d in range(2):
+            DT[:, tok(i + d)] = D[tok(i + d), :].T
+
+    loop((tiles - 2) * blocks // 2, middle)
+    fetched(tiles - 1)
     fetch(tiles)
 
-    def closing(i):
-        normed = second_norm(i)
-        forward(tiles - 1, i + 1)
-        second_norm_kept(i, *normed)
-
-    loop(blocks - 1, closing)
+    @pl.when(me >= 0)
+    def _():
+        forward(tiles - 1, 0)
+        normed = second_norm(0)
+        forward(tiles - 1, 1, DG)
+        second_norm_kept(0, *normed)
+
+    for i in range(2, blocks, 2):
+
+        @pl.when(me >= 0)
+        def _(i=i):
+            normed = second_norm(i - 1)
+            forward(tiles - 1, i)
+            second_norm_kept(i - 1, *normed)
+            normed = second_norm(i)
+            forward(tiles - 1, i + 1, DG)
+            second_norm_kept(i, *normed)
 
     def hidden(slot, j, i, pieces=1):
         size = 2 * tb // pieces

time: 404 us -> 405 us (level)
  no operation moved by 1% of the time
where the time goes in v13:
time: 405 us
  Pallas kernels  400 us (99%)
    pallas_call x1, Pallas kernels, gradients(): pl.pallas_call(functools.partial(grad_kernel, n, layers, (tokens, dim, ff...  228 us
    pallas_call x1, Pallas kernels, update(): pl.pallas_call(functools.partial(update_kernel, n, float(count), parts),...  161 us
    pallas_call x1, Pallas kernels, store(): pl.pallas_call(functools.partial(store_kernel, count), out_shape=tuple((j...  9.49 us
  transfers between devices with their start and end apart: 2, of which 2 were waited for; matrix products, arithmetic and copies ran while one was open for 0% of the time, Pallas kernels for 2%

profile of v13, /device:TPU:30, one launch (start us, length us, event | category | flops | bytes accessed | tf_op | source)
XLA Modules:
  0.0 404.8 jit_solution(12683497659440816656)
XLA Ops:
  0.6 228.2 %grads.1 = (bf16[2,64,3072]{2,1,0:T(8,128)(2,1)S(1)}, bf16[2,64,3072]{2,1,0:T(8,128)(2,1)S(1)}, bf16[2,384,512]{2,1,0:T(8,128)(2,1)S(1)}, f32[8,8,128]{2,1,0:T(8...) custom-call(bf16[1,2048,512]{2,1,0:T(8,128)(2,1)} %refs_0_.1, ...), custom_call_target="tpu_custom_call" | custom-call | tf_op jit(solution)/shard_map/grads/pallas_call | solution.py:543
  228.8 161.0 %update.1 = (bf16[2,512,3072]{2,1,0:T(8,128)(2,1)S(1)}, bf16[2,512,3072]{2,1,0:T(8,128)(2,1)S(1)}, bf16[2,3072,512]{2,1,0:T(8,128)(2,1)S(1)}, f32[2,64,3072]{2,1...) custom-call(bf16[2,64,3072]{2,1,0:T(8,128)(2,1)S(1)} %get-tuple-elem, ...), custom_call_target="tpu_custom_call" | custom-call | tf_op jit(solution)/shard_map/update/pallas_call | solution.py:790
  389.8 1.7 collective-permute-start
  391.5 1.7 collective-permute-start.1
  393.1 9.5 %store.1 = (bf16[2,512,3072]{2,1,0:T(8,128)(2,1)}, bf16[2,512,3072]{2,1,0:T(8,128)(2,1)}, bf16[2,3072,512]{2,1,0:T(8,128)(2,1)}, f32[2,64,3072]{2,1,0:T(8,128)},...) custom-call(bf16[2,512,3072]{2,1,0:T(8,128)(2,1)S(1)} %get-tuple-ele, ...), custom_call_target="tpu_custom_call" | custom-call | flops 10000000000 | tf_op jit(solution)/shard_map/store/pallas_call | solution.py:737
  402.6 0.5 collective-permute-done.refs_2_
  403.1 0.4 collective-permute-done.1.refs_3_
  403.5 1.2 place.1
Async XLA Ops:
  389.8 13.3 %collective-permute-start = (bf16[4,32,3072]{2,1,0:T(8,128)(2,1)S(1)}, bf16[4,32,3072]{2,1,0:T(8,128)(2,1)S(1)}, u32[]{:S(2)}, u32[]{:S(2)}) collective-permute-start(bf16[4,32,3072]{2,1,0:T(8,128)(2,1)S(1)} %get-tuple-element.56), channel_id=1, source_target_pairs={{0,1},{1,2},{2,3},{3,4},{4,5},{5,6},{6,7},{7,0},{8,9},{9,10},{10,1... | collective-permute-start | bytes 2359304 | tf_op jit(solution)/shard_map/ppermute | solution.py:820
  391.5 12.0 %collective-permute-start.1 = (bf16[4,32,3072]{2,1,0:T(8,128)(2,1)S(1)}, bf16[4,32,3072]{2,1,0:T(8,128)(2,1)S(1)}, u32[]{:S(2)}, u32[]{:S(2)}) collective-permute-start(bf16[4,32,3072]{2,1,0:T(8,128)(2,1)S(1)} %get-tuple-element.57), channel_id=1, source_target_pairs={{0,7},{1,0},{2,1},{3,2},{4,3},{5,4},{6,5},{7,6},{8,15},{9,8},{10,9... | collective-permute-start | bytes 2359304 | tf_op jit(solution)/shard_map/ppermute | solution.py:820

commit v14 on v10

--- a/solution.py
+++ b/solution.py
@@ -45,7 +45,7 @@
 def grad_kernel(n, layers, shapes, *refs):
     (x_hbm, dy_hbm, wg_hbm, wu_hbm, wd_hbm, md_hbm, vd_hbm) = refs[:7]
     (OG, OU, OD, ALL, PW, PM, PV) = refs[7:14]
-    (A, AT, D, DT, H, ACT, DG, DU, DA, WG, WU, WD, G, RU, RD, SQ, *sems) = refs[14:]
+    (A, AT, D, DT, H, ACT, DGU, DA, WG, WU, WD, G, RU, RD, SQ, *sems) = refs[14:]
     x_sem, dy_sem, w_sem, ahead_sem, send_sem, recv_sem, low_sem, sq_send, sq_recv = sems
     tokens, dim, ff, blocks = shapes
     share = ff // n
@@ -156,7 +156,7 @@
             dy_copy(2 * j + 1).wait()
 
         forward(q // blocks, lax.rem(q, blocks))
-        forward((q + 1) // blocks, lax.rem(q + 1, blocks), DG)
+        forward((q + 1) // blocks, lax.rem(q + 1, blocks), DGU.at[0])
         for i in seen:
             DT[:, tok(i)] = D[tok(i), :].T
 
@@ -170,10 +170,9 @@
 
     loop(blocks - 1, closing)
 
-    def hidden(slot, j, i, pieces=1):
-        size = 2 * tb // pieces
-        for p, c in [(p, c) for p in range(pieces) for c in range(2)]:
-            place = at(i * pieces + p, size)
+    def hidden(slot, j, i):
+        place = at(i, 2 * tb)
+        for c in range(2):
             here = at(2 * j + c, cols // 2)
             g = dot(A[place, :], WG[slot, :, here])
             u = dot(A[place, :], WU[slot, :, here])
@@ -181,13 +180,10 @@
             s = 0.5 * jnp.tanh(0.5 * g) + 0.5
             silu = g * s
             ACT[place, here] = (silu * u).astype(BF16)
-            DU[place, here] = (back * silu).astype(BF16)
-            DG[place, here] = (back * u * (s + silu * (1.0 - s))).astype(BF16)
-
-    fetched(tiles)
-    normed = second_norm(blocks - 1)
-    hidden(tiles % 2, 0, 0, 2)
-    second_norm_kept(blocks - 1, *normed)
+            DGU[1, place, here] = (back * silu).astype(BF16)
+            DGU[0, place, here] = (back * u * (s + silu * (1.0 - s))).astype(BF16)
+
+    second_norm_kept(blocks - 1, *second_norm(blocks - 1))
 
     pl.semaphore_wait(barrier, n - 1)
 
@@ -293,10 +289,7 @@
         going = k >= 1
         old_t = lax.rem(k - 1 + tiles, tiles)
         old_layer = jnp.where(k - 1 < tiles, 1, 0)
-
-        @pl.when(k > 0)
-        def _():
-            fetched(wk)
+        fetched(wk)
 
         @pl.when(k < 2 * tiles - 1)
         def _():
@@ -305,18 +298,12 @@
         def when(cond):
             return pl.when(going & cond)
 
-        def wide_part(src, unit, j):
-            part = dot(AT[...], src[:, at(j, cols)]).astype(BF16)
-            G[base + unit, :, at(j, hr), :] = part.reshape(n, dim // n, cols)
-
         gate, upper = (u0 + 1, base + 1), (u0 + 2, base + 2)
         old, old_gate, old_upper = (p0, prev), (p0 + 1, prev + 1), (p0 + 2, prev + 2)
 
         def halves(j):
             def some(i):
-                @pl.when((k > 0) | (j > 0) | (i > 0))
-                def _():
-                    hidden(slot, j, i)
+                hidden(slot, j, i)
 
                 @when((j == 0) & (i == 0))
                 def _():
@@ -332,40 +319,36 @@
                     second_low(*upper)
 
             loop(blocks // 2, some)
-            wide_part(DG, 1, j)
-
-            @pl.when(j == 0)
-            def _():
-                begin_low(*gate)
-
-            @pl.when(j == 1)
-            def _():
-                begin_high(*gate)
-
-            @pl.when((j == 1) & (k == 0))
-            def _():
-                second_low(*gate)
-
-            wide_part(DU, 2, j)
-
-            @pl.when(j == 0)
-            def _():
-                begin_low(*upper)
-
-            @pl.when(j == 1)
-            def _():
-                begin_high(*upper)
-
-            @when(j == 1)
-            def _():
-                later(*old, 3)
-                finish(*old_gate, 1, old_layer, old_t)
-                finish(*old_upper, 2, old_layer, old_t)
-                second_low(*gate)
-
-            @pl.when((j == 1) & (k == 0))
-            def _():
-                third_low(*upper)
+
+            def wide_part(c):
+                unit = (u0 + 1 + c, base + 1 + c)
+                part = dot(AT[...], DGU[c, :, at(j, cols)]).astype(BF16)
+                G[unit[1], :, at(j, hr), :] = part.reshape(n, dim // n, cols)
+
+                @pl.when(j == 0)
+                def _():
+                    begin_low(*unit)
+
+                @pl.when(j == 1)
+                def _():
+                    begin_high(*unit)
+
+                @pl.when((j == 1) & (k == 0) & (c == 0))
+                def _():
+                    second_low(*gate)
+
+                @when((j == 1) & (c == 1))
+                def _():
+                    later(*old, 3)
+                    finish(*old_gate, 1, old_layer, old_t)
+                    finish(*old_upper, 2, old_layer, old_t)
+                    second_low(*gate)
+
+                @pl.when((j == 1) & (k == 0) & (c == 1))
+                def _():
+                    third_low(*upper)
+
+            loop(2, wide_part)
 
         loop(2, halves)
 
@@ -413,7 +396,7 @@
         def _():
             def input_part(i):
                 so_far = jnp.where(k == 0, 0.0, DA[tok(i), :])
-                DA[tok(i), :] = so_far + (dot_t(DG[tok(i), :], WG[slot]) + dot_t(DU[tok(i), :], WU[slot]))
+                DA[tok(i), :] = so_far + (dot_t(DGU[0, tok(i), :], WG[slot]) + dot_t(DGU[1, tok(i), :], WU[slot]))
                 ring_part(i)
 
             loop(blocks, input_part)
@@ -548,8 +531,7 @@
             pltpu.VMEM((dim, tokens), BF16),
             pltpu.VMEM((tokens, dim), BF16),
             pltpu.VMEM((tokens, tile), BF16),
-            pltpu.VMEM((tokens, tile), BF16),
-            pltpu.VMEM((tokens, tile), BF16),
+            pltpu.VMEM((2, tokens, tile), BF16),
             pltpu.VMEM((tokens, dim), F32),
             pltpu.VMEM((2, dim, tile), BF16),
             pltpu.VMEM((2, dim, tile), BF16),

time: 404 us -> 404 us (level)
  no operation moved by 1% of the time
where the time goes in v14:
time: 404 us
  Pallas kernels  399 us (99%)
    pallas_call x1, Pallas kernels, gradients(): pl.pallas_call(functools.partial(grad_kernel, n, layers, (tokens, dim, ff...  227 us
    pallas_call x1, Pallas kernels, update(): pl.pallas_call(functools.partial(update_kernel, n, float(count), parts),...  161 us
    pallas_call x1, Pallas kernels, store(): pl.pallas_call(functools.partial(store_kernel, count), out_shape=tuple((j...  9.49 us
  transfers between devices with their start and end apart: 2, of which 2 were waited for; matrix products, arithmetic and copies ran while one was open for 0% of the time, Pallas kernels for 2%

profile of v14, /device:TPU:30, one launch (start us, length us, event | category | flops | bytes accessed | tf_op | source)
XLA Modules:
  0.0 404.2 jit_solution(16092963863394448245)
XLA Ops:
  0.6 227.4 %grads.1 = (bf16[2,64,3072]{2,1,0:T(8,128)(2,1)S(1)}, bf16[2,64,3072]{2,1,0:T(8,128)(2,1)S(1)}, bf16[2,384,512]{2,1,0:T(8,128)(2,1)S(1)}, f32[8,8,128]{2,1,0:T(8...) custom-call(bf16[1,2048,512]{2,1,0:T(8,128)(2,1)} %refs_0_.1, ...), custom_call_target="tpu_custom_call" | custom-call | tf_op jit(solution)/shard_map/grads/pallas_call | solution.py:511
  228.0 161.0 %update.1 = (bf16[2,512,3072]{2,1,0:T(8,128)(2,1)S(1)}, bf16[2,512,3072]{2,1,0:T(8,128)(2,1)S(1)}, bf16[2,3072,512]{2,1,0:T(8,128)(2,1)S(1)}, f32[2,64,3072]{2,1...) custom-call(bf16[2,64,3072]{2,1,0:T(8,128)(2,1)S(1)} %get-tuple-elem, ...), custom_call_target="tpu_custom_call" | custom-call | tf_op jit(solution)/shard_map/update/pallas_call | solution.py:757
  389.0 1.8 collective-permute-start
  390.8 1.5 collective-permute-start.1
  392.3 9.5 %store.1 = (bf16[2,512,3072]{2,1,0:T(8,128)(2,1)}, bf16[2,512,3072]{2,1,0:T(8,128)(2,1)}, bf16[2,3072,512]{2,1,0:T(8,128)(2,1)}, f32[2,64,3072]{2,1,0:T(8,128)},...) custom-call(bf16[2,512,3072]{2,1,0:T(8,128)(2,1)S(1)} %get-tuple-ele, ...), custom_call_target="tpu_custom_call" | custom-call | flops 10000000000 | tf_op jit(solution)/shard_map/store/pallas_call | solution.py:704
  401.8 0.5 collective-permute-done.refs_2_
  402.3 0.5 collective-permute-done.1.refs_3_
  402.8 1.2 place.1
Async XLA Ops:
  389.0 13.3 %collective-permute-start = (bf16[4,32,3072]{2,1,0:T(8,128)(2,1)S(1)}, bf16[4,32,3072]{2,1,0:T(8,128)(2,1)S(1)}, u32[]{:S(2)}, u32[]{:S(2)}) collective-permute-start(bf16[4,32,3072]{2,1,0:T(8,128)(2,1)S(1)} %get-tuple-element.56), channel_id=1, source_target_pairs={{0,1},{1,2},{2,3},{3,4},{4,5},{5,6},{6,7},{7,0},{8,9},{9,10},{10,1... | collective-permute-start | bytes 2359304 | tf_op jit(solution)/shard_map/ppermute | solution.py:787
  390.8 12.0 %collective-permute-start.1 = (bf16[4,32,3072]{2,1,0:T(8,128)(2,1)S(1)}, bf16[4,32,3072]{2,1,0:T(8,128)(2,1)S(1)}, u32[]{:S(2)}, u32[]{:S(2)}) collective-permute-start(bf16[4,32,3072]{2,1,0:T(8,128)(2,1)S(1)} %get-tuple-element.57), channel_id=1, source_target_pairs={{0,7},{1,0},{2,1},{3,2},{4,3},{5,4},{6,5},{7,6},{8,15},{9,8},{10,9... | collective-permute-start | bytes 2359304 | tf_op jit(solution)/shard_map/ppermute | solution.py:787

commit v15 on v14

--- a/solution.py
+++ b/solution.py
@@ -591,7 +591,7 @@
 
     def shape(a):
         rows, cols = G[a].shape[1:]
-        return (rows, cols // parts, 0) if a < 2 else (rows // parts, cols, 1)
+        return (rows, cols // parts[a], 0) if a < 2 else (rows // parts[a], cols, 1)
 
     def place(a, l, p, owner, part):
         rows = G[a].shape[1]
@@ -642,7 +642,7 @@
 
     chunks = []
     for a, l in order:
-        for p in range(parts):
+        for p in range(parts[a]):
             chunks.append((len(chunks), a, l, p))
     for i, a, l, p in chunks:
         if p == 0:
@@ -675,7 +675,7 @@
                     came(i, a, l, p, way, step)
                 if step < hops(a, l) - 1:
                     send(i, a, l, p, way, step + 1).start()
-                elif step == half - 2 and p == parts - 1:
+                elif step == half - 2 and p == parts[a] - 1:
                     to_permute(a, l, way).start()
     for i, a, l, p in chunks:
         for way in range(2):
@@ -688,11 +688,7 @@
 
 def store_kernel(count, *refs):
     src, dst, sem = refs[:count], refs[count : 2 * count], refs[-1]
-    copies = [
-        pltpu.make_async_copy(a.at[l], b.at[l], sem.at[i, l])
-        for i, (a, b) in enumerate(zip(src, dst, strict=True))
-        for l in range(a.shape[0])
-    ]
+    copies = [pltpu.make_async_copy(a, b, sem.at[i]) for i, (a, b) in enumerate(zip(src, dst, strict=True))]
     for copy in copies:
         copy.start()
     for copy in copies:
@@ -706,7 +702,7 @@
         out_shape=tuple(jax.ShapeDtypeStruct(t.shape, t.dtype) for t in arrays),
         in_specs=[pl.BlockSpec(memory_space=pltpu.VMEM)] * count,
         out_specs=(pl.BlockSpec(memory_space=pl.ANY),) * count,
-        scratch_shapes=[pltpu.SemaphoreType.DMA((count, arrays[0].shape[0]))],
+        scratch_shapes=[pltpu.SemaphoreType.DMA((count,))],
         compiler_params=pltpu.CompilerParams(vmem_limit_bytes=2**20),
         cost_estimate=pl.CostEstimate(flops=10_000_000_000, bytes_accessed=0, transcendentals=0),
         name="store",
@@ -747,8 +743,8 @@
 
 def update(n, made, w, m, v):
     layers = w[0].shape[0]
-    parts = 2
-    chunks = layers * 3 * parts
+    parts = (2, 2, 4)
+    chunks = layers * sum(parts)
     count = sum(t.size for t in w)
     any_space = pl.BlockSpec(memory_space=pl.ANY)
     in_vmem = pl.BlockSpec(memory_space=pltpu.VMEM)

time: 404 us -> 404 us (level)
  no operation moved by 1% of the time
where the time goes in v15:
time: 404 us
  Pallas kernels  399 us (99%)
    pallas_call x1, Pallas kernels, gradients(): pl.pallas_call(functools.partial(grad_kernel, n, layers, (tokens, dim, ff...  227 us
    pallas_call x1, Pallas kernels, update(): pl.pallas_call(functools.partial(update_kernel, n, float(count), parts),...  161 us
    pallas_call x1, Pallas kernels, store(): pl.pallas_call(functools.partial(store_kernel, count), out_shape=tuple((j...  9.44 us
  transfers between devices with their start and end apart: 2, of which 2 were waited for; matrix products, arithmetic and copies ran while one was open for 0% of the time, Pallas kernels for 2%

profile of v15, /device:TPU:30, one launch (start us, length us, event | category | flops | bytes accessed | tf_op | source)
XLA Modules:
  0.0 404.2 jit_solution(14744253930630638567)
XLA Ops:
  0.6 227.4 %grads.1 = (bf16[2,64,3072]{2,1,0:T(8,128)(2,1)S(1)}, bf16[2,64,3072]{2,1,0:T(8,128)(2,1)S(1)}, bf16[2,384,512]{2,1,0:T(8,128)(2,1)S(1)}, f32[8,8,128]{2,1,0:T(8...) custom-call(bf16[1,2048,512]{2,1,0:T(8,128)(2,1)} %refs_0_.1, ...), custom_call_target="tpu_custom_call" | custom-call | tf_op jit(solution)/shard_map/grads/pallas_call | solution.py:511
  228.0 161.0 %update.1 = (bf16[2,512,3072]{2,1,0:T(8,128)(2,1)S(1)}, bf16[2,512,3072]{2,1,0:T(8,128)(2,1)S(1)}, bf16[2,3072,512]{2,1,0:T(8,128)(2,1)S(1)}, f32[2,64,3072]{2,1...) custom-call(bf16[2,64,3072]{2,1,0:T(8,128)(2,1)S(1)} %get-tuple-elem, ...), custom_call_target="tpu_custom_call" | custom-call | tf_op jit(solution)/shard_map/update/pallas_call | solution.py:753
  389.0 1.8 collective-permute-start
  390.8 1.5 collective-permute-start.1
  392.3 9.4 %store.1 = (bf16[2,512,3072]{2,1,0:T(8,128)(2,1)}, bf16[2,512,3072]{2,1,0:T(8,128)(2,1)}, bf16[2,3072,512]{2,1,0:T(8,128)(2,1)}, f32[2,64,3072]{2,1,0:T(8,128)},...) custom-call(bf16[2,512,3072]{2,1,0:T(8,128)(2,1)S(1)} %get-tuple-ele, ...), custom_call_target="tpu_custom_call" | custom-call | flops 10000000000 | tf_op jit(solution)/shard_map/store/pallas_call | solution.py:700
  401.8 0.5 collective-permute-done.refs_2_
  402.3 0.5 collective-permute-done.1.refs_3_
  402.8 1.2 place.1
Async XLA Ops:
  389.0 13.3 %collective-permute-start = (bf16[4,32,3072]{2,1,0:T(8,128)(2,1)S(1)}, bf16[4,32,3072]{2,1,0:T(8,128)(2,1)S(1)}, u32[]{:S(2)}, u32[]{:S(2)}) collective-permute-start(bf16[4,32,3072]{2,1,0:T(8,128)(2,1)S(1)} %get-tuple-element.56), channel_id=1, source_target_pairs={{0,1},{1,2},{2,3},{3,4},{4,5},{5,6},{6,7},{7,0},{8,9},{9,10},{10,1... | collective-permute-start | bytes 2359304 | tf_op jit(solution)/shard_map/ppermute | solution.py:783
  390.8 12.0 %collective-permute-start.1 = (bf16[4,32,3072]{2,1,0:T(8,128)(2,1)S(1)}, bf16[4,32,3072]{2,1,0:T(8,128)(2,1)S(1)}, u32[]{:S(2)}, u32[]{:S(2)}) collective-permute-start(bf16[4,32,3072]{2,1,0:T(8,128)(2,1)S(1)} %get-tuple-element.57), channel_id=1, source_target_pairs={{0,7},{1,0},{2,1},{3,2},{4,3},{5,4},{6,5},{7,6},{8,15},{9,8},{10,9... | collective-permute-start | bytes 2359304 | tf_op jit(solution)/shard_map/ppermute | solution.py:783

commit v16 on v10

--- a/solution.py
+++ b/solution.py
@@ -506,9 +506,10 @@
             device_id_type=MESH,
         )
 
-    for d in range(1, n):
+    order = sorted(range(1, n), key=lambda d: -min(d, n - d))
+    for d in order:
         tell(d).start()
-    for d in range(1, n):
+    for d in reversed(order):
         tell(d).wait()
     for copy in ahead:
         copy.wait()

time: 404 us -> 404 us (level)
  no operation moved by 1% of the time
where the time goes in v16:
time: 404 us
  Pallas kernels  399 us (99%)
    pallas_call x1, Pallas kernels, gradients(): pl.pallas_call(functools.partial(grad_kernel, n, layers, (tokens, dim, ff...  227 us
    pallas_call x1, Pallas kernels, update(): pl.pallas_call(functools.partial(update_kernel, n, float(count), parts),...  161 us
    pallas_call x1, Pallas kernels, store(): pl.pallas_call(functools.partial(store_kernel, count), out_shape=tuple((j...  9.49 us
  transfers between devices with their start and end apart: 2, of which 2 were waited for; matrix products, arithmetic and copies ran while one was open for 0% of the time, Pallas kernels for 2%

profile of v16, /device:TPU:30, one launch (start us, length us, event | category | flops | bytes accessed | tf_op | source)
XLA Modules:
  0.0 404.1 jit_solution(4092522352794895054)
XLA Ops:
  0.6 227.4 %grads.1 = (bf16[2,64,3072]{2,1,0:T(8,128)(2,1)S(1)}, bf16[2,64,3072]{2,1,0:T(8,128)(2,1)S(1)}, bf16[2,384,512]{2,1,0:T(8,128)(2,1)S(1)}, f32[8,8,128]{2,1,0:T(8...) custom-call(bf16[1,2048,512]{2,1,0:T(8,128)(2,1)} %refs_0_.1, ...), custom_call_target="tpu_custom_call" | custom-call | tf_op jit(solution)/shard_map/grads/pallas_call | solution.py:529
  228.1 161.0 %update.1 = (bf16[2,512,3072]{2,1,0:T(8,128)(2,1)S(1)}, bf16[2,512,3072]{2,1,0:T(8,128)(2,1)S(1)}, bf16[2,3072,512]{2,1,0:T(8,128)(2,1)S(1)}, f32[2,64,3072]{2,1...) custom-call(bf16[2,64,3072]{2,1,0:T(8,128)(2,1)S(1)} %get-tuple-elem, ...), custom_call_target="tpu_custom_call" | custom-call | tf_op jit(solution)/shard_map/update/pallas_call | solution.py:776
  389.0 1.7 collective-permute-start
  390.7 1.6 collective-permute-start.1
  392.4 9.5 %store.1 = (bf16[2,512,3072]{2,1,0:T(8,128)(2,1)}, bf16[2,512,3072]{2,1,0:T(8,128)(2,1)}, bf16[2,3072,512]{2,1,0:T(8,128)(2,1)}, f32[2,64,3072]{2,1,0:T(8,128)},...) custom-call(bf16[2,512,3072]{2,1,0:T(8,128)(2,1)S(1)} %get-tuple-ele, ...), custom_call_target="tpu_custom_call" | custom-call | flops 10000000000 | tf_op jit(solution)/shard_map/store/pallas_call | solution.py:723
  401.9 0.5 collective-permute-done.refs_2_
  402.3 0.4 collective-permute-done.1.refs_3_
  402.7 1.2 place.1
Async XLA Ops:
  389.0 13.3 %collective-permute-start = (bf16[4,32,3072]{2,1,0:T(8,128)(2,1)S(1)}, bf16[4,32,3072]{2,1,0:T(8,128)(2,1)S(1)}, u32[]{:S(2)}, u32[]{:S(2)}) collective-permute-start(bf16[4,32,3072]{2,1,0:T(8,128)(2,1)S(1)} %get-tuple-element.56), channel_id=1, source_target_pairs={{0,1},{1,2},{2,3},{3,4},{4,5},{5,6},{6,7},{7,0},{8,9},{9,10},{10,1... | collective-permute-start | bytes 2359304 | tf_op jit(solution)/shard_map/ppermute | solution.py:806
  390.7 12.0 %collective-permute-start.1 = (bf16[4,32,3072]{2,1,0:T(8,128)(2,1)S(1)}, bf16[4,32,3072]{2,1,0:T(8,128)(2,1)S(1)}, u32[]{:S(2)}, u32[]{:S(2)}) collective-permute-start(bf16[4,32,3072]{2,1,0:T(8,128)(2,1)S(1)} %get-tuple-element.57), channel_id=1, source_target_pairs={{0,7},{1,0},{2,1},{3,2},{4,3},{5,4},{6,5},{7,6},{8,15},{9,8},{10,9... | collective-permute-start | bytes 2359304 | tf_op jit(solution)/shard_map/ppermute | solution.py:806
